TPU v7x, 32 devices: a whole 2x2x4 slice. The times are simulated.
32 devices in a mesh: fsdp: 8 (over y, x, core), tensor: 4 (over z).
Axes of the slice: x: 2, y: 2, z: 4, core: 2. Of those that a mesh axis runs over, the one named last changes fastest.
Arguments:
- hidden: bfloat16 [16, 1536, 1280], P('fsdp', 'tensor'), may hold values from -6 to 6
- positions: int32 [16, 2, 1536], P('fsdp'), may hold values from 0 to 31
- segments: int32 [16, 1536], P('fsdp'), may hold values from 0 to 2, never falling along the last dimension, each value on 1 to 1024 neighbouring positions
- ln1_gain: bfloat16 [1280], P('fsdp'), may hold values from 0.5 to 1.5
- ln1_bias: bfloat16 [1280], P('fsdp'), may hold values from -1.25 to 1.25
- qkv_weight: bfloat16 [1280, 3, 1280], P('fsdp', None, 'tensor'), may hold values from -0.15625 to 0.15625
- qkv_bias: bfloat16 [3, 1280], P(None, 'tensor'), may hold values from -1.75 to 1.75
- proj_weight: bfloat16 [1280, 1280], P('tensor', 'fsdp'), may hold values from -2.5 to 2.5
- proj_bias: bfloat16 [1280], P('fsdp'), may hold values from -1.75 to 1.75
- ln2_gain: bfloat16 [1280], P('fsdp'), may hold values from 0.5 to 1.5
- ln2_bias: bfloat16 [1280], P('fsdp'), may hold values from -1.25 to 1.25
- fc1_weight: bfloat16 [1280, 5120], P('fsdp', 'tensor'), may hold values from -0.15625 to 0.15625
- fc1_bias: bfloat16 [5120], P('tensor'), may hold values from -1.75 to 1.75
- fc2_weight: bfloat16 [5120, 1280], P('tensor', 'fsdp'), may hold values from -0.078125 to 0.078125
- fc2_bias: bfloat16 [1280], P('fsdp'), may hold values from -1.75 to 1.75
- cotangent: bfloat16 [16, 1536, 1280], P('fsdp', 'tensor'), may hold values from -6 to 6
Outputs:
- output: bfloat16 [16, 1536, 1280], P('fsdp', 'tensor')
- hidden_grad: bfloat16 [16, 1536, 1280], P('fsdp', 'tensor')
- ln1_gain_grad: float32 [1280], P('fsdp')
- ln1_bias_grad: float32 [1280], P('fsdp')
- qkv_weight_grad: float32 [1280, 3, 1280], P('fsdp', None, 'tensor')
- qkv_bias_grad: float32 [3, 1280], P(None, 'tensor')
- proj_weight_grad: float32 [1280, 1280], P('tensor', 'fsdp')
- proj_bias_grad: float32 [1280], P('fsdp')
- ln2_gain_grad: float32 [1280], P('fsdp')
- ln2_bias_grad: float32 [1280], P('fsdp')
- fc1_weight_grad: float32 [1280, 5120], P('fsdp', 'tensor')
- fc1_bias_grad: float32 [5120], P('tensor')
- fc2_weight_grad: float32 [5120, 1280], P('tensor', 'fsdp')
- fc2_bias_grad: float32 [1280], P('fsdp')
Inputs may be any that keep to these rules, and one draw needn't show every extreme that they name: `positions`: arbitrary rotary row and column indices, drawn independently for every patch. `segments`: patches of one image are contiguous in a pack and image numbers never fall; each pack holds images of 1 to 1024 patches, one of exactly 1024.
All inputs are finite; a program needn't handle non-finite values.
Results may differ from a plain program's by a relative error of at most 0.018.
Values may be sent and summed in bfloat16 or wider, within the bound.
A program may use at most 256 MiB of HBM per device.

v0:
```python
import jax
import jax.numpy as jnp
from jax import lax
from jax.sharding import PartitionSpec as P

HEAD_DIM = 80


epsilon = 1e-06


def angle_tables(place):
    quarter = HEAD_DIM // 4
    freqs = 10000.0 ** (-(4.0 * jnp.arange(quarter, dtype=jnp.float32)) / HEAD_DIM)
    row_angles = place[0].astype(jnp.float32)[:, None] * freqs[None, :]
    col_angles = place[1].astype(jnp.float32)[:, None] * freqs[None, :]
    halfway = jnp.concatenate([row_angles, col_angles], axis=1)
    angles = jnp.concatenate([halfway, halfway], axis=1)
    return (jnp.cos(angles), jnp.sin(angles))


def rotate(values, cosine, sine):
    middle_index = HEAD_DIM // 2
    turned = jnp.concatenate([-values[..., middle_index:], values[..., :middle_index]], axis=-1)
    return values * cosine[:, None, :] + turned * sine[:, None, :]


def rotate_back(grads, cosine, sine):
    middle_index = HEAD_DIM // 2
    scaled = grads * sine[:, None, :]
    turned = jnp.concatenate([scaled[..., middle_index:], -scaled[..., :middle_index]], axis=-1)
    return grads * cosine[:, None, :] + turned


def normalize(values, gain, shift):
    center = values - jnp.mean(values, axis=-1, keepdims=True)
    spread = lax.rsqrt(jnp.mean(center * center, axis=-1, keepdims=True) + epsilon)
    unit = center * spread
    return (unit * gain + shift, unit, spread)


def normalize_back(grads, unit, spread, gain):
    scaled = grads * gain
    inner = (
        scaled
        - jnp.mean(scaled, axis=-1, keepdims=True)
        - unit * jnp.mean(scaled * unit, axis=-1, keepdims=True)
    )
    return inner * spread


def fetch_weights(shard_params):
    return (
        lax.all_gather(shard_params[0], "fsdp", axis=0, tiled=True),
        lax.all_gather(shard_params[1], "fsdp", axis=0, tiled=True),
        lax.all_gather(shard_params[2], "fsdp", axis=0, tiled=True),
        lax.all_gather(shard_params[3], "fsdp", axis=1, tiled=True),
        lax.all_gather(shard_params[4], "fsdp", axis=0, tiled=True),
        lax.all_gather(shard_params[5], "fsdp", axis=0, tiled=True),
        lax.all_gather(shard_params[6], "fsdp", axis=0, tiled=True),
        lax.all_gather(shard_params[7], "fsdp", axis=0, tiled=True),
        lax.all_gather(shard_params[8], "fsdp", axis=1, tiled=True),
        lax.all_gather(shard_params[9], "fsdp", axis=0, tiled=True),
    )


def fetch_again(shard_params):
    return (
        lax.all_gather(shard_params[0], "fsdp", axis=0, tiled=True),
        lax.all_gather(shard_params[1], "fsdp", axis=0, tiled=True),
        lax.all_gather(shard_params[2], "fsdp", axis=0, tiled=True),
        lax.all_gather(shard_params[3], "fsdp", axis=1, tiled=True),
        lax.all_gather(shard_params[4], "fsdp", axis=0, tiled=True),
        lax.all_gather(shard_params[5], "fsdp", axis=0, tiled=True),
        lax.all_gather(shard_params[6], "fsdp", axis=0, tiled=True),
        lax.all_gather(shard_params[7], "fsdp", axis=0, tiled=True),
        lax.all_gather(shard_params[8], "fsdp", axis=1, tiled=True),
        lax.all_gather(shard_params[9], "fsdp", axis=0, tiled=True),
    )


def share_rows(values):
    return lax.all_gather(values, "tensor", axis=0, tiled=True)


def share_grads(values):
    return lax.all_gather(values, "tensor", axis=0, tiled=True)


def branch_sum(left, right):
    return lax.psum_scatter(
        jnp.dot(left, right, preferred_element_type=jnp.float32).astype(jnp.bfloat16),
        "tensor",
        scatter_dimension=0,
        tiled=True,
    ).astype(jnp.float32)


def input_sum(left, right, form):
    return lax.psum_scatter(
        jnp.einsum(form, left, right, preferred_element_type=jnp.float32).astype(jnp.bfloat16),
        "tensor",
        scatter_dimension=0,
        tiled=True,
    ).astype(jnp.float32)


def masked_scores(query_block, label_block, keys, labels, scale):
    scores = (
        jnp.einsum("qhd,khd->hqk", query_block, keys, preferred_element_type=jnp.float32) * scale
    )
    same_image = label_block[:, None] == labels[None, :]
    return jnp.where(same_image[None, :, :], scores, -1000000000.0)


def attend(queries, keys, values, labels):
    total, heads, width = queries.shape
    block = min(512, total)
    count = total // block
    scale = width ** (-0.5)

    def one_block(pair):
        query_block, label_block = pair
        scores = masked_scores(query_block, label_block, keys, labels, scale)
        largest = jnp.max(scores, axis=-1, keepdims=True)
        log_total = largest + jnp.log(jnp.sum(jnp.exp(scores - largest), axis=-1, keepdims=True))
        weights = jnp.exp(scores - log_total).astype(jnp.bfloat16)
        mixed = jnp.einsum("hqk,khd->qhd", weights, values, preferred_element_type=jnp.float32)
        return (mixed.astype(jnp.bfloat16), log_total[..., 0])

    mixed, log_total = lax.map(
        one_block, (queries.reshape(count, block, heads, width), labels.reshape(count, block))
    )
    return (mixed.reshape(total, heads * width), log_total)


def attend_back(queries, keys, values, labels, mixed_grad, log_total):
    total, heads, width = queries.shape
    block = min(512, total)
    count = total // block
    scale = width ** (-0.5)

    def one_block(carry, inputs):
        key_grad, value_grad = carry
        query_block, label_block, out_grad, block_total = inputs
        scores = masked_scores(query_block, label_block, keys, labels, scale)
        probs = jnp.exp(scores - block_total[:, :, None])
        rounded = probs.astype(jnp.bfloat16)
        value_grad = value_grad + jnp.einsum(
            "hqk,qhd->khd", rounded, out_grad, preferred_element_type=jnp.float32
        )
        weight_grad = jnp.einsum(
            "qhd,khd->hqk", out_grad, values, preferred_element_type=jnp.float32
        )
        row_inner = jnp.sum(probs * weight_grad, axis=-1, keepdims=True)
        score_grad = (probs * (weight_grad - row_inner)).astype(jnp.bfloat16)
        query_grad = (
            jnp.einsum("hqk,khd->qhd", score_grad, keys, preferred_element_type=jnp.float32) * scale
        )
        key_grad = (
            key_grad
            + jnp.einsum(
                "hqk,qhd->khd", score_grad, query_block, preferred_element_type=jnp.float32
            )
            * scale
        )
        return ((key_grad, value_grad), query_grad)

    zeros = jnp.zeros((total, heads, width), jnp.float32)
    (key_grad, value_grad), query_grad = lax.scan(
        one_block,
        (zeros, zeros),
        (
            queries.reshape(count, block, heads, width),
            labels.reshape(count, block),
            mixed_grad.reshape(count, block, heads, width),
            log_total,
        ),
    )
    return (query_grad.reshape(total, heads, width), key_grad, value_grad)


def on_device(
    hidden,
    positions,
    segments,
    ln1_gain,
    ln1_bias,
    qkv_weight,
    qkv_bias,
    proj_weight,
    proj_bias,
    ln2_gain,
    ln2_bias,
    fc1_weight,
    fc1_bias,
    fc2_weight,
    fc2_bias,
    cotangent,
):
    batches, rows, width = hidden.shape
    local_cols = qkv_weight.shape[2]
    heads = local_cols // HEAD_DIM
    hidden_units = fc1_weight.shape[1]
    shard_params = (
        ln1_gain,
        ln1_bias,
        qkv_weight,
        proj_weight,
        proj_bias,
        ln2_gain,
        ln2_bias,
        fc1_weight,
        fc2_weight,
        fc2_bias,
    )
    qkv_shift = qkv_bias.astype(jnp.float32)
    qkv_total = jnp.zeros((width, 3, local_cols), jnp.float32)
    proj_total = jnp.zeros((local_cols, width), jnp.float32)
    fc1_total = jnp.zeros((width, hidden_units), jnp.float32)
    fc2_total = jnp.zeros((hidden_units, width), jnp.float32)
    small_total = jnp.zeros((6, width), jnp.float32)
    qkv_bias_total = jnp.zeros((3, local_cols), jnp.float32)
    fc1_bias_total = jnp.zeros((hidden_units,), jnp.float32)
    outputs = []
    input_grads = []
    for batch in range(batches):
        gathered = fetch_weights(shard_params)
        (
            gain_one,
            shift_one,
            qkv_full,
            proj_full,
            proj_shift,
            gain_two,
            shift_two,
            fc1_full,
            fc2_full,
            fc2_shift,
        ) = gathered
        gain_one = gain_one.astype(jnp.float32)
        gain_two = gain_two.astype(jnp.float32)
        start_values = hidden[batch].astype(jnp.float32)
        cosine, sine = angle_tables(positions[batch])
        labels = segments[batch]
        normed, unit_one, spread_one = normalize(
            start_values, gain_one, shift_one.astype(jnp.float32)
        )
        normed_full = share_rows(normed.astype(jnp.bfloat16))
        total = normed_full.shape[0]
        projected = (
            jnp.einsum("pd,dtc->ptc", normed_full, qkv_full, preferred_element_type=jnp.float32)
            + qkv_shift
        )
        queries = rotate(projected[:, 0].reshape(total, heads, HEAD_DIM), cosine, sine).astype(
            jnp.bfloat16
        )
        keys = rotate(projected[:, 1].reshape(total, heads, HEAD_DIM), cosine, sine).astype(
            jnp.bfloat16
        )
        values = projected[:, 2].reshape(total, heads, HEAD_DIM).astype(jnp.bfloat16)
        mixed, log_total = attend(queries, keys, values, labels)
        middle = start_values + branch_sum(mixed, proj_full) + proj_shift.astype(jnp.float32)
        normed_two, unit_two, spread_two = normalize(
            middle, gain_two, shift_two.astype(jnp.float32)
        )
        ffn_input = share_rows(normed_two.astype(jnp.bfloat16))
        before = jnp.dot(ffn_input, fc1_full, preferred_element_type=jnp.float32) + fc1_bias.astype(
            jnp.float32
        )
        sigma = jax.nn.sigmoid(1.702 * before)
        after = (before * sigma).astype(jnp.bfloat16)
        outcome = middle + branch_sum(after, fc2_full) + fc2_shift.astype(jnp.float32)
        outputs.append(outcome.astype(jnp.bfloat16))
        weights_back = fetch_again(shard_params)
        qkv_back = weights_back[2]
        proj_back = weights_back[3]
        out_grad = cotangent[batch]
        out_grad_wide = out_grad.astype(jnp.float32)
        fc1_back = weights_back[7]
        fc2_back = weights_back[8]
        out_grad_full = share_grads(out_grad)
        fc2_total = fc2_total + jnp.einsum(
            "pf,pd->fd", after, out_grad_full, preferred_element_type=jnp.float32
        )
        after_grad = jnp.einsum(
            "pd,fd->pf", out_grad_full, fc2_back, preferred_element_type=jnp.float32
        )
        before_grad = (after_grad * (sigma + 1.702 * before * sigma * (1.0 - sigma))).astype(
            jnp.bfloat16
        )
        fc1_total = fc1_total + jnp.einsum(
            "pd,pf->df", ffn_input, before_grad, preferred_element_type=jnp.float32
        )
        fc1_bias_total = fc1_bias_total + jnp.sum(before_grad.astype(jnp.float32), axis=0)
        normed_two_grad = input_sum(before_grad, fc1_back, "pf,df->pd")
        middle_grad = out_grad_wide + normalize_back(
            normed_two_grad, unit_two, spread_two, gain_two
        )
        branch_grad_full = share_grads(middle_grad.astype(jnp.bfloat16))
        proj_total = proj_total + jnp.einsum(
            "pc,pd->cd", mixed, branch_grad_full, preferred_element_type=jnp.float32
        )
        mixed_grad = jnp.einsum(
            "pd,cd->pc", branch_grad_full, proj_back, preferred_element_type=jnp.float32
        ).astype(jnp.bfloat16)
        query_turned, key_turned, value_grad = attend_back(
            queries, keys, values, labels, mixed_grad.reshape(total, heads, HEAD_DIM), log_total
        )
        query_grad = rotate_back(query_turned, cosine, sine).reshape(total, local_cols)
        key_grad = rotate_back(key_turned, cosine, sine).reshape(total, local_cols)
        projected_grad = jnp.stack(
            [query_grad, key_grad, value_grad.reshape(total, local_cols)], axis=1
        ).astype(jnp.bfloat16)
        qkv_bias_total = qkv_bias_total + jnp.sum(projected_grad.astype(jnp.float32), axis=0)
        qkv_total = qkv_total + jnp.einsum(
            "pd,ptc->dtc", normed_full, projected_grad, preferred_element_type=jnp.float32
        )
        normed_grad = input_sum(projected_grad, qkv_back, "ptc,dtc->pd")
        input_grads.append(
            (middle_grad + normalize_back(normed_grad, unit_one, spread_one, gain_one)).astype(
                jnp.bfloat16
            )
        )
        small_total = small_total + jnp.stack(
            [
                jnp.sum(normed_grad * unit_one, axis=0),
                jnp.sum(normed_grad, axis=0),
                jnp.sum(middle_grad, axis=0),
                jnp.sum(normed_two_grad * unit_two, axis=0),
                jnp.sum(normed_two_grad, axis=0),
                jnp.sum(out_grad_wide, axis=0),
            ]
        )
    qkv_part, proj_part, fc1_part, fc2_part, small_part = (
        lax.psum_scatter(qkv_total, "fsdp", scatter_dimension=0, tiled=True),
        lax.psum_scatter(proj_total, "fsdp", scatter_dimension=1, tiled=True),
        lax.psum_scatter(fc1_total, "fsdp", scatter_dimension=0, tiled=True),
        lax.psum_scatter(fc2_total, "fsdp", scatter_dimension=1, tiled=True),
        lax.psum_scatter(small_total, "fsdp", scatter_dimension=1, tiled=True),
    )
    small_sums = lax.psum(small_part, "tensor")
    qkv_bias_sum, fc1_bias_sum = lax.psum((qkv_bias_total, fc1_bias_total), "fsdp")
    return (
        jnp.stack(outputs),
        jnp.stack(input_grads),
        small_sums[0],
        small_sums[1],
        qkv_part,
        qkv_bias_sum,
        proj_part,
        small_sums[2],
        small_sums[3],
        small_sums[4],
        fc1_part,
        fc1_bias_sum,
        fc2_part,
        small_sums[5],
    )


def solution(mesh):
    in_specs = (
        P("fsdp", "tensor", None),
        P("fsdp", None, None),
        P("fsdp", None),
        P("fsdp"),
        P("fsdp"),
        P("fsdp", None, "tensor"),
        P(None, "tensor"),
        P("tensor", "fsdp"),
        P("fsdp"),
        P("fsdp"),
        P("fsdp"),
        P("fsdp", "tensor"),
        P("tensor"),
        P("tensor", "fsdp"),
        P("fsdp"),
        P("fsdp", "tensor", None),
    )
    out_specs = (
        P("fsdp", "tensor", None),
        P("fsdp", "tensor", None),
        P("fsdp"),
        P("fsdp"),
        P("fsdp", None, "tensor"),
        P(None, "tensor"),
        P("tensor", "fsdp"),
        P("fsdp"),
        P("fsdp"),
        P("fsdp"),
        P("fsdp", "tensor"),
        P("tensor"),
        P("tensor", "fsdp"),
        P("fsdp"),
    )
    return jax.shard_map(
        on_device, mesh=mesh, in_specs=in_specs, out_specs=out_specs, check_vma=False
    )
```

profile of v0, /device:TPU:11, one launch (start us, length us, event | category | flops | bytes accessed | tf_op | source)
XLA Modules:
  0.0 1862.2 jit_solution(4578080762869005025)
XLA Ops:
  15.0 22.9 %all-reduce.7 = (bf16[1280]{0:T(1024)(128)(2,1)}, bf16[1280]{0:T(1024)(128)(2,1)S(1)}, bf16[1280]{0:T(1024)(128)(2,1)S(1)}, bf16[1280]{0:T(1024)(128)(2,1)}, bf1...) all-reduce(bf16[1280]{0:T(1024)(128)(2,1)S(1)} %dynamic-update-slice.2,, ...), channel_id=1, replica_groups=mesh['fsdp'=8,'tensor'=4] {'fsdp'}, use_global_device_ids=true, to_apply=%add.2 | all-reduce | flops 7680 | bytes 30720
  73.9 44.6 %all-gather.14.cloned.1.call-done = bf16[1536,1280]{1,0:T(8,128)(2,1)} async-done(((bf16[384,1280]{1,0:T(8,128)(2,1)}), bf16[1536,1280]{1,0:T(8,128)(2,1)}) %all-gather.14.cloned.1.call-update) | async-done | bytes 3932176 | tf_op jit(solution)/shard_map/all_gather | solution.py:83
  128.5 66.7 %all-gather.24.cloned.1.call-done = bf16[1536,1280]{1,0:T(8,128)(2,1)} async-done(((bf16[384,1280]{1,0:T(8,128)(2,1)}), bf16[1536,1280]{1,0:T(8,128)(2,1)}) %all-gather.24.cloned.1.call-update) | async-done | bytes 3932176 | tf_op jit(solution)/shard_map/all_gather | solution.py:83
  226.4 49.9 %while.54 = (s32[]{:T(128)}, bf16[3,512,4,80]{1,3,2,0:T(8,128)(2,1)}, f32[3,4,512]{2,1,0:T(4,128)S(1)}, s32[3,512]{1,0:T(4,128)S(1)}, s32[1,1536]{1,0:T(1,128)S(...) while((s32[]{:T(128)}, ...), condition=%wide.region_5.6_spmd, body=%wide.region_2.5_spmd.sunk | while | flops 1042184192 | bytes 93937816 | solution.py:131
  302.4 48.5 %while.55 = (s32[]{:T(128)}, bf16[3,512,4,80]{1,3,2,0:T(8,128)(2,1)S(1)}, f32[3,4,512]{2,1,0:T(4,128)S(1)}, s32[3,512]{1,0:T(4,128)S(1)}, s32[1,1536]{1,0:T(1,12...) while((s32[]{:T(128)}, ...), condition=%wide.region_15.16_spmd, body=%wide.region_12.15_spmd.sunk | while | flops 1042184192 | bytes 93937816 | solution.py:131
  358.3 75.2 %reduce-scatter.20.cloned.1.call-done = bf16[384,1280]{1,0:T(8,128)(2,1)} async-done(((bf16[1536,1280]{1,0:T(8,128)(2,1)}), bf16[384,1280]{1,0:T(8,128)(2,1)}) %reduce-scatter.20.cloned.1.call-update) | async-done | bytes 983056 | tf_op jit(solution)/shard_map/reduce_scatter | solution.py:91
  444.4 24.6 %all-gather.20.cloned.1.call-done = bf16[1280,1280]{1,0:T(8,128)(2,1)} async-done(((bf16[160,1280]{1,0:T(8,128)(2,1)}), bf16[1280,1280]{1,0:T(8,128)(2,1)}) %all-gather.20.cloned.1.call-update) | async-done | bytes 3276816 | tf_op jit(solution)/shard_map/all_gather | solution.py:61
  469.0 75.6 %all-gather.26.cloned.1.call-done = bf16[1536,1280]{1,0:T(8,128)(2,1)} async-done(((bf16[384,1280]{1,0:T(8,128)(2,1)}), bf16[1536,1280]{1,0:T(8,128)(2,1)}) %all-gather.26.cloned.1.call-update) | async-done | bytes 3932176 | tf_op jit(solution)/shard_map/all_gather | solution.py:83
  554.4 26.4 %all-gather.22.cloned.1.call-done = bf16[1280,1280]{0,1:T(8,128)(2,1)} async-done(((bf16[1280,160]{0,1:T(8,128)(2,1)}), bf16[1280,1280]{0,1:T(8,128)(2,1)}) %all-gather.22.cloned.1.call-update) | async-done | bytes 3276816 | tf_op jit(solution)/shard_map/all_gather | solution.py:62
  591.7 64.1 %all-gather.34.cloned.1.call-done = bf16[1,1536,1280]{2,1,0:T(8,128)(2,1)} async-done(((bf16[1,384,1280]{2,1,0:T(8,128)(2,1)}), bf16[1,1536,1280]{2,1,0:T(8,128)(2,1)}) %all-gather.34.cloned.1.call-update) | async-done | bytes 3932176 | tf_op jit(solution)/shard_map/all_gather | solution.py:87
  676.9 55.9 %all-gather.18.cloned.1.call-done = bf16[1536,1280]{1,0:T(8,128)(2,1)} async-done(((bf16[384,1280]{1,0:T(8,128)(2,1)}), bf16[1536,1280]{1,0:T(8,128)(2,1)}) %all-gather.18.cloned.1.call-update) | async-done | bytes 3932176 | tf_op jit(solution)/shard_map/all_gather | solution.py:83
  752.6 56.7 %all-gather.32.cloned.1.call-done = bf16[1,1536,1280]{2,1,0:T(8,128)(2,1)} async-done(((bf16[1,384,1280]{2,1,0:T(8,128)(2,1)}), bf16[1,1536,1280]{2,1,0:T(8,128)(2,1)}) %all-gather.32.cloned.1.call-update) | async-done | bytes 3932176 | tf_op jit(solution)/shard_map/all_gather | solution.py:87
  830.8 54.4 %reduce-scatter.22.cloned.1.call-done = bf16[384,1280]{1,0:T(8,128)(2,1)} async-done(((bf16[1536,1280]{1,0:T(8,128)(2,1)}), bf16[384,1280]{1,0:T(8,128)(2,1)}) %reduce-scatter.22.cloned.1.call-update) | async-done | bytes 983056 | tf_op jit(solution)/shard_map/reduce_scatter | solution.py:91
  885.1 75.4 %reduce-scatter.28.cloned.1.call-done = bf16[384,1280]{1,0:T(8,128)(2,1)} async-done(((bf16[1536,1280]{1,0:T(8,128)(2,1)}), bf16[384,1280]{1,0:T(8,128)(2,1)}) %reduce-scatter.28.cloned.1.call-update) | async-done | bytes 983056 | tf_op jit(solution)/shard_map/reduce_scatter | solution.py:100
  960.5 75.3 %reduce-scatter.18.cloned.1.call-done = bf16[384,1280]{1,0:T(8,128)(2,1)} async-done(((bf16[1536,1280]{1,0:T(8,128)(2,1)}), bf16[384,1280]{1,0:T(8,128)(2,1)}) %reduce-scatter.18.cloned.1.call-update) | async-done | bytes 983056 | tf_op jit(solution)/shard_map/reduce_scatter | solution.py:91
  1035.8 75.2 %reduce-scatter.24.cloned.1.call-done = bf16[384,1280]{1,0:T(8,128)(2,1)} async-done(((bf16[1536,1280]{1,0:T(8,128)(2,1)}), bf16[384,1280]{1,0:T(8,128)(2,1)}) %reduce-scatter.24.cloned.1.call-update) | async-done | bytes 983056 | tf_op jit(solution)/shard_map/reduce_scatter | solution.py:100
  1124.7 73.3 %all-gather.28.cloned.1.call-done = bf16[1536,1280]{1,0:T(8,128)(2,1)} async-done(((bf16[384,1280]{1,0:T(8,128)(2,1)}), bf16[1536,1280]{1,0:T(8,128)(2,1)}) %all-gather.28.cloned.1.call-update) | async-done | bytes 3932176 | tf_op jit(solution)/shard_map/all_gather | solution.py:87
  1208.9 115.3 %while.56 = (s32[]{:T(128)}, f32[1536,4,80]{0,2,1:T(8,128)}, f32[1536,4,80]{0,2,1:T(8,128)}, f32[3,512,4,80]{1,0,3,2:T(4,128)}, bf16[3,512,4,80]{1,3,2,0:T(8,128...) while((s32[]{:T(128)}, f32[1536,4,80]{0,2,1:T(8,128)}, ...), condition=%wide.region_25.26_spmd.clone, body=%wide.region_23.25_spmd.clone.sunk | while | flops 2548299776 | bytes 156238128 | solution.py:170
  1360.3 115.0 %while.57 = (s32[]{:T(128)}, f32[1536,4,80]{0,2,1:T(8,128)}, f32[1536,4,80]{0,2,1:T(8,128)}, f32[3,512,4,80]{1,0,3,2:T(4,128)}, bf16[3,512,4,80]{1,3,2,0:T(8,128...) while((s32[]{:T(128)}, f32[1536,4,80]{0,2,1:T(8,128)}, ...), condition=%wide.region_34.35_spmd.clone, body=%wide.region_32.34_spmd.clone.sunk | while | flops 2548299776 | bytes 156238128 | solution.py:170
  1513.1 59.9 %reduce-scatter.30.cloned.1.call-done = bf16[384,1280]{1,0:T(8,128)(2,1)} async-done(((bf16[1536,1280]{1,0:T(8,128)(2,1)}), bf16[384,1280]{1,0:T(8,128)(2,1)}) %reduce-scatter.30.cloned.1.call-update) | async-done | bytes 983056 | tf_op jit(solution)/shard_map/reduce_scatter | solution.py:100
  1639.0 23.6 %all-reduce.6 = (f32[3,320]{1,0:T(4,128)}, f32[1280]{0:T(1024)}) all-reduce(f32[3,320]{1,0:T(4,128)S(1)} %add.349, f32[1280]{0:T(1024)S(1)} %add.352), channel_id=1, replica_groups=mesh['fsdp'=8,'tensor'=4] {'fsdp'}, use_global_device_ids=true, to_apply=%region_55.56 | all-reduce | flops 2240 | bytes 17920 | tf_op jit(solution)/shard_map/psum | solution.py:343
  1680.3 67.1 %reduce-scatter.36.cloned.1.call-done = f32[160,1280]{1,0:T(8,128)} async-done(((f32[1280,1280]{1,0:T(8,128)}), f32[160,1280]{1,0:T(8,128)}) %reduce-scatter.36.cloned.1.call-update) | async-done | bytes 819216 | tf_op jit(solution)/shard_map/reduce_scatter | solution.py:338
  1747.4 44.2 %reduce-scatter.34.cloned.1.call-done = f32[320,160]{0,1:T(8,128)} async-done(((f32[320,1280]{0,1:T(8,128)}), f32[320,160]{0,1:T(8,128)}) %reduce-scatter.34.cloned.1.call-update) | async-done | bytes 204816 | tf_op jit(solution)/shard_map/reduce_scatter | solution.py:337
  1791.6 63.4 %reduce-scatter.32.cloned.1.call-done = f32[160,3,320]{2,0,1:T(8,128)} async-done(((f32[1280,3,320]{2,0,1:T(8,128)}), f32[160,3,320]{2,0,1:T(8,128)}) %reduce-scatter.32.cloned.1.call-update) | async-done | bytes 614416 | tf_op jit(solution)/shard_map/reduce_scatter | solution.py:336
  (619 shorter events, 719.8 us)
Async XLA Ops:
  7.2 66.7 %all-gather.16.cloned.1.call-start = ((), (), s32[]{:S(2)}) async-start(), calls=%async_computation.14 | async-start | bytes 3317760 | tf_op jit(solution)/shard_map/all_gather | solution.py:56
  7.9 110.6 %all-gather.14.cloned.1.call-start = ((), (), s32[]{:S(2)}) async-start(), calls=%async_computation.13 | async-start | bytes 4915200 | tf_op jit(solution)/shard_map/all_gather | solution.py:83
  42.6 152.5 %all-gather.24.cloned.1.call-start = ((), (), s32[]{:S(2)}) async-start(), calls=%async_computation.20 | async-start | bytes 4915200 | tf_op jit(solution)/shard_map/all_gather | solution.py:83
  43.4 314.9 %reduce-scatter.16.cloned.1.call-start = ((), (), s32[]{:S(2)}) async-start(), calls=%async_computation.15 | async-start | bytes 4915200 | tf_op jit(solution)/shard_map/reduce_scatter | solution.py:91
  284.5 149.0 %reduce-scatter.20.cloned.1.call-start = ((), (), s32[]{:S(2)}) async-start(), calls=%async_computation.21 | async-start | bytes 4915200 | tf_op jit(solution)/shard_map/reduce_scatter | solution.py:91
  357.2 111.8 %all-gather.20.cloned.1.call-start = ((), (), s32[]{:S(2)}) async-start(), calls=%async_computation.17 | async-start | bytes 3686400 | tf_op jit(solution)/shard_map/all_gather | solution.py:61
  357.8 186.8 %all-gather.26.cloned.1.call-start = ((), (), s32[]{:S(2)}) async-start(), calls=%async_computation.22 | async-start | bytes 4915200 | tf_op jit(solution)/shard_map/all_gather | solution.py:83
  439.3 141.5 %all-gather.22.cloned.1.call-start = ((), (), s32[]{:S(2)}) async-start(), calls=%async_computation.18 | async-start | bytes 3686400 | tf_op jit(solution)/shard_map/all_gather | solution.py:62
  440.1 215.7 %all-gather.34.cloned.1.call-start = ((), (), s32[]{:S(2)}) async-start(), calls=%async_computation.35 | async-start | bytes 4915200 | tf_op jit(solution)/shard_map/all_gather | solution.py:87
  443.0 289.7 %all-gather.18.cloned.1.call-start = ((), (), s32[]{:S(2)}) async-start(), calls=%async_computation.16 | async-start | bytes 4915200 | tf_op jit(solution)/shard_map/all_gather | solution.py:83
  443.6 365.7 %all-gather.32.cloned.1.call-start = ((), (), s32[]{:S(2)}) async-start(), calls=%async_computation.34 | async-start | bytes 4915200 | tf_op jit(solution)/shard_map/all_gather | solution.py:87
  444.4 440.8 %reduce-scatter.22.cloned.1.call-start = ((), (), s32[]{:S(2)}) async-start(), calls=%async_computation.23 | async-start | bytes 4915200 | tf_op jit(solution)/shard_map/reduce_scatter | solution.py:91
  591.7 368.8 %reduce-scatter.28.cloned.1.call-start = ((), (), s32[]{:S(2)}) async-start(), calls=%async_computation.27 | async-start | bytes 4915200 | tf_op jit(solution)/shard_map/reduce_scatter | solution.py:100
  676.8 359.0 %reduce-scatter.18.cloned.1.call-start = ((), (), s32[]{:S(2)}) async-start(), calls=%async_computation.19 | async-start | bytes 4915200 | tf_op jit(solution)/shard_map/reduce_scatter | solution.py:91
  752.6 358.4 %reduce-scatter.24.cloned.1.call-start = ((), (), s32[]{:S(2)}) async-start(), calls=%async_computation.24 | async-start | bytes 4915200 | tf_op jit(solution)/shard_map/reduce_scatter | solution.py:100
  830.1 367.9 %all-gather.28.cloned.1.call-start = ((), (), s32[]{:S(2)}) async-start(), calls=%async_computation.25 | async-start | bytes 4915200 | tf_op jit(solution)/shard_map/all_gather | solution.py:87
  1123.5 210.9 %all-gather.30.cloned.1.call-start = ((), (), s32[]{:S(2)}) async-start(), calls=%async_computation.28 | async-start | bytes 4915200 | tf_op jit(solution)/shard_map/all_gather | solution.py:87
  1124.7 388.4 %reduce-scatter.26.cloned.1.call-start = ((), (), s32[]{:S(2)}) async-start(), calls=%async_computation.26 | async-start | bytes 4915200 | tf_op jit(solution)/shard_map/reduce_scatter | solution.py:100
  1358.3 214.7 %reduce-scatter.30.cloned.1.call-start = ((), (), s32[]{:S(2)}) async-start(), calls=%async_computation.29 | async-start | bytes 4915200 | tf_op jit(solution)/shard_map/reduce_scatter | solution.py:100
  1499.4 167.9 %reduce-scatter.40.cloned.1.call-start = ((), (), s32[]{:S(2)}) async-start(), calls=%async_computation.36 | async-start | bytes 737280
  1577.6 102.7 %reduce-scatter.38.cloned.1.call-start = ((), (), s32[]{:S(2)}) async-start(), calls=%async_computation.33 | async-start | bytes 7372800 | tf_op jit(solution)/shard_map/reduce_scatter | solution.py:339
  1592.4 155.0 %reduce-scatter.36.cloned.1.call-start = ((), (), s32[]{:S(2)}) async-start(), calls=%async_computation.32 | async-start | bytes 7372800 | tf_op jit(solution)/shard_map/reduce_scatter | solution.py:338
  1609.2 182.4 %reduce-scatter.34.cloned.1.call-start = ((), (), s32[]{:S(2)}) async-start(), calls=%async_computation.31 | async-start | bytes 2211840 | tf_op jit(solution)/shard_map/reduce_scatter | solution.py:337
  1618.5 236.5 %reduce-scatter.32.cloned.1.call-start = ((), (), s32[]{:S(2)}) async-start(), calls=%async_computation.30 | async-start | bytes 6635520 | tf_op jit(solution)/shard_map/reduce_scatter | solution.py:336
  (140 other events, 2017.9 us)
Sparse Core Ops, SparseCore 0:
  9.9 32.9 all-gather.15
  45.1 73.4 all-gather.13
  120.1 74.9 all-gather.23
  284.7 73.5 reduce-scatter.15
  360.4 73.0 reduce-scatter.19
  435.3 33.6 all-gather.19
  471.2 73.3 all-gather.25
  546.5 34.2 all-gather.21
  582.4 73.3 all-gather.33
  657.8 74.9 all-gather.17
  734.4 74.9 all-gather.31
  811.5 73.6 reduce-scatter.21
  887.4 73.0 reduce-scatter.27
  962.7 73.0 reduce-scatter.17
  1037.9 73.0 reduce-scatter.23
  1123.6 74.3 all-gather.27
  1199.5 74.9 all-gather.29
  1358.4 73.5 reduce-scatter.25
  1499.5 73.4 reduce-scatter.29
  1577.8 34.7 reduce-scatter.39
  1616.6 63.6 reduce-scatter.37
  1684.3 63.0 reduce-scatter.35
  1751.4 40.1 reduce-scatter.33
  1795.5 59.4 reduce-scatter.31
where the time goes:
time: 1870 us; the launch traced here: 1860 us
  waiting for transfers between devices  1090 us (58%)
  matrix products  361 us (19%)
  local copies, waits for them, and re-layouts  202 us (11%)
  other arithmetic  126 us (7%)
  blocking collectives  68.2 us (4%)
    all_gather x4, waiting for transfers between devices, share_rows(): return lax.all_gather(values, 'tensor', axis=0, tiled=True)  243 us
    reduce_scatter x4, waiting for transfers between devices, input_sum(): lax.psum_scatter(jnp.einsum(form, left, right, preferred_element_type=jnp...  211 us
    reduce_scatter x4, waiting for transfers between devices, branch_sum(): lax.psum_scatter(jnp.dot(left, right, preferred_element_type=jnp.float32)...  205 us
    all_gather x4, waiting for transfers between devices, share_grads(): return lax.all_gather(values, 'tensor', axis=0, tiled=True)  194 us
    dynamic_update_slice x12, local copies, waits for them, and re-layouts, attend_back(): lax.scan(one_block, (zeros, zeros), (queries.reshape(count, block, heads,...  85.6 us
    reduce_scatter x1, waiting for transfers between devices, on_device(): lax.psum_scatter(fc1_total, 'fsdp', scatter_dimension=0, tiled=True)  67.1 us
    reduce_scatter x1, waiting for transfers between devices, on_device(): lax.psum_scatter(qkv_total, 'fsdp', scatter_dimension=0, tiled=True)  63.4 us
    dot_general x12, matrix products, masked_scores(): jnp.einsum('qhd,khd->hqk', query_block, keys, preferred_element_type=jnp....  52.3 us
  transfers between devices with their start and end apart: 24, of which 20 were waited for; matrix products, arithmetic and copies ran while one was open for 29% of the time, Pallas kernels for 0%

commit v1 on v0

v1 whole, which is shorter than its diff:
```python
import jax
import jax.numpy as jnp
from jax import lax
from jax.sharding import Mesh, PartitionSpec as P

HEAD_DIM = 80

epsilon = 1e-06


def angle_tables(place):
    quarter = HEAD_DIM // 4
    freqs = 10000.0 ** (-(4.0 * jnp.arange(quarter, dtype=jnp.float32)) / HEAD_DIM)
    row_angles = place[0].astype(jnp.float32)[:, None] * freqs[None, :]
    col_angles = place[1].astype(jnp.float32)[:, None] * freqs[None, :]
    halfway = jnp.concatenate([row_angles, col_angles], axis=1)
    angles = jnp.concatenate([halfway, halfway], axis=1)
    return (jnp.cos(angles), jnp.sin(angles))


def rotate(values, cosine, sine):
    middle_index = HEAD_DIM // 2
    turned = jnp.concatenate([-values[..., middle_index:], values[..., :middle_index]], axis=-1)
    return values * cosine[:, None, :] + turned * sine[:, None, :]


def rotate_back(grads, cosine, sine):
    middle_index = HEAD_DIM // 2
    scaled = grads * sine[:, None, :]
    turned = jnp.concatenate([scaled[..., middle_index:], -scaled[..., :middle_index]], axis=-1)
    return grads * cosine[:, None, :] + turned


def normalize(values, gain, shift):
    center = values - jnp.mean(values, axis=-1, keepdims=True)
    spread = lax.rsqrt(jnp.mean(center * center, axis=-1, keepdims=True) + epsilon)
    unit = center * spread
    return (unit * gain + shift, unit, spread)


def normalize_back(grads, unit, spread, gain):
    scaled = grads * gain
    inner = (
        scaled
        - jnp.mean(scaled, axis=-1, keepdims=True)
        - unit * jnp.mean(scaled * unit, axis=-1, keepdims=True)
    )
    return inner * spread


def masked_scores(query_block, label_block, keys, labels, scale):
    scores = (
        jnp.einsum("qhd,khd->hqk", query_block, keys, preferred_element_type=jnp.float32) * scale
    )
    same_image = label_block[:, None] == labels[None, :]
    return jnp.where(same_image[None, :, :], scores, -1000000000.0)


def attend(queries, keys, values, labels):
    total, heads, width = queries.shape
    block = min(512, total)
    count = total // block
    scale = width ** (-0.5)

    def one_block(pair):
        query_block, label_block = pair
        scores = masked_scores(query_block, label_block, keys, labels, scale)
        largest = jnp.max(scores, axis=-1, keepdims=True)
        log_total = largest + jnp.log(jnp.sum(jnp.exp(scores - largest), axis=-1, keepdims=True))
        weights = jnp.exp(scores - log_total).astype(jnp.bfloat16)
        mixed = jnp.einsum("hqk,khd->qhd", weights, values, preferred_element_type=jnp.float32)
        return (mixed.astype(jnp.bfloat16), log_total[..., 0])

    mixed, log_total = lax.map(
        one_block, (queries.reshape(count, block, heads, width), labels.reshape(count, block))
    )
    return (mixed.reshape(total, heads * width), log_total)


def attend_back(queries, keys, values, labels, mixed_grad, log_total):
    total, heads, width = queries.shape
    block = min(512, total)
    count = total // block
    scale = width ** (-0.5)

    def one_block(carry, inputs):
        key_grad, value_grad = carry
        query_block, label_block, out_grad, block_total = inputs
        scores = masked_scores(query_block, label_block, keys, labels, scale)
        probs = jnp.exp(scores - block_total[:, :, None])
        rounded = probs.astype(jnp.bfloat16)
        value_grad = value_grad + jnp.einsum(
            "hqk,qhd->khd", rounded, out_grad, preferred_element_type=jnp.float32
        )
        weight_grad = jnp.einsum(
            "qhd,khd->hqk", out_grad, values, preferred_element_type=jnp.float32
        )
        row_inner = jnp.sum(probs * weight_grad, axis=-1, keepdims=True)
        score_grad = (probs * (weight_grad - row_inner)).astype(jnp.bfloat16)
        query_grad = (
            jnp.einsum("hqk,khd->qhd", score_grad, keys, preferred_element_type=jnp.float32) * scale
        )
        key_grad = (
            key_grad
            + jnp.einsum(
                "hqk,qhd->khd", score_grad, query_block, preferred_element_type=jnp.float32
            )
            * scale
        )
        return ((key_grad, value_grad), query_grad)

    zeros = jnp.zeros((total, heads, width), jnp.float32)
    (key_grad, value_grad), query_grad = lax.scan(
        one_block,
        (zeros, zeros),
        (
            queries.reshape(count, block, heads, width),
            labels.reshape(count, block),
            mixed_grad.reshape(count, block, heads, width),
            log_total,
        ),
    )
    return (query_grad.reshape(total, heads, width), key_grad, value_grad)


def swap(values):
    return lax.ppermute(values, "c", [(0, 1), (1, 0)])


def travel(step, size):
    runs = size // 2
    pairs = []
    for core in range(2):
        for place in range(size):
            half, part = divmod(place, runs)
            pairs.append((core * size + place, half * size + runs * core + (part + step) % runs))
    return pairs


def bring(packs, place, size):
    runs = size // 2
    parts = [
        lax.ppermute(
            lax.dynamic_index_in_dim(packs, lax.rem(place + step, runs), 0, keepdims=False),
            ("c", "z"),
            travel(step, size),
        )
        for step in range(runs)
    ]
    return jnp.concatenate(parts, axis=0)


def take_back(rows, place, size):
    runs = size // 2
    count = rows.shape[0] // runs
    parts = jnp.stack(
        [
            lax.ppermute(
                rows[step * count : (step + 1) * count],
                ("c", "z"),
                [(target, source) for source, target in travel(step, size)],
            )
            for step in range(runs)
        ]
    )
    return jnp.stack(
        [
            lax.dynamic_index_in_dim(
                parts, lax.rem(index + size - place, runs), 0, keepdims=False
            )
            for index in range(runs)
        ]
    )


def pair_sum(partial):
    count = partial.shape[0] // 2
    return partial[:count] + swap(partial[count:].astype(jnp.bfloat16)).astype(jnp.float32)


def share(own):
    return jnp.concatenate([own, swap(own)], axis=0)


def gather_all(block):
    return lax.all_gather(block, ("z", "g"), axis=0, tiled=True)


def scatter_all(total):
    depth, cols = total.shape[-2:]
    return lax.psum_scatter(
        total.reshape(-1, cols), ("z", "g"), scatter_dimension=0, tiled=True
    )


def dot(form, left, right):
    return jnp.einsum(form, left, right, preferred_element_type=jnp.float32)


def on_device(
    hidden,
    positions,
    segments,
    ln1_gain,
    ln1_bias,
    qkv_weight,
    qkv_bias,
    proj_weight,
    proj_bias,
    ln2_gain,
    ln2_bias,
    fc1_weight,
    fc1_bias,
    fc2_weight,
    fc2_bias,
    cotangent,
):
    wide = jnp.float32
    size = lax.axis_size("z")
    core = lax.axis_index("c")
    place = lax.axis_index("z")
    group = lax.axis_index("g")
    batches, rows, width = hidden.shape
    runs = size // 2
    assert batches == runs
    shard = qkv_weight.shape[0]
    local_cols = qkv_weight.shape[2]
    half_cols = local_cols // 2
    units = fc1_weight.shape[1]
    half_units = units // 2
    heads = size * half_cols // HEAD_DIM
    total = 2 * runs * rows
    first = core == 0

    first_part = jnp.concatenate(
        [
            qkv_weight.reshape(shard, 3, 2, half_cols).transpose(0, 2, 1, 3).reshape(
                shard, 2, 3 * half_cols
            ),
            proj_weight.T.reshape(shard, 2, half_cols),
        ],
        axis=2,
    )
    packed = jnp.concatenate(
        [
            first_part,
            fc1_weight.reshape(shard, 2, half_units),
            fc2_weight.T.reshape(shard, 2, half_units),
        ],
        axis=2,
    )
    keep = jnp.where(first, packed[:, 0], packed[:, 1])
    other = swap(jnp.where(first, packed[:, 1], packed[:, 0]))
    block = jnp.where(
        first, jnp.concatenate([keep, other], axis=0), jnp.concatenate([other, keep], axis=0)
    )
    attn_cols = 4 * half_cols
    attn_full = gather_all(block[:, :attn_cols]).reshape(size, width, attn_cols)
    fc1_full = gather_all(block[:, attn_cols : attn_cols + half_units]).reshape(
        size, width, half_units
    )
    fc2_full = gather_all(block[:, attn_cols + half_units :]).reshape(size, width, half_units)
    qkv_full = attn_full[:, :, : 3 * half_cols].reshape(size, width, 3, half_cols)
    proj_full = attn_full[:, :, 3 * half_cols :]

    small = jnp.concatenate(
        [
            ln1_gain,
            ln1_bias,
            proj_bias,
            ln2_gain,
            ln2_bias,
            fc2_bias,
            qkv_bias.reshape(-1),
            fc1_bias,
        ]
    )
    small_full = lax.all_gather(small, ("g", "c", "z"), axis=0).reshape(-1, size, small.shape[0])
    vectors = (
        small_full[:, 0, : 6 * shard].reshape(-1, 6, shard).transpose(1, 0, 2).reshape(6, width)
    ).astype(wide)
    gain_one, shift_one, proj_shift, gain_two, shift_two, fc2_shift = (
        vectors[index] for index in range(6)
    )
    tail = small_full[0, :, 6 * shard :].astype(wide)
    qkv_shifts = tail[:, : 3 * local_cols].reshape(size, 3, 2, half_cols)
    qkv_shift = jnp.where(first, qkv_shifts[:, :, 0], qkv_shifts[:, :, 1]).transpose(1, 0, 2)
    fc1_shifts = tail[:, 3 * local_cols :].reshape(size, 2, half_units)
    fc1_shift = jnp.where(first, fc1_shifts[:, 0], fc1_shifts[:, 1])

    marks = jnp.concatenate([positions, segments[:, None, :]], axis=1)
    marks_other = swap(marks)
    own_pack = place // runs == core
    batch = lax.rem(place, runs)
    marks = lax.dynamic_index_in_dim(
        jnp.where(own_pack, marks, marks_other), batch, 0, keepdims=False
    ).reshape(3, size, rows)
    order = [
        runs * (core if side == 0 else 1 - core) + lax.rem(batch + runs - step, runs)
        for side in range(2)
        for step in range(runs)
    ]
    marks = jnp.concatenate(
        [lax.dynamic_index_in_dim(marks, index, 1, keepdims=False) for index in order], axis=1
    )
    cosine, sine = angle_tables(marks[:2])
    labels = marks[2]

    start_values = bring(hidden, place, size).astype(wide)
    out_grad = bring(cotangent, place, size)
    normed, unit_one, spread_one = normalize(start_values, gain_one, shift_one)
    normed_full = share(normed.astype(jnp.bfloat16))
    projected = dot("pd,zdtc->ptzc", normed_full, qkv_full) + qkv_shift
    split = projected.reshape(total, 3, heads, HEAD_DIM)
    queries = rotate(split[:, 0], cosine, sine).astype(jnp.bfloat16)
    keys = rotate(split[:, 1], cosine, sine).astype(jnp.bfloat16)
    values = split[:, 2].astype(jnp.bfloat16)
    mixed, log_total = attend(queries, keys, values, labels)
    mixed = mixed.reshape(total, size, half_cols)
    middle = start_values + pair_sum(dot("pzk,zdk->pd", mixed, proj_full)) + proj_shift
    normed_two, unit_two, spread_two = normalize(middle, gain_two, shift_two)
    ffn_input = share(normed_two.astype(jnp.bfloat16))
    before = dot("pd,zdf->pzf", ffn_input, fc1_full) + fc1_shift
    sigma = jax.nn.sigmoid(1.702 * before)
    after = (before * sigma).astype(jnp.bfloat16)
    outcome = middle + pair_sum(dot("pzf,zdf->pd", after, fc2_full)) + fc2_shift
    output = take_back(outcome.astype(jnp.bfloat16), place, size)

    out_grad_wide = out_grad.astype(wide)
    out_grad_full = share(out_grad)
    fc2_part = scatter_all(dot("pd,pzf->zdf", out_grad_full, after).astype(jnp.bfloat16))
    after_grad = dot("pd,zdf->pzf", out_grad_full, fc2_full)
    before_grad = (after_grad * (sigma + 1.702 * before * sigma * (1.0 - sigma))).astype(
        jnp.bfloat16
    )
    fc1_part = scatter_all(dot("pd,pzf->zdf", ffn_input, before_grad).astype(jnp.bfloat16))
    fc1_bias_total = jnp.sum(before_grad.astype(wide), axis=0)
    normed_two_grad = pair_sum(dot("pzf,zdf->pd", before_grad, fc1_full))
    middle_grad = out_grad_wide + normalize_back(normed_two_grad, unit_two, spread_two, gain_two)
    branch_grad_full = share(middle_grad.astype(jnp.bfloat16))
    proj_grad = dot("pd,pzk->zdk", branch_grad_full, mixed).astype(jnp.bfloat16)
    mixed_grad = dot("pd,zdk->pzk", branch_grad_full, proj_full).astype(jnp.bfloat16)
    query_turned, key_turned, value_grad = attend_back(
        queries, keys, values, labels, mixed_grad.reshape(total, heads, HEAD_DIM), log_total
    )
    projected_grad = jnp.stack(
        [
            rotate_back(query_turned, cosine, sine).reshape(total, size, half_cols),
            rotate_back(key_turned, cosine, sine).reshape(total, size, half_cols),
            value_grad.reshape(total, size, half_cols),
        ],
        axis=2,
    ).astype(jnp.bfloat16)
    qkv_bias_total = jnp.sum(projected_grad.astype(wide), axis=0)
    qkv_grad = dot("pd,pztc->zdtc", normed_full, projected_grad).astype(jnp.bfloat16)
    attn_part = scatter_all(
        jnp.concatenate([qkv_grad.reshape(size, width, 3 * half_cols), proj_grad], axis=2)
    )
    normed_grad = pair_sum(dot("pztc,zdtc->pd", projected_grad, qkv_full))
    hidden_grad = middle_grad + normalize_back(normed_grad, unit_one, spread_one, gain_one)
    input_grad = take_back(hidden_grad.astype(jnp.bfloat16), place, size)

    def halves(values):
        zero = jnp.zeros_like(values)
        return jnp.where(first, jnp.stack([values, zero], 1), jnp.stack([zero, values], 1))

    small_sums = lax.psum(
        jnp.concatenate(
            [
                jnp.concatenate(
                    [
                        jnp.sum(normed_grad * unit_one, axis=0),
                        jnp.sum(normed_grad, axis=0),
                        jnp.sum(middle_grad, axis=0),
                        jnp.sum(normed_two_grad * unit_two, axis=0),
                        jnp.sum(normed_two_grad, axis=0),
                        jnp.sum(out_grad_wide, axis=0),
                    ]
                ),
                halves(qkv_bias_total.reshape(size, 3 * half_cols)).reshape(-1),
                halves(fc1_bias_total).reshape(-1),
            ]
        ),
        ("g", "c", "z"),
    )
    start = 6 * width
    vector_sums = lax.dynamic_slice_in_dim(
        small_sums[:start].reshape(6, width), (2 * group + core) * shard, shard, 1
    )
    middle_at = start + size * 3 * local_cols
    qkv_bias_sum = lax.dynamic_index_in_dim(
        small_sums[start:middle_at].reshape(size, 2, 3, half_cols), place, 0, keepdims=False
    )
    qkv_bias_sum = qkv_bias_sum.transpose(1, 0, 2).reshape(3, local_cols)
    fc1_bias_sum = lax.dynamic_index_in_dim(
        small_sums[middle_at:].reshape(size, units), place, 0, keepdims=False
    )

    def own_rows(part):
        mine = jnp.where(first, part[:shard], part[shard:])
        theirs = swap(jnp.where(first, part[shard:], part[:shard]))
        return jnp.where(first, jnp.stack([mine, theirs]), jnp.stack([theirs, mine])).astype(wide)

    fc2_sum = own_rows(fc2_part).transpose(0, 2, 1).reshape(units, shard)
    fc1_sum = own_rows(fc1_part).transpose(1, 0, 2).reshape(shard, units)
    attn_sum = own_rows(attn_part)
    qkv_sum = (
        attn_sum[:, :, : 3 * half_cols]
        .reshape(2, shard, 3, half_cols)
        .transpose(1, 2, 0, 3)
        .reshape(shard, 3, local_cols)
    )
    proj_sum = attn_sum[:, :, 3 * half_cols :].transpose(0, 2, 1).reshape(local_cols, shard)
    return (
        output,
        input_grad,
        vector_sums[0],
        vector_sums[1],
        qkv_sum,
        qkv_bias_sum,
        proj_sum,
        vector_sums[2],
        vector_sums[3],
        vector_sums[4],
        fc1_sum,
        fc1_bias_sum,
        fc2_sum,
        vector_sums[5],
    )


def solution(mesh):
    fsdp, tensor = mesh.shape["fsdp"], mesh.shape["tensor"]
    cut = Mesh(mesh.devices.reshape(fsdp // 2, 2, tensor), ("g", "c", "z"))
    f = ("g", "c")
    in_specs = (
        P(f, "z", None),
        P(f, None, None),
        P(f, None),
        P(f),
        P(f),
        P(f, None, "z"),
        P(None, "z"),
        P("z", f),
        P(f),
        P(f),
        P(f),
        P(f, "z"),
        P("z"),
        P("z", f),
        P(f),
        P(f, "z", None),
    )
    out_specs = (
        P(f, "z", None),
        P(f, "z", None),
        P(f),
        P(f),
        P(f, None, "z"),
        P(None, "z"),
        P("z", f),
        P(f),
        P(f),
        P(f),
        P(f, "z"),
        P("z"),
        P("z", f),
        P(f),
    )
    return jax.shard_map(
        on_device, mesh=cut, in_specs=in_specs, out_specs=out_specs, check_vma=False
    )
```

time: 1870 us -> 1570 us (0.84)
  waiting for transfers between devices: 1090 us -> 483 us
  local copies, waits for them, and re-layouts: 202 us -> 278 us
  matrix products: 361 us -> 435 us
  other arithmetic: 126 us -> 191 us
  blocking collectives: 68.2 us -> 128 us
  starting transfers between devices: 1.36 us -> 28.4 us
    reduce_scatter x12 -> x0, waiting for transfers between devices: 594 us -> none  [the longest x4 211 us: input_sum(): lax.psum_scatter(jnp.einsum(form, left, right, preferred_element_type=jnp...]
    all_gather x11 -> x3, waiting for transfers between devices: 488 us -> 0.04 us  [gather_all(): return lax.all_gather(block, ('z', 'g'), axis=0, tiled=True)]
    unnamed x25 -> x10, waiting for transfers between devices: 4.09 us -> 372 us
    all_gather x1, blocking collectives: 13.7 us -> 128 us  [on_device(): lax.all_gather(small, ('g', 'c', 'z'), axis=0)]
    ppermute x0 -> x21, waiting for transfers between devices: none -> 103 us  [the longest x4 51.2 us: take_back(): lax.ppermute(rows[step * count:(step + 1) * count], ('c', 'z'), [(target,...]
    dot_general x12 -> x6, matrix products: 52.3 us -> 103 us  [masked_scores(): jnp.einsum('qhd,khd->hqk', query_block, keys, preferred_element_type=jnp....]
    convert_element_type x6 -> x3, other arithmetic: 21.4 us -> 64.1 us  [one_block(): score_grad = (probs * (weight_grad - row_inner)).astype(jnp.bfloat16)]
    dot_general x24 -> x11, matrix products: 187 us -> 155 us  [dot(): return jnp.einsum(form, left, right, preferred_element_type=jnp.float32)]
  transfers between devices with their start and end apart: 24 -> 28, of which waited for: 20 -> 12; matrix products, arithmetic and copies ran while one was open for 29% -> 26% of each run, Pallas kernels for 0% -> 0%
where the time goes in v1:
time: 1570 us; the launch traced here: 1560 us
  waiting for transfers between devices  483 us (31%)
  matrix products  435 us (28%)
  local copies, waits for them, and re-layouts  278 us (18%)
  other arithmetic  191 us (12%)
  blocking collectives  128 us (8%)
  starting transfers between devices  28.4 us (2%)
  between operations  16 us (1%)
    unnamed x10, waiting for transfers between devices  372 us
    dot_general x11, matrix products, dot(): return jnp.einsum(form, left, right, preferred_element_type=jnp.float32)  155 us
    all_gather x1, blocking collectives, on_device(): lax.all_gather(small, ('g', 'c', 'z'), axis=0)  128 us
    dot_general x6, matrix products, masked_scores(): jnp.einsum('qhd,khd->hqk', query_block, keys, preferred_element_type=jnp....  103 us
    dynamic_update_slice x6, local copies, waits for them, and re-layouts, attend_back(): lax.scan(one_block, (zeros, zeros), (queries.reshape(count, block, heads,...  82 us
    convert_element_type x3, other arithmetic, one_block(): score_grad = (probs * (weight_grad - row_inner)).astype(jnp.bfloat16)  64.1 us
    ppermute x4, waiting for transfers between devices, take_back(): lax.ppermute(rows[step * count:(step + 1) * count], ('c', 'z'), [(target,...  51.2 us
    unnamed x155, local copies, waits for them, and re-layouts  45.2 us
  transfers between devices with their start and end apart: 28, of which 12 were waited for; matrix products, arithmetic and copies ran while one was open for 26% of the time, Pallas kernels for 0%

profile of v1, /device:TPU:11, one launch (start us, length us, event | category | flops | bytes accessed | tf_op | source)
XLA Modules:
  0.0 1559.8 jit_solution(6992755781566238386)
XLA Ops:
  30.0 127.5 %all-gather.1 = bf16[32,1,3200]{2,1,0:T(2,128)(2,1)S(1)} all-gather(bf16[1,1,3200]{2,1,0:T(2,128)(2,1)S(1)} %reshape.538), channel_id=2, replica_groups=mesh['g'=4,'c'=2,'z'=4] {'g','c','z'}, dimensions={0}, use_global_device_ids=true | all-gather | bytes 211200 | tf_op jit(solution)/shard_map/all_gather | solution.py:278
  188.8 13.8 bitcast_add_fusion.2
  254.8 108.6 %while.27 = (s32[]{:T(128)}, bf16[3,512,8,80]{1,3,2,0:T(8,128)(2,1)}, f32[3,8,512]{2,1,0:T(8,128)}, s32[3,512]{1,0:T(4,128)S(1)}, s32[1,1536]{1,0:T(1,128)S(1)},...) while((s32[]{:T(128)}, ...), condition=%wide.region_5.6_spmd, body=%wide.region_2.5_spmd.sunk | while | flops 2058416128 | bytes 90333336 | solution.py:74
  406.8 31.6 %collective-permute-done.10 = bf16[384,1280]{1,0:T(8,128)(2,1)S(1)} collective-permute-done((bf16[384,1280]{1,0:T(8,128)(2,1)S(1)}, bf16[384,1280]{1,0:T(8,128)(2,1)S(1)}, u32[]{:S(2)}, u32[]{:S(2)}) %collective-permute-start.10) | collective-permute-done | bytes 983072 | tf_op jit(solution)/shard_map/ppermute | solution.py:143
  449.9 20.3 %multiply_convert_fusion.2 = (bf16[1536,4,640]{2,0,1:T(8,128)(2,1)}, f32[1536,4,640]{2,0,1:T(8,128)}) fusion(f32[4,640]{1,0:T(4,128)S(1)} %fusion.85, bf16[4,1280,640]{2,1,0:T(8,128)(2,1)} %bitcast.324, bf16[768,1280]{1,0:T(8,128)(2,1)} %collective-permute-done.6, bf16[768,1280]{1,0:T(8,128)(2,1)} %add_convert_fusion.1), kind=kOutput, calls=%fused_computation.42 | convolution fusion | flops 10101719040 | bytes 34088960 | tf_op jit(solution)/shard_map/pd,zdf->pzf/dot_general | solution.py:197
  470.2 23.4 %convert_reduce_fusion = (f32[4,640]{1,0:T(4,128)}, bf16[1536,4,640]{2,0,1:T(8,128)(2,1)}) fusion(f32[1536,4,640]{2,0,1:T(8,128)} %get-tuple-element.464, f32[4,640]{1,0:T(4,128)S(1)} %fusion.85, bf16[4,1280,640]{2,1,0:T(8,128)(2,1)} %bitcast.326, bf16[768,1280]{1,0:T(8,128)(2,1)} %collective-permute-done.12, bf16[384,1280]{1,0:T(8,128)(2,1)} %copy-done.33, ...), kind=kOutput, calls=%fused_computation.40 | convolution fusion | flops 10129242112 | bytes 34099200 | tf_op jit(solution)/shard_map/pd,zdf->pzf/dot_general | solution.py:197
  493.6 15.1 convolution_bitcast_fusion
  510.4 16.2 %convolution_bitcast_fusion.1 = f32[1536,1280]{1,0:T(8,128)S(1)} fusion(bf16[1536,4,640]{2,0,1:T(8,128)(2,1)} %get-tuple-element.463, bf16[4,1280,640]{2,1,0:T(8,128)(2,1)} %bitcast.327), kind=kOutput, calls=%fused_computation.47 | convolution fusion | flops 10066329600 | bytes 22282240 | tf_op jit(solution)/shard_map/pzf,zdf->pd/dot_general | solution.py:197
  569.6 357.6 %while.28 = (s32[]{:T(128)}, f32[1536,8,80]{0,2,1:T(8,128)}, f32[1536,8,80]{0,2,1:T(8,128)}, f32[3,512,8,80]{1,0,3,2:T(4,128)}, bf16[3,512,8,80]{1,3,2,0:T(8,128...) while((s32[]{:T(128)}, f32[1536,8,80]{0,2,1:T(8,128)}, ...), condition=%wide.region_12.13_spmd.clone, body=%wide.region_10.12_spmd.clone.sunk | while | flops 5095813120 | bytes 226468016 | solution.py:113
  585.3 22.0 %multiply_reduce_fusion.7 = (f32[8,512]{1,0:T(8,128)S(1)}, f32[8,512,1536]{2,1,0:T(8,128)}) fusion(f32[8,512,1536]{2,1,0:T(8,128)} %fusion.163, f32[8,512]{1,0:T(8,128)S(1)} %dynamic-slice_bitcast_fusion.10, bf16[1536,8,80]{0,2,1:T(8,128)(2,1)S(1)} %get-tuple-element.660, bf16[3,512,8,80]{1,3,2,0:T(8,128)(2,1)} %get-tuple-element.657, ...), kind=kOutput, calls=%fused_computation.16.clone.1 | convolution fusion | flops 1038086144 | bytes 53772292 | tf_op jit(solution)/shard_map/while/body/eval_jaxpr/qhd,khd->hqk/dot_general | solution.py:53
  607.3 21.4 %multiply_convert_fusion.4 = bf16[8,512,1536]{2,1,0:T(8,128)(2,1)} fusion(f32[8,512,1536]{2,1,0:T(8,128)} %get-tuple-element.595, f32[8,512,1536]{2,1,0:T(8,128)} %fusion.163, f32[8,512]{1,0:T(8,128)S(1)} %get-tuple-element.596), kind=kLoop, calls=%fused_computation.15.clone.1 | loop fusion | flops 18874368 | bytes 62930944 | tf_op jit(solution)/shard_map/while/body/eval_jaxpr/convert_element_type | solution.py:99
  661.3 26.0 %dynamic_update_slice.20 = f32[3,512,8,80]{1,0,3,2:T(4,128)} dynamic-update-slice(f32[3,512,8,80]{1,0,3,2:T(4,128)} %get-tuple-element.643, f32[1,512,8,80]{1,0,3,2:T(1,128)S(1)} %copy.300, s32[]{:T(128)S(6)} %copy.318, s32[]{:T(128)} %constant.143.clone.1..sunk.1, s32[]{:T(128)} %constant.143.clone.1..sunk.1, s32[]{:T(128)} %constant.143.clone.1..sunk.1) | dynamic-update-slice | bytes 2621444 | tf_op jit(solution)/shard_map/while/body/jit(dynamic_update_index_in_dim)/dynamic_update_slice | solution.py:113
  702.8 22.1 %multiply_reduce_fusion.7 = (f32[8,512]{1,0:T(8,128)S(1)}, f32[8,512,1536]{2,1,0:T(8,128)}) fusion(f32[8,512,1536]{2,1,0:T(8,128)} %fusion.163, f32[8,512]{1,0:T(8,128)S(1)} %dynamic-slice_bitcast_fusion.10, bf16[1536,8,80]{0,2,1:T(8,128)(2,1)S(1)} %get-tuple-element.660, bf16[3,512,8,80]{1,3,2,0:T(8,128)(2,1)} %get-tuple-element.657, ...), kind=kOutput, calls=%fused_computation.16.clone.1 | convolution fusion | flops 1038086144 | bytes 53772292 | tf_op jit(solution)/shard_map/while/body/eval_jaxpr/qhd,khd->hqk/dot_general | solution.py:53
  724.9 21.4 %multiply_convert_fusion.4 = bf16[8,512,1536]{2,1,0:T(8,128)(2,1)} fusion(f32[8,512,1536]{2,1,0:T(8,128)} %get-tuple-element.595, f32[8,512,1536]{2,1,0:T(8,128)} %fusion.163, f32[8,512]{1,0:T(8,128)S(1)} %get-tuple-element.596), kind=kLoop, calls=%fused_computation.15.clone.1 | loop fusion | flops 18874368 | bytes 62930944 | tf_op jit(solution)/shard_map/while/body/eval_jaxpr/convert_element_type | solution.py:99
  781.1 26.0 %dynamic_update_slice.20 = f32[3,512,8,80]{1,0,3,2:T(4,128)} dynamic-update-slice(f32[3,512,8,80]{1,0,3,2:T(4,128)} %get-tuple-element.643, f32[1,512,8,80]{1,0,3,2:T(1,128)S(1)} %copy.300, s32[]{:T(128)S(6)} %copy.318, s32[]{:T(128)} %constant.143.clone.1..sunk.1, s32[]{:T(128)} %constant.143.clone.1..sunk.1, s32[]{:T(128)} %constant.143.clone.1..sunk.1) | dynamic-update-slice | bytes 2621444 | tf_op jit(solution)/shard_map/while/body/jit(dynamic_update_index_in_dim)/dynamic_update_slice | solution.py:113
  822.6 22.1 %multiply_reduce_fusion.7 = (f32[8,512]{1,0:T(8,128)S(1)}, f32[8,512,1536]{2,1,0:T(8,128)}) fusion(f32[8,512,1536]{2,1,0:T(8,128)} %fusion.163, f32[8,512]{1,0:T(8,128)S(1)} %dynamic-slice_bitcast_fusion.10, bf16[1536,8,80]{0,2,1:T(8,128)(2,1)S(1)} %get-tuple-element.660, bf16[3,512,8,80]{1,3,2,0:T(8,128)(2,1)} %get-tuple-element.657, ...), kind=kOutput, calls=%fused_computation.16.clone.1 | convolution fusion | flops 1038086144 | bytes 53772292 | tf_op jit(solution)/shard_map/while/body/eval_jaxpr/qhd,khd->hqk/dot_general | solution.py:53
  844.7 21.4 %multiply_convert_fusion.4 = bf16[8,512,1536]{2,1,0:T(8,128)(2,1)} fusion(f32[8,512,1536]{2,1,0:T(8,128)} %get-tuple-element.595, f32[8,512,1536]{2,1,0:T(8,128)} %fusion.163, f32[8,512]{1,0:T(8,128)S(1)} %get-tuple-element.596), kind=kLoop, calls=%fused_computation.15.clone.1 | loop fusion | flops 18874368 | bytes 62930944 | tf_op jit(solution)/shard_map/while/body/eval_jaxpr/convert_element_type | solution.py:99
  900.9 26.0 %dynamic_update_slice.20 = f32[3,512,8,80]{1,0,3,2:T(4,128)} dynamic-update-slice(f32[3,512,8,80]{1,0,3,2:T(4,128)} %get-tuple-element.643, f32[1,512,8,80]{1,0,3,2:T(1,128)S(1)} %copy.300, s32[]{:T(128)S(6)} %copy.318, s32[]{:T(128)} %constant.143.clone.1..sunk.1, s32[]{:T(128)} %constant.143.clone.1..sunk.1, s32[]{:T(128)} %constant.143.clone.1..sunk.1) | dynamic-update-slice | bytes 2621444 | tf_op jit(solution)/shard_map/while/body/jit(dynamic_update_index_in_dim)/dynamic_update_slice | solution.py:113
  980.3 15.9 %convert_bitcast_fusion.1 = bf16[4,1280,640]{1,2,0:T(8,128)(2,1)} fusion(bf16[1536,4,640]{2,0,1:T(8,128)(2,1)} %get-tuple-element.466, bf16[768,1280]{1,0:T(8,128)(2,1)} %collective-permute-done.6, bf16[768,1280]{1,0:T(8,128)(2,1)} %add_convert_fusion.1), kind=kOutput, calls=%fused_computation.52 | convolution fusion | flops 10077470720 | bytes 18350080 | tf_op jit(solution)/shard_map/pd,pzf->zdf/dot_general | solution.py:197
  1006.9 15.5 convert_bitcast_fusion
  1106.6 30.2 %collective-permute-done.8 = bf16[384,1280]{1,0:T(8,128)(2,1)} collective-permute-done((bf16[384,1280]{1,0:T(8,128)(2,1)}, bf16[384,1280]{1,0:T(8,128)(2,1)}, u32[]{:S(2)}, u32[]{:S(2)}) %collective-permute-start.8) | collective-permute-done | bytes 983072 | tf_op jit(solution)/shard_map/ppermute | solution.py:158
  1163.2 87.5 %reduce-scatter.12.cloned.1.call-done = bf16[320,640]{1,0:T(8,128)(2,1)} async-done(((bf16[5120,640]{1,0:T(8,128)(2,1)}), bf16[320,640]{1,0:T(8,128)(2,1)}) %reduce-scatter.12.cloned.1.call-update) | async-done | bytes 409616
  1253.9 142.0 %reduce-scatter.14.cloned.1.call-done = bf16[320,640]{1,0:T(8,128)(2,1)} async-done(((bf16[5120,640]{1,0:T(8,128)(2,1)}), bf16[320,640]{1,0:T(8,128)(2,1)}) %reduce-scatter.14.cloned.1.call-update) | async-done | bytes 409616
  1399.4 141.6 %reduce-scatter.10.cloned.1.call-done = bf16[320,640]{1,0:T(8,128)(2,1)} async-done(((bf16[5120,640]{1,0:T(8,128)(2,1)}), bf16[320,640]{1,0:T(8,128)(2,1)}) %reduce-scatter.10.cloned.1.call-update) | async-done | bytes 409616
  (430 shorter events, 654.0 us)
Async XLA Ops:
  7.2 168.6 %all-gather.6.cloned.1.call-start = ((), (), s32[]{:S(2)}) async-start(), calls=%async_computation.3 | async-start | bytes 6963200 | tf_op jit(solution)/shard_map/all_gather | solution.py:186
  23.1 426.7 %all-gather.8.cloned.1.call-start = ((), (), s32[]{:S(2)}) async-start(), calls=%async_computation.4 | async-start | bytes 6963200 | tf_op jit(solution)/shard_map/all_gather | solution.py:186
  23.9 446.3 %all-gather.10.cloned.1.call-start = ((), (), s32[]{:S(2)}) async-start(), calls=%async_computation.5 | async-start | bytes 6963200 | tf_op jit(solution)/shard_map/all_gather | solution.py:186
  25.0 136.4 %collective-permute-start = (bf16[384,1280]{1,0:T(8,128)(2,1)}, bf16[384,1280]{1,0:T(8,128)(2,1)S(1)}, u32[]{:S(2)}, u32[]{:S(2)}) collective-permute-start(bf16[384,1280]{1,0:T(8,128)(2,1)} %get-tuple-element.424), channel_id=1, source_target_pairs={{0,0},{1,1},{2,4},{3,5},{4,2},{5,3},{6,6},{7,7},{8,8},{9,9},{10,12... | collective-permute-start | bytes 2949128 | tf_op jit(solution)/shard_map/ppermute | solution.py:143
  29.5 131.9 %collective-permute-start.1 = (bf16[384,1280]{1,0:T(8,128)(2,1)S(1)}, bf16[384,1280]{1,0:T(8,128)(2,1)S(1)}, u32[]{:S(2)}, u32[]{:S(2)}) collective-permute-start(bf16[384,1280]{1,0:T(8,128)(2,1)S(1)} %get-tuple-element.425), channel_id=1, source_target_pairs={{0,1},{1,0},{2,5},{3,4},{4,3},{5,2},{6,7},{7,6},{8,9},{9,8},{10,13... | collective-permute-start | bytes 2949128 | tf_op jit(solution)/shard_map/ppermute | solution.py:143
  29.7 136.7 %collective-permute-start.2 = (s32[2,3,1536]{2,1,0:T(4,128)S(1)}, s32[2,3,1536]{2,1,0:T(4,128)S(1)}, u32[]{:S(2)}, u32[]{:S(2)}) collective-permute-start(s32[2,3,1536]{2,1,0:T(4,128)S(1)} %pad_add_fusion), channel_id=1, source_target_pairs={{0,4},{4,0},{1,5},{5,1},{2,6},{6,2},{3,7},{7,3},{8,12},{12,8},{9,1... | collective-permute-start | bytes 110600 | tf_op jit(solution)/shard_map/ppermute | solution.py:127
  164.5 24.3 %collective-permute-start.4 = (bf16[768,1280]{1,0:T(8,128)(2,1)}, bf16[768,1280]{1,0:T(8,128)(2,1)}, u32[]{:S(2)}, u32[]{:S(2)}) collective-permute-start(bf16[768,1280]{1,0:T(8,128)(2,1)} %fusion.44), channel_id=1, source_target_pairs={{0,4},{4,0},{1,5},{5,1},{2,6},{6,2},{3,7},{7,3},{8,12},{12,8},{9,1... | collective-permute-start | bytes 5898248 | tf_op jit(solution)/shard_map/ppermute | solution.py:127
  175.5 926.8 %all-reduce.6.cloned.1.call-start = ((), (), s32[]{:S(2)}) async-start(), calls=%async_computation.6 | async-start | bytes 139264 | tf_op jit(solution)/shard_map/psum | solution.py:367
  398.5 51.3 %collective-permute-start.6 = (bf16[768,1280]{1,0:T(8,128)(2,1)}, bf16[768,1280]{1,0:T(8,128)(2,1)}, u32[]{:S(2)}, u32[]{:S(2)}) collective-permute-start(bf16[768,1280]{1,0:T(8,128)(2,1)} %add_convert_fusion.1), channel_id=1, source_target_pairs={{0,4},{4,0},{1,5},{5,1},{2,6},{6,2},{3,7},{7,3},{8,12},{12,8},{9,1... | collective-permute-start | bytes 5898248 | tf_op jit(solution)/shard_map/ppermute | solution.py:127
  399.5 38.8 %collective-permute-start.10 = (bf16[384,1280]{1,0:T(8,128)(2,1)S(1)}, bf16[384,1280]{1,0:T(8,128)(2,1)S(1)}, u32[]{:S(2)}, u32[]{:S(2)}) collective-permute-start(bf16[384,1280]{1,0:T(8,128)(2,1)S(1)} %get-tuple-element.419), channel_id=1, source_target_pairs={{0,0},{1,1},{2,4},{3,5},{4,2},{5,3},{6,6},{7,7},{8,8},{9,9},{10,12... | collective-permute-start | bytes 2949128 | tf_op jit(solution)/shard_map/ppermute | solution.py:143
  406.6 42.3 %collective-permute-start.11 = (bf16[384,1280]{1,0:T(8,128)(2,1)S(1)}, bf16[384,1280]{1,0:T(8,128)(2,1)S(1)}, u32[]{:S(2)}, u32[]{:S(2)}) collective-permute-start(bf16[384,1280]{1,0:T(8,128)(2,1)S(1)} %get-tuple-element.418), channel_id=1, source_target_pairs={{0,1},{1,0},{2,5},{3,4},{4,3},{5,2},{6,7},{7,6},{8,9},{9,8},{10,13... | collective-permute-start | bytes 2949128 | tf_op jit(solution)/shard_map/ppermute | solution.py:143
  449.9 20.3 %collective-permute-start.12 = (bf16[768,1280]{1,0:T(8,128)(2,1)S(1)}, bf16[768,1280]{1,0:T(8,128)(2,1)}, u32[]{:S(2)}, u32[]{:S(2)}) collective-permute-start(bf16[768,1280]{1,0:T(8,128)(2,1)S(1)} %constant_dynamic-update-slice_fusion), channel_id=1, source_target_pairs={{0,4},{4,0},{1,5},{5,1},{2,6},{6,2},{3,7},{7,3},{8,12},{12,8},{9,1... | collective-permute-start | bytes 5898248 | tf_op jit(solution)/shard_map/ppermute | solution.py:127
  510.4 20.0 %collective-permute-start.13 = (bf16[768,1280]{1,0:T(8,128)(2,1)}, bf16[768,1280]{1,0:T(8,128)(2,1)S(1)}, u32[]{:S(2)}, u32[]{:S(2)}) collective-permute-start(bf16[768,1280]{1,0:T(8,128)(2,1)} %slice.427), channel_id=1, source_target_pairs={{0,4},{4,0},{1,5},{5,1},{2,6},{6,2},{3,7},{7,3},{8,12},{12,8},{9,1... | collective-permute-start | bytes 5898248 | tf_op jit(solution)/shard_map/ppermute | solution.py:127
  530.3 5.2 collective-permute-start.7
  546.3 5.9 collective-permute-start.14
  980.2 270.5 %reduce-scatter.12.cloned.1.call-start = ((), (), s32[]{:S(2)}) async-start(), calls=%async_computation.8 | async-start | bytes 6963200
  1005.7 390.2 %reduce-scatter.14.cloned.1.call-start = ((), (), s32[]{:S(2)}) async-start(), calls=%async_computation.9 | async-start | bytes 6963200
  1032.0 509.0 %reduce-scatter.10.cloned.1.call-start = ((), (), s32[]{:S(2)}) async-start(), calls=%async_computation.7 | async-start | bytes 6963200
  1078.0 28.5 %collective-permute-start.9 = (bf16[384,1280]{1,0:T(8,128)(2,1)}, bf16[384,1280]{1,0:T(8,128)(2,1)S(1)}, u32[]{:S(2)}, u32[]{:S(2)}) collective-permute-start(bf16[384,1280]{1,0:T(8,128)(2,1)} %get-tuple-element.422), channel_id=1, source_target_pairs={{1,0},{0,1},{5,2},{4,3},{3,4},{2,5},{7,6},{6,7},{9,8},{8,9},{13,10... | collective-permute-start | bytes 2949128 | tf_op jit(solution)/shard_map/ppermute | solution.py:158
  1080.5 56.2 %collective-permute-start.8 = (bf16[384,1280]{1,0:T(8,128)(2,1)}, bf16[384,1280]{1,0:T(8,128)(2,1)}, u32[]{:S(2)}, u32[]{:S(2)}) collective-permute-start(bf16[384,1280]{1,0:T(8,128)(2,1)} %get-tuple-element.423), channel_id=1, source_target_pairs={{0,0},{1,1},{4,2},{5,3},{2,4},{3,5},{6,6},{7,7},{8,8},{9,9},{12,10... | collective-permute-start | bytes 2949128 | tf_op jit(solution)/shard_map/ppermute | solution.py:158
  1088.4 58.8 %collective-permute-start.17 = (bf16[384,1280]{1,0:T(8,128)(2,1)}, bf16[384,1280]{1,0:T(8,128)(2,1)S(1)}, u32[]{:S(2)}, u32[]{:S(2)}) collective-permute-start(bf16[384,1280]{1,0:T(8,128)(2,1)} %get-tuple-element.416), channel_id=1, source_target_pairs={{1,0},{0,1},{5,2},{4,3},{3,4},{2,5},{7,6},{6,7},{9,8},{8,9},{13,10... | collective-permute-start | bytes 2949128 | tf_op jit(solution)/shard_map/ppermute | solution.py:158
  1088.4 69.3 %collective-permute-start.16 = (bf16[384,1280]{1,0:T(8,128)(2,1)}, bf16[384,1280]{1,0:T(8,128)(2,1)S(1)}, u32[]{:S(2)}, u32[]{:S(2)}) collective-permute-start(bf16[384,1280]{1,0:T(8,128)(2,1)} %get-tuple-element.417), channel_id=1, source_target_pairs={{0,0},{1,1},{4,2},{5,3},{2,4},{3,5},{6,6},{7,7},{8,8},{9,9},{12,10... | collective-permute-start | bytes 2949128 | tf_op jit(solution)/shard_map/ppermute | solution.py:158
  1252.2 291.9 %collective-permute-start.19 = (bf16[160,640]{0,1:T(8,128)(2,1)S(1)}, bf16[160,640]{0,1:T(8,128)(2,1)S(1)}, u32[]{:S(2)}, u32[]{:S(2)}) collective-permute-start(bf16[160,640]{0,1:T(8,128)(2,1)S(1)} %get-tuple-element.434), channel_id=1, source_target_pairs={{0,4},{4,0},{1,5},{5,1},{2,6},{6,2},{3,7},{7,3},{8,12},{12,8},{9,1... | collective-permute-start | bytes 614408 | tf_op jit(solution)/shard_map/ppermute | solution.py:127
  1398.4 147.2 %collective-permute-start.20 = (bf16[160,640]{0,1:T(8,128)(2,1)}, bf16[160,640]{0,1:T(8,128)(2,1)S(1)}, u32[]{:S(2)}, u32[]{:S(2)}) collective-permute-start(bf16[160,640]{0,1:T(8,128)(2,1)} %get-tuple-element.432), channel_id=1, source_target_pairs={{0,4},{4,0},{1,5},{5,1},{2,6},{6,2},{3,7},{7,3},{8,12},{12,8},{9,1... | collective-permute-start | bytes 614408 | tf_op jit(solution)/shard_map/ppermute | solution.py:127
  (75 other events, 560.3 us)
Sparse Core Ops, SparseCore 0:
  23.3 118.2 all-gather.5
  144.2 95.3 all-gather.7
  242.3 94.3 all-gather.9
  980.4 121.8 all-reduce.5
  1104.4 146.3 reduce-scatter.11
  1252.9 142.9 reduce-scatter.13
  1398.2 142.7 reduce-scatter.9

commit v2 on v1

v2 whole, which is shorter than its diff:
```python
import jax
import jax.numpy as jnp
import numpy as np
from jax import lax
from jax.experimental import pallas as pl
from jax.experimental.pallas import tpu as pltpu
from jax.sharding import Mesh, PartitionSpec as P

HEAD_DIM = 80

epsilon = 1e-06


LANES = 128
HALF = LANES // 2
MID = HEAD_DIM // 2
FREE = HALF - MID
FAR = -1.0e9
LOG2E = 1.4426950408889634
SCALE = HEAD_DIM ** (-0.5)
BLOCK = 256


def angle_tables(place):
    quarter = HEAD_DIM // 4
    freqs = 10000.0 ** (-(4.0 * jnp.arange(quarter, dtype=jnp.float32)) / HEAD_DIM)
    row_angles = place[0].astype(jnp.float32)[:, None] * freqs[None, :]
    col_angles = place[1].astype(jnp.float32)[:, None] * freqs[None, :]
    half = jnp.concatenate([row_angles, col_angles], axis=1)
    cosine = jnp.pad(jnp.cos(half), ((0, 0), (0, FREE)))
    sine = jnp.pad(jnp.sin(half), ((0, 0), (0, FREE)))
    return (
        jnp.concatenate([cosine, cosine], axis=1),
        jnp.concatenate([-sine, sine], axis=1),
    )


def label_tables(labels):
    lane = jnp.arange(LANES)[None, :] - MID
    free = (lane >= 0) & (lane < FREE)
    same = lane == labels[:, None]
    return (
        jnp.where(free & same, 1.0, 0.0).astype(jnp.bfloat16),
        jnp.where(free & ~same, FAR, 0.0).astype(jnp.bfloat16),
    )


def lane_of(index):
    return index if index < MID else index - MID + HALF


def pad_tables(cols):
    heads = cols // HEAD_DIM
    first = np.zeros((4 * cols, heads * 3 * LANES), np.float32)
    second = np.zeros((4 * cols, heads * LANES), np.float32)
    for head in range(heads):
        for index in range(HEAD_DIM):
            for kind in range(3):
                source = kind * cols + head * HEAD_DIM + index
                first[source, (head * 3 + kind) * LANES + lane_of(index)] = 1.0
            source = 3 * cols + head * HEAD_DIM + index
            second[source, head * LANES + lane_of(index)] = 1.0
    return jnp.asarray(first, jnp.bfloat16), jnp.asarray(second, jnp.bfloat16)


def product(left, right, dims):
    return lax.dot_general(left, right, (dims, ((), ())), preferred_element_type=jnp.float32)


def attend_kernel(
    x_ref, w_ref, b_ref, cos_ref, sin_ref, qa_ref, ka_ref, qkv_ref, o_ref, total_ref, vt_ref
):
    total = x_ref.shape[0]
    weight = w_ref[0]
    shift = b_ref[0]
    ones = jnp.where(lax.broadcasted_iota(jnp.int32, (BLOCK, LANES), 1) == LANES - 1, 1.0, 0.0)

    def project(index, carry):
        at = pl.ds(pl.multiple_of(index * BLOCK, BLOCK), BLOCK)
        made = product(x_ref[at, :], weight, ((1,), (0,))) + shift
        cosine, sine = cos_ref[at, :], sin_ref[at, :]
        query, key = made[:, :LANES], made[:, LANES : 2 * LANES]
        value = made[:, 2 * LANES :] + ones
        query = query * cosine + pltpu.roll(query, HALF, 1) * sine
        key = key * cosine + pltpu.roll(key, HALF, 1) * sine
        qkv_ref[at, :LANES] = (query * (SCALE * LOG2E)).astype(jnp.bfloat16) + qa_ref[at, :]
        qkv_ref[at, LANES : 2 * LANES] = key.astype(jnp.bfloat16) + ka_ref[at, :]
        qkv_ref[at, 2 * LANES :] = value.astype(jnp.bfloat16)
        vt_ref[:, at] = value.T.astype(jnp.bfloat16)
        return carry

    lax.fori_loop(0, total // BLOCK, project, 0)

    def mix(index, carry):
        at = pl.ds(pl.multiple_of(index * BLOCK, BLOCK), BLOCK)
        scores = product(qkv_ref[:, LANES : 2 * LANES], qkv_ref[at, :LANES], ((1,), (1,)))
        largest = jnp.max(scores, axis=0, keepdims=True)
        probs = jnp.exp2(scores - largest).astype(jnp.bfloat16)
        mixed = product(vt_ref[...], probs, ((1,), (0,)))
        amount = mixed[LANES - 1 :, :]
        o_ref[at, :] = (mixed * (1.0 / amount)).T.astype(jnp.bfloat16)
        total_ref[0, :, at] = largest + jnp.log2(amount)
        return carry

    lax.fori_loop(0, total // BLOCK, mix, 0)


def attend(normed, weight, shift, cosine, sine, query_mark, key_mark):
    total, width = normed.shape
    size = weight.shape[0]
    pairs = weight.shape[2] // (3 * LANES)
    heads = size * pairs
    whole = lambda cols: pl.BlockSpec((total, cols), lambda h: (0, 0), pipeline_mode=pl.Buffered(1))
    return pl.pallas_call(
        attend_kernel,
        grid=(heads,),
        in_specs=[
            whole(width),
            pl.BlockSpec((1, width, 3 * LANES), lambda h: (h // pairs, 0, h % pairs)),
            pl.BlockSpec((1, 1, 3 * LANES), lambda h: (h, 0, 0)),
            whole(LANES),
            whole(LANES),
            whole(LANES),
            whole(LANES),
        ],
        out_specs=[
            pl.BlockSpec((total, 3 * LANES), lambda h: (0, h)),
            pl.BlockSpec((total, LANES), lambda h: (0, h)),
            pl.BlockSpec((1, 1, total), lambda h: (h, 0, 0)),
        ],
        out_shape=[
            jax.ShapeDtypeStruct((total, heads * 3 * LANES), jnp.bfloat16),
            jax.ShapeDtypeStruct((total, heads * LANES), jnp.bfloat16),
            jax.ShapeDtypeStruct((heads, 1, total), jnp.float32),
        ],
        scratch_shapes=[pltpu.VMEM((LANES, total), jnp.bfloat16)],
        compiler_params=pltpu.CompilerParams(vmem_limit_bytes=40 * 2**20),
        cost_estimate=pl.CostEstimate(
            flops=2 * heads * total * LANES * (3 * width + 4 * total),
            bytes_accessed=8 * total * heads * LANES + 2 * total * width,
            transcendentals=heads * total * total,
        ),
    )(normed, weight, shift, cosine, sine, query_mark, key_mark)


def back_kernel(
    qkv_ref, o_ref, grad_ref, total_ref, cos_ref, sin_ref, out_ref, bias_ref, kt_ref, dk_ref, dv_ref
):
    total = qkv_ref.shape[0]
    dk_ref[...] = jnp.zeros_like(dk_ref)
    dv_ref[...] = jnp.zeros_like(dv_ref)
    kt_ref[...] = qkv_ref[:, LANES : 2 * LANES].T

    def turn_back(grads, at):
        return (grads * cos_ref[at, :] + pltpu.roll(grads * sin_ref[at, :], HALF, 1)).astype(
            jnp.bfloat16
        )

    def step(index, carry):
        at = pl.ds(pl.multiple_of(index * BLOCK, BLOCK), BLOCK)
        query = qkv_ref[at, :LANES]
        grad = grad_ref[at, :]
        inner = grad.astype(jnp.float32) * o_ref[at, :].astype(jnp.float32)
        row = jnp.sum(inner.T, axis=0, keepdims=True)
        scores = product(qkv_ref[:, LANES : 2 * LANES], query, ((1,), (1,)))
        probs = jnp.exp2(scores - total_ref[0, :, at])
        weight_grad = product(qkv_ref[:, 2 * LANES :], grad, ((1,), (1,)))
        score_grad = (probs * (weight_grad - row)).astype(jnp.bfloat16)
        dv_ref[...] += product(probs.astype(jnp.bfloat16), grad, ((1,), (0,)))
        dk_ref[...] += product(score_grad, query, ((1,), (0,)))
        turned = product(kt_ref[...], score_grad, ((1,), (0,))).T * SCALE
        made = turn_back(turned, at)
        out_ref[at, :LANES] = made
        return carry + jnp.sum(made.astype(jnp.float32), axis=0, keepdims=True)

    zero = jnp.zeros((1, LANES), jnp.float32)
    query_bias = lax.fori_loop(0, total // BLOCK, step, zero)

    def finish(index, carry):
        at = pl.ds(pl.multiple_of(index * BLOCK, BLOCK), BLOCK)
        key = turn_back(dk_ref[at, :] * (1.0 / LOG2E), at)
        value = dv_ref[at, :].astype(jnp.bfloat16)
        out_ref[at, LANES : 2 * LANES] = key
        out_ref[at, 2 * LANES :] = value
        return (
            carry[0] + jnp.sum(key.astype(jnp.float32), axis=0, keepdims=True),
            carry[1] + jnp.sum(value.astype(jnp.float32), axis=0, keepdims=True),
        )

    key_bias, value_bias = lax.fori_loop(0, total // BLOCK, finish, (zero, zero))
    bias_ref[0] = jnp.concatenate([query_bias, key_bias, value_bias], axis=1)


def attend_back(qkv, mixed, mixed_grad, log_total, cosine, sine):
    total = qkv.shape[0]
    heads = mixed.shape[1] // LANES
    whole = lambda cols: pl.BlockSpec((total, cols), lambda h: (0, 0), pipeline_mode=pl.Buffered(1))
    wide = pl.BlockSpec((total, 3 * LANES), lambda h: (0, h))
    thin = pl.BlockSpec((total, LANES), lambda h: (0, h))
    return pl.pallas_call(
        back_kernel,
        grid=(heads,),
        in_specs=[
            wide,
            thin,
            thin,
            pl.BlockSpec((1, 1, total), lambda h: (h, 0, 0)),
            whole(LANES),
            whole(LANES),
        ],
        out_specs=[wide, pl.BlockSpec((1, 1, 3 * LANES), lambda h: (h, 0, 0))],
        out_shape=[
            jax.ShapeDtypeStruct((total, heads * 3 * LANES), jnp.bfloat16),
            jax.ShapeDtypeStruct((heads, 1, 3 * LANES), jnp.float32),
        ],
        scratch_shapes=[
            pltpu.VMEM((LANES, total), jnp.bfloat16),
            pltpu.VMEM((total, LANES), jnp.float32),
            pltpu.VMEM((total, LANES), jnp.float32),
        ],
        compiler_params=pltpu.CompilerParams(vmem_limit_bytes=40 * 2**20),
        cost_estimate=pl.CostEstimate(
            flops=2 * heads * total * total * LANES * 5,
            bytes_accessed=2 * total * heads * LANES * 8,
            transcendentals=heads * total * total,
        ),
    )(qkv, mixed, mixed_grad, log_total, cosine, sine)


def normalize(values, gain, shift):
    center = values - jnp.mean(values, axis=-1, keepdims=True)
    spread = lax.rsqrt(jnp.mean(center * center, axis=-1, keepdims=True) + epsilon)
    unit = center * spread
    return (unit * gain + shift, unit, spread)


def normalize_back(grads, unit, spread, gain):
    scaled = grads * gain
    inner = (
        scaled
        - jnp.mean(scaled, axis=-1, keepdims=True)
        - unit * jnp.mean(scaled * unit, axis=-1, keepdims=True)
    )
    return inner * spread


def swap(values):
    return lax.ppermute(values, "c", [(0, 1), (1, 0)])


def travel(step, size):
    runs = size // 2
    pairs = []
    for core in range(2):
        for place in range(size):
            half, part = divmod(place, runs)
            pairs.append((core * size + place, half * size + runs * core + (part + step) % runs))
    return pairs


def bring(packs, place, size):
    runs = size // 2
    parts = [
        lax.ppermute(
            lax.dynamic_index_in_dim(packs, lax.rem(place + step, runs), 0, keepdims=False),
            ("c", "z"),
            travel(step, size),
        )
        for step in range(runs)
    ]
    return jnp.concatenate(parts, axis=0)


def take_back(rows, place, size):
    runs = size // 2
    count = rows.shape[0] // runs
    parts = jnp.stack(
        [
            lax.ppermute(
                rows[step * count : (step + 1) * count],
                ("c", "z"),
                [(target, source) for source, target in travel(step, size)],
            )
            for step in range(runs)
        ]
    )
    return jnp.stack(
        [
            lax.dynamic_index_in_dim(
                parts, lax.rem(index + size - place, runs), 0, keepdims=False
            )
            for index in range(runs)
        ]
    )


def pair_sum(partial):
    count = partial.shape[0] // 2
    return partial[:count] + swap(partial[count:].astype(jnp.bfloat16)).astype(jnp.float32)


def share(own):
    return jnp.concatenate([own, swap(own)], axis=0)


def gather_all(block):
    return lax.all_gather(block, ("z", "g"), axis=0, tiled=True)


def flat(blocks):
    return blocks.reshape(-1, blocks.shape[-1])


def scatter_all(total):
    return lax.psum_scatter(total, ("z", "g"), scatter_dimension=0, tiled=True)


def sum_all(values):
    for axis in ("c", "g", "z"):
        size, apart = lax.axis_size(axis), 1
        assert size & (size - 1) == 0
        while apart < size:
            values = values + lax.ppermute(values, axis, [(i, i ^ apart) for i in range(size)])
            apart *= 2
    return values


def dot(form, left, right):
    return jnp.einsum(form, left, right, preferred_element_type=jnp.float32)


def on_device(
    hidden,
    positions,
    segments,
    ln1_gain,
    ln1_bias,
    qkv_weight,
    qkv_bias,
    proj_weight,
    proj_bias,
    ln2_gain,
    ln2_bias,
    fc1_weight,
    fc1_bias,
    fc2_weight,
    fc2_bias,
    cotangent,
):
    wide = jnp.float32
    size = lax.axis_size("z")
    core = lax.axis_index("c")
    place = lax.axis_index("z")
    group = lax.axis_index("g")
    batches, rows, width = hidden.shape
    runs = size // 2
    assert batches == runs
    shard = qkv_weight.shape[0]
    local_cols = qkv_weight.shape[2]
    half_cols = local_cols // 2
    units = fc1_weight.shape[1]
    half_units = units // 2
    pairs = half_cols // HEAD_DIM
    heads = size * pairs
    first = core == 0

    first_part = jnp.concatenate(
        [
            qkv_weight.reshape(shard, 3, 2, half_cols).transpose(0, 2, 1, 3).reshape(
                shard, 2, 3 * half_cols
            ),
            proj_weight.T.reshape(shard, 2, half_cols),
        ],
        axis=2,
    )
    packed = jnp.concatenate(
        [
            first_part,
            fc1_weight.reshape(shard, 2, half_units),
            fc2_weight.T.reshape(shard, 2, half_units),
        ],
        axis=2,
    )
    keep = jnp.where(first, packed[:, 0], packed[:, 1])
    other = swap(jnp.where(first, packed[:, 1], packed[:, 0]))
    block = jnp.where(
        first, jnp.concatenate([keep, other], axis=0), jnp.concatenate([other, keep], axis=0)
    )
    attn_cols = 4 * half_cols
    small = jnp.concatenate(
        [
            ln1_gain,
            ln1_bias,
            proj_bias,
            ln2_gain,
            ln2_bias,
            fc2_bias,
            qkv_bias.reshape(-1),
            fc1_bias,
        ]
    )
    length = small.shape[0]
    lines = -(-length // attn_cols)
    small = jnp.pad(small, (0, lines * attn_cols - length)).reshape(lines, attn_cols)
    small_other = swap(small)
    extra = -(-(2 * lines) // 16) * 16 - 2 * lines
    sent = jnp.concatenate(
        [
            block[:, :attn_cols],
            jnp.where(first, small, small_other),
            jnp.where(first, small_other, small),
            jnp.zeros((extra, attn_cols), small.dtype),
        ],
        axis=0,
    )
    arrived = gather_all(sent).reshape(size, -1, sent.shape[0], attn_cols)
    attn_full = arrived[:, :, : 2 * shard].reshape(size, width, attn_cols)
    small_full = arrived[:, :, 2 * shard : 2 * shard + 2 * lines].reshape(
        size, -1, lines * attn_cols
    )[:, :, :length]
    fc1_full = gather_all(block[:, attn_cols : attn_cols + half_units]).reshape(
        size, width, half_units
    )
    fc2_full = gather_all(block[:, attn_cols + half_units :]).reshape(size, width, half_units)
    qkv_table, proj_table = pad_tables(half_cols)
    qkv_full = dot("zdc,ck->zdk", attn_full, qkv_table).astype(jnp.bfloat16)
    proj_full = (
        dot("zdc,ck->dzk", attn_full, proj_table).astype(jnp.bfloat16).reshape(width, -1)
    )
    vectors = (
        small_full[0, :, : 6 * shard].reshape(-1, 6, shard).transpose(1, 0, 2).reshape(6, width)
    ).astype(wide)
    gain_one, shift_one, proj_shift, gain_two, shift_two, fc2_shift = (
        vectors[index] for index in range(6)
    )
    tail = small_full[:, 0, 6 * shard :].astype(wide)
    qkv_shifts = tail[:, : 3 * local_cols].reshape(size, 3, 2, half_cols)
    qkv_shift = jnp.where(first, qkv_shifts[:, :, 0], qkv_shifts[:, :, 1])
    qkv_shift = qkv_shift.reshape(size, 3, pairs, 2, MID).transpose(0, 2, 1, 3, 4)
    qkv_shift = jnp.pad(qkv_shift, ((0, 0),) * 4 + ((0, FREE),)).reshape(heads, 1, 3 * LANES)
    fc1_shifts = tail[:, 3 * local_cols :].reshape(size, 2, half_units)
    fc1_shift = jnp.where(first, fc1_shifts[:, 0], fc1_shifts[:, 1])

    marks = jnp.concatenate([positions, segments[:, None, :]], axis=1)
    marks_other = swap(marks)
    own_pack = place // runs == core
    batch = lax.rem(place, runs)
    marks = lax.dynamic_index_in_dim(
        jnp.where(own_pack, marks, marks_other), batch, 0, keepdims=False
    ).reshape(3, size, rows)
    order = [
        runs * (core if side == 0 else 1 - core) + lax.rem(batch + runs - step, runs)
        for side in range(2)
        for step in range(runs)
    ]
    marks = jnp.concatenate(
        [lax.dynamic_index_in_dim(marks, index, 1, keepdims=False) for index in order], axis=1
    )
    cosine, sine = angle_tables(marks[:2])
    query_mark, key_mark = label_tables(marks[2])

    start_values = bring(hidden, place, size).astype(wide)
    normed, unit_one, spread_one = normalize(start_values, gain_one, shift_one)
    normed_full = share(normed.astype(jnp.bfloat16))
    normed_full, cotangent = lax.optimization_barrier((normed_full, cotangent))
    out_grad = bring(cotangent, place, size)
    qkv, mixed, log_total = attend(
        normed_full, qkv_full, qkv_shift, cosine, sine, query_mark, key_mark
    )
    middle = start_values + pair_sum(dot("pk,dk->pd", mixed, proj_full)) + proj_shift
    normed_two, unit_two, spread_two = normalize(middle, gain_two, shift_two)
    ffn_input = share(normed_two.astype(jnp.bfloat16))
    before = dot("pd,zdf->pzf", ffn_input, fc1_full) + fc1_shift
    sigma = jax.nn.sigmoid(1.702 * before)
    after = (before * sigma).astype(jnp.bfloat16)
    outcome = middle + pair_sum(dot("pzf,zdf->pd", after, fc2_full)) + fc2_shift
    output = take_back(outcome.astype(jnp.bfloat16), place, size)

    out_grad_wide = out_grad.astype(wide)
    out_grad_full = share(out_grad)
    fc2_grad = flat(dot("pd,pzf->zdf", out_grad_full, after).astype(jnp.bfloat16))
    fc2_grad, out_grad_full = lax.optimization_barrier((fc2_grad, out_grad_full))
    fc2_part = scatter_all(fc2_grad)
    after_grad = dot("pd,zdf->pzf", out_grad_full, fc2_full)
    before_grad = (after_grad * (sigma + 1.702 * before * sigma * (1.0 - sigma))).astype(
        jnp.bfloat16
    )
    fc1_grad = flat(dot("pd,pzf->zdf", ffn_input, before_grad).astype(jnp.bfloat16))
    fc1_bias_total = jnp.sum(before_grad.astype(wide), axis=0)
    normed_two_grad = pair_sum(dot("pzf,zdf->pd", before_grad, fc1_full))
    middle_grad = out_grad_wide + normalize_back(normed_two_grad, unit_two, spread_two, gain_two)
    branch_grad_full = share(middle_grad.astype(jnp.bfloat16))
    branch_grad_full, fc1_grad = lax.optimization_barrier((branch_grad_full, fc1_grad))
    fc1_part = scatter_all(fc1_grad)
    proj_grad = dot("pd,pk->dk", branch_grad_full, mixed).astype(jnp.bfloat16)
    mixed_grad = dot("pd,dk->pk", branch_grad_full, proj_full).astype(jnp.bfloat16)
    projected_grad, qkv_bias_total = attend_back(
        qkv, mixed, mixed_grad, log_total, cosine, sine
    )
    split_grad = projected_grad.reshape(projected_grad.shape[0], size, -1)
    qkv_grad = dot("pd,pzk->zdk", normed_full, split_grad).astype(jnp.bfloat16)
    attn_part = scatter_all(
        flat(
            (
                dot("zdk,ck->zdc", qkv_grad, qkv_table)
                + dot("dzk,ck->zdc", proj_grad.reshape(width, size, -1), proj_table)
            ).astype(jnp.bfloat16)
        )
    )
    normed_grad = pair_sum(dot("pzk,zdk->pd", split_grad, qkv_full))
    hidden_grad = middle_grad + normalize_back(normed_grad, unit_one, spread_one, gain_one)
    input_grad = take_back(hidden_grad.astype(jnp.bfloat16), place, size)

    qkv_bias_total = qkv_bias_total.reshape(size, pairs, 3, 2, HALF)[..., :MID]
    qkv_bias_total = qkv_bias_total.transpose(0, 2, 1, 3, 4).reshape(size, 3 * half_cols)

    def halves(values):
        zero = jnp.zeros_like(values)
        return jnp.where(first, jnp.stack([values, zero], 1), jnp.stack([zero, values], 1))

    small_sums = sum_all(
        jnp.concatenate(
            [
                jnp.concatenate(
                    [
                        jnp.sum(normed_grad * unit_one, axis=0),
                        jnp.sum(normed_grad, axis=0),
                        jnp.sum(middle_grad, axis=0),
                        jnp.sum(normed_two_grad * unit_two, axis=0),
                        jnp.sum(normed_two_grad, axis=0),
                        jnp.sum(out_grad_wide, axis=0),
                    ]
                ),
                halves(qkv_bias_total).reshape(-1),
                halves(fc1_bias_total).reshape(-1),
            ]
        )
    )
    start = 6 * width
    vector_sums = lax.dynamic_slice_in_dim(
        small_sums[:start].reshape(6, width), (2 * group + core) * shard, shard, 1
    )
    middle_at = start + size * 3 * local_cols
    qkv_bias_sum = lax.dynamic_index_in_dim(
        small_sums[start:middle_at].reshape(size, 2, 3, half_cols), place, 0, keepdims=False
    )
    qkv_bias_sum = qkv_bias_sum.transpose(1, 0, 2).reshape(3, local_cols)
    fc1_bias_sum = lax.dynamic_index_in_dim(
        small_sums[middle_at:].reshape(size, units), place, 0, keepdims=False
    )

    def own_rows(part):
        mine = jnp.where(first, part[:shard], part[shard:])
        theirs = swap(jnp.where(first, part[shard:], part[:shard]))
        return jnp.where(first, jnp.stack([mine, theirs]), jnp.stack([theirs, mine])).astype(wide)

    fc2_sum = own_rows(fc2_part).transpose(0, 2, 1).reshape(units, shard)
    fc1_sum = own_rows(fc1_part).transpose(1, 0, 2).reshape(shard, units)
    attn_sum = own_rows(attn_part)
    qkv_sum = (
        attn_sum[:, :, : 3 * half_cols]
        .reshape(2, shard, 3, half_cols)
        .transpose(1, 2, 0, 3)
        .reshape(shard, 3, local_cols)
    )
    proj_sum = attn_sum[:, :, 3 * half_cols :].transpose(0, 2, 1).reshape(local_cols, shard)
    return (
        output,
        input_grad,
        vector_sums[0],
        vector_sums[1],
        qkv_sum,
        qkv_bias_sum,
        proj_sum,
        vector_sums[2],
        vector_sums[3],
        vector_sums[4],
        fc1_sum,
        fc1_bias_sum,
        fc2_sum,
        vector_sums[5],
    )


def solution(mesh):
    fsdp, tensor = mesh.shape["fsdp"], mesh.shape["tensor"]
    cut = Mesh(mesh.devices.reshape(fsdp // 2, 2, tensor), ("g", "c", "z"))
    f = ("g", "c")
    in_specs = (
        P(f, "z", None),
        P(f, None, None),
        P(f, None),
        P(f),
        P(f),
        P(f, None, "z"),
        P(None, "z"),
        P("z", f),
        P(f),
        P(f),
        P(f),
        P(f, "z"),
        P("z"),
        P("z", f),
        P(f),
        P(f, "z", None),
    )
    out_specs = (
        P(f, "z", None),
        P(f, "z", None),
        P(f),
        P(f),
        P(f, None, "z"),
        P(None, "z"),
        P("z", f),
        P(f),
        P(f),
        P(f),
        P(f, "z"),
        P("z"),
        P("z", f),
        P(f),
    )
    return jax.shard_map(
        on_device, mesh=cut, in_specs=in_specs, out_specs=out_specs, check_vma=False
    )
```

time: 1570 us -> 991 us (0.63)
  matrix products: 435 us -> 191 us
  local copies, waits for them, and re-layouts: 278 us -> 93 us
  Pallas kernels: 0 us -> 158 us
  other arithmetic: 191 us -> 61.7 us
  blocking collectives: 128 us -> 0 us
  waiting for transfers between devices: 483 us -> 435 us
    unnamed x10 -> x6, waiting for transfers between devices: 372 us -> 1.29 us
    dot_general x21 -> x0, matrix products: 275 us -> none  [the longest x6 103 us: masked_scores(): jnp.einsum('qhd,khd->hqk', query_block, keys, preferred_element_type=jnp....]
    reduce_scatter x0 -> x3, waiting for transfers between devices: none -> 174 us  [scatter_all(): return lax.psum_scatter(total, ('z', 'g'), scatter_dimension=0, tiled=True)]
    pallas_call x0 -> x2, Pallas kernels: none -> 158 us  [the longest x1 86.5 us: attend(): pl.pallas_call(attend_kernel, grid=(heads,), in_specs=[whole(width), pl.B...]
    all_gather x1 -> x0, blocking collectives: 128 us -> none  [on_device(): lax.all_gather(small, ('g', 'c', 'z'), axis=0)]
    ppermute x4, waiting for transfers between devices: 42 us -> 150 us  [bring(): lax.ppermute(lax.dynamic_index_in_dim(packs, lax.rem(place + step, runs),...]
    dynamic_update_slice x6 -> x0, local copies, waits for them, and re-layouts: 82 us -> none  [attend_back(): lax.scan(one_block, (zeros, zeros), (queries.reshape(count, block, heads,...]
    convert_element_type x8 -> x3, other arithmetic: 75.4 us -> 2.08 us  [the longest x1 1.01 us: on_device(): tail = small_full[:, 0, 6 * shard:].astype(wide)]
  transfers between devices with their start and end apart: 28 -> 33, of which waited for: 12 -> 16; matrix products, arithmetic and copies ran while one was open for 26% -> 28% of each run, Pallas kernels for 0% -> 16%
where the time goes in v2:
time: 991 us; the launch traced here: 981 us
  waiting for transfers between devices  435 us (44%)
  matrix products  191 us (19%)
  Pallas kernels  158 us (16%)
  local copies, waits for them, and re-layouts  93 us (9%)
  other arithmetic  61.7 us (6%)
  starting transfers between devices  27.1 us (3%)
  between operations  15.9 us (2%)
    dot_general x14, matrix products, dot(): return jnp.einsum(form, left, right, preferred_element_type=jnp.float32)  191 us
    reduce_scatter x3, waiting for transfers between devices, scatter_all(): return lax.psum_scatter(total, ('z', 'g'), scatter_dimension=0, tiled=True)  174 us
    ppermute x4, waiting for transfers between devices, bring(): lax.ppermute(lax.dynamic_index_in_dim(packs, lax.rem(place + step, runs),...  150 us
    pallas_call x1, Pallas kernels, attend(): pl.pallas_call(attend_kernel, grid=(heads,), in_specs=[whole(width), pl.B...  86.5 us
    pallas_call x1, Pallas kernels, attend_back(): pl.pallas_call(back_kernel, grid=(heads,), in_specs=[wide, thin, thin, pl...  71.3 us
    ppermute x5, waiting for transfers between devices, sum_all(): lax.ppermute(values, axis, [(i, i ^ apart) for i in range(size)])  66.5 us
    all_gather x3, waiting for transfers between devices, gather_all(): return lax.all_gather(block, ('z', 'g'), axis=0, tiled=True)  37.3 us
  transfers between devices with their start and end apart: 33, of which 16 were waited for; matrix products, arithmetic and copies ran while one was open for 28% of the time, Pallas kernels for 16%

profile of v2, /device:TPU:11, one launch (start us, length us, event | category | flops | bytes accessed | tf_op | source)
XLA Modules:
  0.0 981.0 jit_solution(2785224300969230475)
XLA Ops:
  32.6 29.7 %collective-permute-done = bf16[384,1280]{1,0:T(8,128)(2,1)S(1)} collective-permute-done((bf16[384,1280]{1,0:T(8,128)(2,1)}, bf16[384,1280]{1,0:T(8,128)(2,1)S(1)}, u32[]{:S(2)}, u32[]{:S(2)}) %collective-permute-start) | collective-permute-done | bytes 983072 | tf_op jit(solution)/shard_map/ppermute | solution.py:264
  62.3 34.5 %collective-permute-done.1 = bf16[384,1280]{1,0:T(8,128)(2,1)} collective-permute-done((bf16[384,1280]{1,0:T(8,128)(2,1)}, bf16[384,1280]{1,0:T(8,128)(2,1)}, u32[]{:S(2)}, u32[]{:S(2)}) %collective-permute-start.1) | collective-permute-done | bytes 983072 | tf_op jit(solution)/shard_map/ppermute | solution.py:264
  100.5 37.2 %all-gather.4.cloned.1.call-done = bf16[5376,640]{1,0:T(8,128)(2,1)} async-done(((bf16[336,640]{1,0:T(8,128)(2,1)}), bf16[5376,640]{1,0:T(8,128)(2,1)}) %all-gather.4.cloned.1.call-update) | async-done | bytes 6881296 | tf_op jit(solution)/shard_map/all_gather | solution.py:307
  161.6 12.2 %convolution_convert_fusion.w_ref = bf16[4,1280,768]{2,1,0:T(8,128)(2,1)} fusion(bf16[4,1280,640]{2,1,0:T(8,128)(2,1)} %bitcast.183, bf16[640,768,1]{1,0,2:T(8,128)(2,1)S(1)} %copy-done.43), kind=kOutput, calls=%fused_computation.12 | convolution fusion | flops 5037096960 | bytes 15400960 | tf_op jit(solution)/shard_map/zdc,ck->zdk/dot_general | solution.py:329
  176.2 86.5 %shard_map.281 = (bf16[1536,3072]{1,0:T(8,128)(2,1)}, bf16[1536,1024]{1,0:T(8,128)(2,1)S(1)}, f32[8,1,1536]{2,1,0:T(1,128)S(1)}) custom-call(bf16[1536,1280]{1,0:T(8,128)(2,1)S(1)} %pad_maximum_fusion.x_ref, bf16[4,1280,768]{2,1,0:T(8,128)(2,1)} %convolution_convert_fusion.w_ref, f32[8,1,384]{2,1,0:T(1,128)S(1)} %reshape.270.b_ref, ...), custom_call_target="tpu_custom_call" | custom-call | flops 31406948352 | bytes 16515072 | tf_op jit(solution)/shard_map/pallas_call | solution.py:114
  275.9 49.6 %collective-permute-done.11 = bf16[384,1280]{1,0:T(8,128)(2,1)} collective-permute-done((bf16[384,1280]{1,0:T(8,128)(2,1)}, bf16[384,1280]{1,0:T(8,128)(2,1)}, u32[]{:S(2)}, u32[]{:S(2)}) %collective-permute-start.11) | collective-permute-done | bytes 983072 | tf_op jit(solution)/shard_map/ppermute | solution.py:264
  327.8 36.2 %collective-permute-done.12 = bf16[384,1280]{1,0:T(8,128)(2,1)} collective-permute-done((bf16[384,1280]{1,0:T(8,128)(2,1)}, bf16[384,1280]{1,0:T(8,128)(2,1)}, u32[]{:S(2)}, u32[]{:S(2)}) %collective-permute-start.12) | collective-permute-done | bytes 983072 | tf_op jit(solution)/shard_map/ppermute | solution.py:264
  377.6 18.9 %multiply_convert_fusion.1 = (bf16[1536,4,640]{2,0,1:T(8,128)(2,1)S(1)}, f32[1536,4,640]{2,0,1:T(8,128)}) fusion(f32[4,640]{1,0:T(4,128)S(1)} %fusion.38, bf16[4,1280,640]{2,1,0:T(8,128)(2,1)} %bitcast.221, bf16[768,1280]{1,0:T(8,128)(2,1)} %collective-permute-done.7, bf16[768,1280]{1,0:T(8,128)(2,1)} %add_convert_fusion), kind=kOutput, calls=%fused_computation.2 | convolution fusion | flops 10101719040 | bytes 34088960 | tf_op jit(solution)/shard_map/pd,zdf->pzf/dot_general | solution.py:329
  399.6 14.6 %convert_bitcast_fusion.1 = bf16[4,1280,640]{1,2,0:T(8,128)(2,1)} fusion(bf16[1536,4,640]{2,0,1:T(8,128)(2,1)S(1)} %get-tuple-element.107, bf16[1536,1280]{1,0:T(8,128)(2,1)} %constant_dynamic-update-slice_fusion.2), kind=kOutput, calls=%fused_computation.14 | convolution fusion | flops 10069606400 | bytes 18350080 | tf_op jit(solution)/shard_map/pd,pzf->zdf/dot_general | solution.py:329
  414.2 9.5 copy.138
  423.7 22.8 %convert_reduce_fusion = (f32[4,640]{1,0:T(4,128)}, bf16[1536,4,640]{2,0,1:T(8,128)(2,1)}) fusion(f32[1536,4,640]{2,0,1:T(8,128)} %get-tuple-element.108, f32[4,640]{1,0:T(4,128)S(1)} %fusion.38, bf16[4,1280,640]{2,1,0:T(8,128)(2,1)} %bitcast.223, bf16[1536,1280]{1,0:T(8,128)(2,1)} %constant_dynamic-update-slice_fusion.2), kind=kOutput, calls=%fused_computation | convolution fusion | flops 10117445632 | bytes 34099200 | tf_op jit(solution)/shard_map/pd,zdf->pzf/dot_general | solution.py:329
  446.6 14.7 %convolution_bitcast_fusion = f32[1536,1280]{1,0:T(8,128)S(1)} fusion(bf16[1536,4,640]{2,0,1:T(8,128)(2,1)} %get-tuple-element.110, bf16[4,1280,640]{2,1,0:T(8,128)(2,1)} %bitcast.222), kind=kOutput, calls=%fused_computation.6 | convolution fusion | flops 10066329600 | bytes 22282240 | tf_op jit(solution)/shard_map/pzf,zdf->pd/dot_general | solution.py:329
  463.1 14.2 %convolution_bitcast_fusion.1 = f32[1536,1280]{1,0:T(8,128)S(1)} fusion(bf16[1536,4,640]{2,0,1:T(8,128)(2,1)} %copy-done.44, bf16[4,1280,640]{2,1,0:T(8,128)(2,1)S(1)} %bitcast.224), kind=kOutput, calls=%fused_computation.7 | convolution fusion | flops 10066329600 | bytes 22282240 | tf_op jit(solution)/shard_map/pzf,zdf->pd/dot_general | solution.py:329
  498.5 14.6 %convert_bitcast_fusion = bf16[4,1280,640]{1,2,0:T(8,128)(2,1)} fusion(bf16[1536,4,640]{2,0,1:T(8,128)(2,1)S(1)} %bitcast.228, bf16[768,1280]{1,0:T(8,128)(2,1)} %collective-permute-done.7, bf16[768,1280]{1,0:T(8,128)(2,1)} %add_convert_fusion), kind=kOutput, calls=%fused_computation.13 | convolution fusion | flops 10077470720 | bytes 18350080 | tf_op jit(solution)/shard_map/pd,pzf->zdf/dot_general | solution.py:329
  513.1 9.5 copy.140
  534.3 71.3 %shard_map.282 = (bf16[1536,3072]{1,0:T(8,128)(2,1)}, f32[8,1,384]{2,1,0:T(1,128)S(1)}) custom-call(bf16[1536,3072]{1,0:T(8,128)(2,1)} %get-tuple-element.29.qkv_ref, bf16[1536,1024]{1,0:T(8,128)(2,1)S(1)} %copy-done.2, bf16[1536,1024]{1,0:T(8,128)(2,1)S(1)} %convolution_convert_fusion.3.grad_ref, f32[8,1,1536]{2,1,0:T(1,128)S(1)} %get-tuple-element.31.total_ref, ...), custom_call_target="tpu_custom_call" | custom-call | flops 24159191040 | bytes 25165824 | tf_op jit(solution)/shard_map/pallas_call | solution.py:200
  605.6 12.8 %copy.169 = bf16[1536,3072]{0,1:T(8,128)(2,1)} copy(bf16[1536,3072]{1,0:T(8,128)(2,1)} %get-tuple-element.32) | data formatting | bytes 18874368 | tf_op jit(solution)/shard_map/reshape | solution.py:500
  625.8 28.5 %fusion.1 = f32[4,1280,640]{2,1,0:T(8,128)} fusion(bf16[640,768,1]{1,0,2:T(8,128)(2,1)} %constant.152, bf16[1536,4,768]{0,2,1:T(8,128)(2,1)} %bitcast.178, bf16[1536,1280]{1,0:T(8,128)(2,1)} %copy-done), kind=kOutput, calls=%fused_computation.9 | convolution fusion | flops 17112760320 | bytes 27459584 | tf_op jit(solution)/shard_map/zdk,ck->zdc/dot_general | solution.py:329
  654.3 9.7 fusion
  664.6 16.0 %convolution_bitcast_fusion.2 = f32[1536,1280]{1,0:T(8,128)S(1)} fusion(bf16[1536,4,768]{0,2,1:T(8,128)(2,1)} %bitcast.179, bf16[4,1280,768]{2,1,0:T(8,128)(2,1)} %convolution_convert_fusion.w_ref), kind=kOutput, calls=%fused_computation.8 | convolution fusion | flops 12079595520 | bytes 25165824 | tf_op jit(solution)/shard_map/pzk,zdk->pd/dot_general | solution.py:329
  724.2 33.4 %collective-permute-done.22 = f32[16640]{0:T(1024)S(1)} collective-permute-done((f32[16640]{0:T(1024)S(1)}, f32[16640]{0:T(1024)S(1)}, u32[]{:S(2)}, u32[]{:S(2)}) %collective-permute-start.22) | collective-permute-done | bytes 66592 | tf_op jit(solution)/shard_map/ppermute | solution.py:323
  757.7 19.7 %collective-permute-done.23 = f32[16640]{0:T(1024)S(1)} collective-permute-done((f32[16640]{0:T(1024)S(1)}, f32[16640]{0:T(1024)S(1)}, u32[]{:S(2)}, u32[]{:S(2)}) %collective-permute-start.23) | collective-permute-done | bytes 66592 | tf_op jit(solution)/shard_map/ppermute | solution.py:323
  789.2 18.2 %reduce-scatter.4.cloned.1.call-done = bf16[320,640]{1,0:T(8,128)(2,1)} async-done(((bf16[5120,640]{1,0:T(8,128)(2,1)}), bf16[320,640]{1,0:T(8,128)(2,1)}) %reduce-scatter.4.cloned.1.call-update) | async-done | bytes 409616 | tf_op jit(solution)/shard_map/reduce_scatter | solution.py:315
  809.4 156.0 %reduce-scatter.6.cloned.1.call-done = bf16[320,640]{1,0:T(8,128)(2,1)} async-done(((bf16[5120,640]{1,0:T(8,128)(2,1)}), bf16[320,640]{1,0:T(8,128)(2,1)}) %reduce-scatter.6.cloned.1.call-update) | async-done | bytes 409616 | tf_op jit(solution)/shard_map/reduce_scatter | solution.py:315
  (312 shorter events, 194.7 us)
Async XLA Ops:
  7.2 130.5 %all-gather.4.cloned.1.call-start = ((), (), s32[]{:S(2)}) async-start(), calls=%async_computation.3 | async-start | bytes 7311360 | tf_op jit(solution)/shard_map/all_gather | solution.py:307
  18.1 356.9 %all-gather.6.cloned.1.call-start = ((), (), s32[]{:S(2)}) async-start(), calls=%async_computation.4 | async-start | bytes 6963200 | tf_op jit(solution)/shard_map/all_gather | solution.py:307
  18.8 404.9 %all-gather.8.cloned.1.call-start = ((), (), s32[]{:S(2)}) async-start(), calls=%async_computation.5 | async-start | bytes 6963200 | tf_op jit(solution)/shard_map/all_gather | solution.py:307
  21.8 40.5 %collective-permute-start = (bf16[384,1280]{1,0:T(8,128)(2,1)}, bf16[384,1280]{1,0:T(8,128)(2,1)S(1)}, u32[]{:S(2)}, u32[]{:S(2)}) collective-permute-start(bf16[384,1280]{1,0:T(8,128)(2,1)} %get-tuple-element.68), channel_id=1, source_target_pairs={{0,0},{1,1},{2,4},{3,5},{4,2},{5,3},{6,6},{7,7},{8,8},{9,9},{10,12... | collective-permute-start | bytes 2949128 | tf_op jit(solution)/shard_map/ppermute | solution.py:264
  26.3 70.5 %collective-permute-start.1 = (bf16[384,1280]{1,0:T(8,128)(2,1)}, bf16[384,1280]{1,0:T(8,128)(2,1)}, u32[]{:S(2)}, u32[]{:S(2)}) collective-permute-start(bf16[384,1280]{1,0:T(8,128)(2,1)} %get-tuple-element.69), channel_id=1, source_target_pairs={{0,1},{1,0},{2,5},{3,4},{4,3},{5,2},{6,7},{7,6},{8,9},{9,8},{10,13... | collective-permute-start | bytes 2949128 | tf_op jit(solution)/shard_map/ppermute | solution.py:264
  32.5 753.0 %reduce-scatter.8.cloned.1.call-start = ((), (), s32[]{:S(2)}) async-start(), calls=%async_computation.8 | async-start | bytes 6963200 | tf_op jit(solution)/shard_map/reduce_scatter | solution.py:315
  153.5 20.3 %collective-permute-start.4 = (bf16[768,1280]{1,0:T(8,128)(2,1)}, bf16[768,1280]{1,0:T(8,128)(2,1)}, u32[]{:S(2)}, u32[]{:S(2)}) collective-permute-start(bf16[768,1280]{1,0:T(8,128)(2,1)} %fusion.11), channel_id=1, source_target_pairs={{0,4},{4,0},{1,5},{5,1},{2,6},{6,2},{3,7},{7,3},{8,12},{12,8},{9,1... | collective-permute-start | bytes 5898248 | tf_op jit(solution)/shard_map/ppermute | solution.py:248
  268.4 97.8 %collective-permute-start.6 = (bf16[768,1280]{1,0:T(8,128)(2,1)}, bf16[768,1280]{1,0:T(8,128)(2,1)}, u32[]{:S(2)}, u32[]{:S(2)}) collective-permute-start(bf16[768,1280]{1,0:T(8,128)(2,1)} %slice.372), channel_id=1, source_target_pairs={{0,4},{4,0},{1,5},{5,1},{2,6},{6,2},{3,7},{7,3},{8,12},{12,8},{9,1... | collective-permute-start | bytes 5898248 | tf_op jit(solution)/shard_map/ppermute | solution.py:248
  271.6 54.0 %collective-permute-start.11 = (bf16[384,1280]{1,0:T(8,128)(2,1)}, bf16[384,1280]{1,0:T(8,128)(2,1)}, u32[]{:S(2)}, u32[]{:S(2)}) collective-permute-start(bf16[384,1280]{1,0:T(8,128)(2,1)} %get-tuple-element.63), channel_id=1, source_target_pairs={{0,0},{1,1},{2,4},{3,5},{4,2},{5,3},{6,6},{7,7},{8,8},{9,9},{10,12... | collective-permute-start | bytes 2949128 | tf_op jit(solution)/shard_map/ppermute | solution.py:264
  274.4 89.6 %collective-permute-start.12 = (bf16[384,1280]{1,0:T(8,128)(2,1)}, bf16[384,1280]{1,0:T(8,128)(2,1)}, u32[]{:S(2)}, u32[]{:S(2)}) collective-permute-start(bf16[384,1280]{1,0:T(8,128)(2,1)} %get-tuple-element.62), channel_id=1, source_target_pairs={{0,1},{1,0},{2,5},{3,4},{4,3},{5,2},{6,7},{7,6},{8,9},{9,8},{10,13... | collective-permute-start | bytes 2949128 | tf_op jit(solution)/shard_map/ppermute | solution.py:264
  366.2 7.2 collective-permute-start.13
  463.0 18.4 %collective-permute-start.14 = (bf16[768,1280]{1,0:T(8,128)(2,1)}, bf16[768,1280]{1,0:T(8,128)(2,1)}, u32[]{:S(2)}, u32[]{:S(2)}) collective-permute-start(bf16[768,1280]{1,0:T(8,128)(2,1)} %slice.370), channel_id=1, source_target_pairs={{0,4},{4,0},{1,5},{5,1},{2,6},{6,2},{3,7},{7,3},{8,12},{12,8},{9,1... | collective-permute-start | bytes 5898248 | tf_op jit(solution)/shard_map/ppermute | solution.py:248
  481.0 6.5 collective-permute-start.8
  481.3 326.1 %reduce-scatter.4.cloned.1.call-start = ((), (), s32[]{:S(2)}) async-start(), calls=%async_computation.6 | async-start | bytes 6963200 | tf_op jit(solution)/shard_map/reduce_scatter | solution.py:315
  498.1 24.5 %collective-permute-start.15 = (bf16[768,1280]{1,0:T(8,128)(2,1)}, bf16[768,1280]{1,0:T(8,128)(2,1)}, u32[]{:S(2)}, u32[]{:S(2)}) collective-permute-start(bf16[768,1280]{1,0:T(8,128)(2,1)} %convert_element_type.160), channel_id=1, source_target_pairs={{0,4},{4,0},{1,5},{5,1},{2,6},{6,2},{3,7},{7,3},{8,12},{12,8},{9,1... | collective-permute-start | bytes 5898248 | tf_op jit(solution)/shard_map/ppermute | solution.py:248
  664.1 301.3 %reduce-scatter.6.cloned.1.call-start = ((), (), s32[]{:S(2)}) async-start(), calls=%async_computation.7 | async-start | bytes 6963200 | tf_op jit(solution)/shard_map/reduce_scatter | solution.py:315
  687.5 92.1 %collective-permute-start.9 = (bf16[384,1280]{1,0:T(8,128)(2,1)}, bf16[384,1280]{1,0:T(8,128)(2,1)S(1)}, u32[]{:S(2)}, u32[]{:S(2)}) collective-permute-start(bf16[384,1280]{1,0:T(8,128)(2,1)} %get-tuple-element.67), channel_id=1, source_target_pairs={{0,0},{1,1},{4,2},{5,3},{2,4},{3,5},{6,6},{7,7},{8,8},{9,9},{12,10... | collective-permute-start | bytes 2949128 | tf_op jit(solution)/shard_map/ppermute | solution.py:279
  689.4 90.2 %collective-permute-start.10 = (bf16[384,1280]{1,0:T(8,128)(2,1)}, bf16[384,1280]{1,0:T(8,128)(2,1)}, u32[]{:S(2)}, u32[]{:S(2)}) collective-permute-start(bf16[384,1280]{1,0:T(8,128)(2,1)} %get-tuple-element.66), channel_id=1, source_target_pairs={{1,0},{0,1},{5,2},{4,3},{3,4},{2,5},{7,6},{6,7},{9,8},{8,9},{13,10... | collective-permute-start | bytes 2949128 | tf_op jit(solution)/shard_map/ppermute | solution.py:279
  701.5 78.1 %collective-permute-start.17 = (bf16[384,1280]{1,0:T(8,128)(2,1)}, bf16[384,1280]{1,0:T(8,128)(2,1)S(1)}, u32[]{:S(2)}, u32[]{:S(2)}) collective-permute-start(bf16[384,1280]{1,0:T(8,128)(2,1)} %get-tuple-element.61), channel_id=1, source_target_pairs={{0,0},{1,1},{4,2},{5,3},{2,4},{3,5},{6,6},{7,7},{8,8},{9,9},{12,10... | collective-permute-start | bytes 2949128 | tf_op jit(solution)/shard_map/ppermute | solution.py:279
  707.2 72.4 %collective-permute-start.18 = (bf16[384,1280]{1,0:T(8,128)(2,1)}, bf16[384,1280]{1,0:T(8,128)(2,1)S(1)}, u32[]{:S(2)}, u32[]{:S(2)}) collective-permute-start(bf16[384,1280]{1,0:T(8,128)(2,1)} %get-tuple-element.60), channel_id=1, source_target_pairs={{1,0},{0,1},{5,2},{4,3},{3,4},{2,5},{7,6},{6,7},{9,8},{8,9},{13,10... | collective-permute-start | bytes 2949128 | tf_op jit(solution)/shard_map/ppermute | solution.py:279
  709.6 8.7 collective-permute-start.20
  722.1 35.5 %collective-permute-start.22 = (f32[16640]{0:T(1024)S(1)}, f32[16640]{0:T(1024)S(1)}, u32[]{:S(2)}, u32[]{:S(2)}) collective-permute-start(f32[16640]{0:T(1024)S(1)} %add.250), channel_id=1, source_target_pairs={{0,1},{1,0},{2,3},{3,2},{4,5},{5,4},{6,7},{7,6},{8,9},{9,8},{10,11... | collective-permute-start | bytes 199688 | tf_op jit(solution)/shard_map/ppermute | solution.py:323
  757.6 19.8 %collective-permute-start.23 = (f32[16640]{0:T(1024)S(1)}, f32[16640]{0:T(1024)S(1)}, u32[]{:S(2)}, u32[]{:S(2)}) collective-permute-start(f32[16640]{0:T(1024)S(1)} %add.251), channel_id=1, source_target_pairs={{0,2},{1,3},{2,0},{3,1},{4,6},{5,7},{6,4},{7,5},{8,10},{9,11},{10,... | collective-permute-start | bytes 199688 | tf_op jit(solution)/shard_map/ppermute | solution.py:323
  808.5 159.0 %collective-permute-start.24 = (bf16[160,640]{1,0:T(8,128)(2,1)S(1)}, bf16[160,640]{1,0:T(8,128)(2,1)S(1)}, u32[]{:S(2)}, u32[]{:S(2)}) collective-permute-start(bf16[160,640]{1,0:T(8,128)(2,1)S(1)} %get-tuple-element.86), channel_id=1, source_target_pairs={{0,4},{4,0},{1,5},{5,1},{2,6},{6,2},{3,7},{7,3},{8,12},{12,8},{9,1... | collective-permute-start | bytes 614408 | tf_op jit(solution)/shard_map/ppermute | solution.py:248
  (56 other events, 895.8 us)
Sparse Core Ops, SparseCore 0:
  18.2 119.4 all-gather.3
  140.4 94.5 all-gather.5
  238.3 118.8 all-gather.7
  481.4 141.6 reduce-scatter.7
  664.2 143.1 reduce-scatter.3
  809.6 155.7 reduce-scatter.5

commit v3 on v2

--- a/solution.py
+++ b/solution.py
@@ -5,6 +5,7 @@
 from jax.experimental import pallas as pl
 from jax.experimental.pallas import tpu as pltpu
 from jax.sharding import Mesh, PartitionSpec as P
+
 
 HEAD_DIM = 80
 
@@ -107,9 +108,8 @@
 
 def attend(normed, weight, shift, cosine, sine, query_mark, key_mark):
     total, width = normed.shape
-    size = weight.shape[0]
     pairs = weight.shape[2] // (3 * LANES)
-    heads = size * pairs
+    heads = weight.shape[0] * pairs
     whole = lambda cols: pl.BlockSpec((total, cols), lambda h: (0, 0), pipeline_mode=pl.Buffered(1))
     return pl.pallas_call(
         attend_kernel,
@@ -307,12 +307,26 @@
     return lax.all_gather(block, ("z", "g"), axis=0, tiled=True)
 
 
-def flat(blocks):
-    return blocks.reshape(-1, blocks.shape[-1])
-
-
-def scatter_all(total):
-    return lax.psum_scatter(total, ("z", "g"), scatter_dimension=0, tiled=True)
+def flat(gathered, size):
+    rows, cols = gathered.shape
+    return gathered.reshape(size, rows // size, cols).transpose(1, 0, 2).reshape(rows // size, -1)
+
+
+def scatter_rows(total):
+    return lax.psum_scatter(total, "g", scatter_dimension=0, tiled=True)
+
+
+def scatter_cols(part, place, size):
+    cols = part.shape[1] // size
+
+    def piece(index):
+        return lax.dynamic_slice_in_dim(part, lax.rem(index, size) * cols, cols, 1)
+
+    result = piece(place).astype(jnp.float32)
+    for step in range(1, size):
+        pairs = [(source, (source + step) % size) for source in range(size)]
+        result = result + lax.ppermute(piece(place + step), "z", pairs).astype(jnp.float32)
+    return result
 
 
 def sum_all(values):
@@ -418,12 +432,11 @@
     small_full = arrived[:, :, 2 * shard : 2 * shard + 2 * lines].reshape(
         size, -1, lines * attn_cols
     )[:, :, :length]
-    fc1_full = gather_all(block[:, attn_cols : attn_cols + half_units]).reshape(
-        size, width, half_units
-    )
-    fc2_full = gather_all(block[:, attn_cols + half_units :]).reshape(size, width, half_units)
+    fc1_full = flat(gather_all(block[:, attn_cols : attn_cols + half_units]), size)
+    fc2_full = flat(gather_all(block[:, attn_cols + half_units :]), size)
     qkv_table, proj_table = pad_tables(half_cols)
-    qkv_full = dot("zdc,ck->zdk", attn_full, qkv_table).astype(jnp.bfloat16)
+    qkv_blocks = dot("zdc,ck->zdk", attn_full, qkv_table).astype(jnp.bfloat16)
+    qkv_full = qkv_blocks.transpose(1, 0, 2).reshape(width, -1)
     proj_full = (
         dot("zdc,ck->dzk", attn_full, proj_table).astype(jnp.bfloat16).reshape(width, -1)
     )
@@ -439,7 +452,7 @@
     qkv_shift = qkv_shift.reshape(size, 3, pairs, 2, MID).transpose(0, 2, 1, 3, 4)
     qkv_shift = jnp.pad(qkv_shift, ((0, 0),) * 4 + ((0, FREE),)).reshape(heads, 1, 3 * LANES)
     fc1_shifts = tail[:, 3 * local_cols :].reshape(size, 2, half_units)
-    fc1_shift = jnp.where(first, fc1_shifts[:, 0], fc1_shifts[:, 1])
+    fc1_shift = jnp.where(first, fc1_shifts[:, 0], fc1_shifts[:, 1]).reshape(-1)
 
     marks = jnp.concatenate([positions, segments[:, None, :]], axis=1)
     marks_other = swap(marks)
@@ -464,50 +477,56 @@
     normed_full = share(normed.astype(jnp.bfloat16))
     normed_full, cotangent = lax.optimization_barrier((normed_full, cotangent))
     out_grad = bring(cotangent, place, size)
+    out_grad_full = share(out_grad)
     qkv, mixed, log_total = attend(
-        normed_full, qkv_full, qkv_shift, cosine, sine, query_mark, key_mark
+        normed_full, qkv_blocks, qkv_shift, cosine, sine, query_mark, key_mark
     )
     middle = start_values + pair_sum(dot("pk,dk->pd", mixed, proj_full)) + proj_shift
     normed_two, unit_two, spread_two = normalize(middle, gain_two, shift_two)
     ffn_input = share(normed_two.astype(jnp.bfloat16))
-    before = dot("pd,zdf->pzf", ffn_input, fc1_full) + fc1_shift
+    before = dot("pd,df->pf", ffn_input, fc1_full) + fc1_shift
     sigma = jax.nn.sigmoid(1.702 * before)
     after = (before * sigma).astype(jnp.bfloat16)
-    outcome = middle + pair_sum(dot("pzf,zdf->pd", after, fc2_full)) + fc2_shift
+    outcome = middle + pair_sum(dot("pf,df->pd", after, fc2_full)) + fc2_shift
     output = take_back(outcome.astype(jnp.bfloat16), place, size)
 
     out_grad_wide = out_grad.astype(wide)
-    out_grad_full = share(out_grad)
-    fc2_grad = flat(dot("pd,pzf->zdf", out_grad_full, after).astype(jnp.bfloat16))
+    fc2_grad = dot("pd,pf->df", out_grad_full, after).astype(jnp.bfloat16)
     fc2_grad, out_grad_full = lax.optimization_barrier((fc2_grad, out_grad_full))
-    fc2_part = scatter_all(fc2_grad)
-    after_grad = dot("pd,zdf->pzf", out_grad_full, fc2_full)
+    fc2_rows = scatter_rows(fc2_grad)
+    after_grad = dot("pd,df->pf", out_grad_full, fc2_full)
     before_grad = (after_grad * (sigma + 1.702 * before * sigma * (1.0 - sigma))).astype(
         jnp.bfloat16
     )
-    fc1_grad = flat(dot("pd,pzf->zdf", ffn_input, before_grad).astype(jnp.bfloat16))
+    fc1_grad = dot("pd,pf->df", ffn_input, before_grad).astype(jnp.bfloat16)
     fc1_bias_total = jnp.sum(before_grad.astype(wide), axis=0)
-    normed_two_grad = pair_sum(dot("pzf,zdf->pd", before_grad, fc1_full))
+    normed_two_grad = pair_sum(dot("pf,df->pd", before_grad, fc1_full))
     middle_grad = out_grad_wide + normalize_back(normed_two_grad, unit_two, spread_two, gain_two)
     branch_grad_full = share(middle_grad.astype(jnp.bfloat16))
     branch_grad_full, fc1_grad = lax.optimization_barrier((branch_grad_full, fc1_grad))
-    fc1_part = scatter_all(fc1_grad)
+    fc1_rows = scatter_rows(fc1_grad)
     proj_grad = dot("pd,pk->dk", branch_grad_full, mixed).astype(jnp.bfloat16)
     mixed_grad = dot("pd,dk->pk", branch_grad_full, proj_full).astype(jnp.bfloat16)
-    projected_grad, qkv_bias_total = attend_back(
-        qkv, mixed, mixed_grad, log_total, cosine, sine
-    )
-    split_grad = projected_grad.reshape(projected_grad.shape[0], size, -1)
-    qkv_grad = dot("pd,pzk->zdk", normed_full, split_grad).astype(jnp.bfloat16)
-    attn_part = scatter_all(
-        flat(
-            (
-                dot("zdk,ck->zdc", qkv_grad, qkv_table)
-                + dot("dzk,ck->zdc", proj_grad.reshape(width, size, -1), proj_table)
-            ).astype(jnp.bfloat16)
+    fc2_part = scatter_cols(fc2_rows, place, size)
+    projected_grad, qkv_bias_total = attend_back(qkv, mixed, mixed_grad, log_total, cosine, sine)
+    qkv_grad = dot("pd,pk->dk", normed_full, projected_grad).astype(jnp.bfloat16)
+    lanes = pairs * LANES
+    attn_rows = scatter_rows(
+        jnp.concatenate(
+            [
+                (
+                    dot("dk,ck->dc", qkv_grad[:, 3 * lanes * n : 3 * lanes * (n + 1)], qkv_table)
+                    + dot("dk,ck->dc", proj_grad[:, lanes * n : lanes * (n + 1)], proj_table)
+                ).astype(jnp.bfloat16)
+                for n in range(size)
+            ],
+            axis=1,
         )
     )
-    normed_grad = pair_sum(dot("pzk,zdk->pd", split_grad, qkv_full))
+    fc1_part = scatter_cols(fc1_rows, place, size)
+    normed_partial = dot("pk,dk->pd", projected_grad, qkv_full)
+    normed_grad = pair_sum(normed_partial)
+    attn_part = scatter_cols(attn_rows, place, size)
     hidden_grad = middle_grad + normalize_back(normed_grad, unit_one, spread_one, gain_one)
     input_grad = take_back(hidden_grad.astype(jnp.bfloat16), place, size)
 
@@ -532,7 +551,7 @@
                     ]
                 ),
                 halves(qkv_bias_total).reshape(-1),
-                halves(fc1_bias_total).reshape(-1),
+                halves(fc1_bias_total.reshape(size, half_units)).reshape(-1),
             ]
         )
     )
@@ -551,8 +570,9 @@
 
     def own_rows(part):
         mine = jnp.where(first, part[:shard], part[shard:])
-        theirs = swap(jnp.where(first, part[shard:], part[:shard]))
-        return jnp.where(first, jnp.stack([mine, theirs]), jnp.stack([theirs, mine])).astype(wide)
+        theirs = jnp.where(first, part[shard:], part[:shard]).astype(jnp.bfloat16)
+        theirs = swap(theirs).astype(wide)
+        return jnp.where(first, jnp.stack([mine, theirs]), jnp.stack([theirs, mine]))
 
     fc2_sum = own_rows(fc2_part).transpose(0, 2, 1).reshape(units, shard)
     fc1_sum = own_rows(fc1_part).transpose(1, 0, 2).reshape(shard, units)
@@ -620,6 +640,7 @@
         P("z", f),
         P(f),
     )
+
     return jax.shard_map(
         on_device, mesh=cut, in_specs=in_specs, out_specs=out_specs, check_vma=False
     )

time: 991 us -> 912 us (0.920)
  waiting for transfers between devices: 435 us -> 347 us
  matrix products: 191 us -> 178 us
  starting transfers between devices: 27.1 us -> 37.1 us
    reduce_scatter x3, waiting for transfers between devices: 174 us -> 0.02 us  [scatter_rows(): return lax.psum_scatter(total, 'g', scatter_dimension=0, tiled=True)]
    ppermute x0 -> x9, waiting for transfers between devices: none -> 88.3 us  [scatter_cols(): lax.ppermute(piece(place + step), 'z', pairs).astype(jnp.float32)]
    dot_general x14 -> x21, matrix products: 191 us -> 178 us  [dot(): return jnp.einsum(form, left, right, preferred_element_type=jnp.float32)]
    ppermute x0 -> x9, starting transfers between devices: none -> 9.99 us  [scatter_cols(): lax.ppermute(piece(place + step), 'z', pairs).astype(jnp.float32)]
  transfers between devices with their start and end apart: 33 -> 42, of which waited for: 16 -> 21; matrix products, arithmetic and copies ran while one was open for 28% -> 31% of each run, Pallas kernels for 16% -> 17%
where the time goes in v3:
time: 912 us; the launch traced here: 903 us
  waiting for transfers between devices  347 us (38%)
  matrix products  178 us (20%)
  Pallas kernels  158 us (17%)
  local copies, waits for them, and re-layouts  97.7 us (11%)
  other arithmetic  70.1 us (8%)
  starting transfers between devices  37.1 us (4%)
  between operations  15.9 us (2%)
    dot_general x21, matrix products, dot(): return jnp.einsum(form, left, right, preferred_element_type=jnp.float32)  178 us
    ppermute x4, waiting for transfers between devices, bring(): lax.ppermute(lax.dynamic_index_in_dim(packs, lax.rem(place + step, runs),...  150 us
    ppermute x9, waiting for transfers between devices, scatter_cols(): lax.ppermute(piece(place + step), 'z', pairs).astype(jnp.float32)  88.3 us
    pallas_call x1, Pallas kernels, attend(): pl.pallas_call(attend_kernel, grid=(heads,), in_specs=[whole(width), pl.B...  86.4 us
    pallas_call x1, Pallas kernels, attend_back(): pl.pallas_call(back_kernel, grid=(heads,), in_specs=[wide, thin, thin, pl...  71.4 us
    ppermute x5, waiting for transfers between devices, sum_all(): lax.ppermute(values, axis, [(i, i ^ apart) for i in range(size)])  66.9 us
    all_gather x3, waiting for transfers between devices, gather_all(): return lax.all_gather(block, ('z', 'g'), axis=0, tiled=True)  37.6 us
    reshape x2, local copies, waits for them, and re-layouts, flat(): gathered.reshape(size, rows // size, cols).transpose(1, 0, 2)  19.2 us
  transfers between devices with their start and end apart: 42, of which 21 were waited for; matrix products, arithmetic and copies ran while one was open for 31% of the time, Pallas kernels for 17%

profile of v3, /device:TPU:11, one launch (start us, length us, event | category | flops | bytes accessed | tf_op | source)
XLA Modules:
  0.0 903.5 jit_solution(12283252125518773858)
XLA Ops:
  38.2 28.0 %collective-permute-done = bf16[384,1280]{1,0:T(8,128)(2,1)S(1)} collective-permute-done((bf16[384,1280]{1,0:T(8,128)(2,1)}, bf16[384,1280]{1,0:T(8,128)(2,1)S(1)}, u32[]{:S(2)}, u32[]{:S(2)}) %collective-permute-start) | collective-permute-done | bytes 983072 | tf_op jit(solution)/shard_map/ppermute | solution.py:264
  66.2 35.7 %collective-permute-done.1 = bf16[384,1280]{1,0:T(8,128)(2,1)} collective-permute-done((bf16[384,1280]{1,0:T(8,128)(2,1)}, bf16[384,1280]{1,0:T(8,128)(2,1)}, u32[]{:S(2)}, u32[]{:S(2)}) %collective-permute-start.1) | collective-permute-done | bytes 983072 | tf_op jit(solution)/shard_map/ppermute | solution.py:264
  105.6 37.6 %all-gather.4.cloned.1.call-done = bf16[5376,640]{1,0:T(8,128)(2,1)} async-done(((bf16[336,640]{1,0:T(8,128)(2,1)}), bf16[5376,640]{1,0:T(8,128)(2,1)}) %all-gather.4.cloned.1.call-update) | async-done | bytes 6881296 | tf_op jit(solution)/shard_map/all_gather | solution.py:307
  166.9 12.2 %convolution_convert_fusion.3.w_ref = bf16[4,1280,768]{2,1,0:T(8,128)(2,1)} fusion(bf16[4,1280,640]{2,1,0:T(8,128)(2,1)} %bitcast.148, bf16[640,768,1]{0,1,2:T(8,128)(2,1)S(1)} %copy-done.45), kind=kOutput, calls=%fused_computation.7 | convolution fusion | flops 5037096960 | bytes 15400960 | tf_op jit(solution)/shard_map/zdc,ck->zdk/dot_general | solution.py:343
  181.5 86.4 %shard_map.281 = (bf16[1536,3072]{1,0:T(8,128)(2,1)}, bf16[1536,1024]{1,0:T(8,128)(2,1)S(1)}, f32[8,1,1536]{2,1,0:T(1,128)S(1)}) custom-call(bf16[1536,1280]{1,0:T(8,128)(2,1)S(1)} %pad_maximum_fusion.1.x_ref, bf16[4,1280,768]{2,1,0:T(8,128)(2,1)} %convolution_convert_fusion.3.w_ref, f32[8,1,384]{2,1,0:T(1,128)S(1)} %reshape.258.b_ref, ...), custom_call_target="tpu_custom_call" | custom-call | flops 31406948352 | bytes 16515072 | tf_op jit(solution)/shard_map/pallas_call | solution.py:114
  281.2 49.4 %collective-permute-done.11 = bf16[384,1280]{1,0:T(8,128)(2,1)} collective-permute-done((bf16[384,1280]{1,0:T(8,128)(2,1)}, bf16[384,1280]{1,0:T(8,128)(2,1)}, u32[]{:S(2)}, u32[]{:S(2)}) %collective-permute-start.11) | collective-permute-done | bytes 983072 | tf_op jit(solution)/shard_map/ppermute | solution.py:264
  332.9 36.5 %collective-permute-done.12 = bf16[384,1280]{1,0:T(8,128)(2,1)} collective-permute-done((bf16[384,1280]{1,0:T(8,128)(2,1)}, bf16[384,1280]{1,0:T(8,128)(2,1)}, u32[]{:S(2)}, u32[]{:S(2)}) %collective-permute-start.12) | collective-permute-done | bytes 983072 | tf_op jit(solution)/shard_map/ppermute | solution.py:264
  380.2 9.7 %copy.160 = bf16[4,1280,640]{1,2,0:T(8,128)(2,1)} copy(bf16[4,1280,640]{2,1,0:T(8,128)(2,1)} %bitcast.143) | data formatting | bytes 13107200 | tf_op jit(solution)/shard_map/reshape | solution.py:312
  389.9 9.5 %copy.161 = bf16[4,1280,640]{1,2,0:T(8,128)(2,1)} copy(bf16[4,1280,640]{2,1,0:T(8,128)(2,1)} %bitcast.144) | data formatting | bytes 13107200 | tf_op jit(solution)/shard_map/reshape | solution.py:312
  402.7 20.3 %multiply_convert_fusion.1 = (bf16[1536,2560]{1,0:T(8,128)(2,1)}, f32[1536,2560]{1,0:T(8,128)}) fusion(f32[2560]{0:T(1024)S(1)} %select_n.232, bf16[1280,2560]{0,1:T(8,128)(2,1)} %bitcast.149, bf16[768,1280]{1,0:T(8,128)(2,1)} %collective-permute-done.7, bf16[768,1280]{1,0:T(8,128)(2,1)} %add_convert_fusion), kind=kOutput, calls=%fused_computation.2 | convolution fusion | flops 10101719040 | bytes 34088960 | tf_op jit(solution)/shard_map/pd,df->pf/dot_general | solution.py:343
  423.0 14.7 %convolution_convert_fusion.2 = bf16[1280,2560]{1,0:T(8,128)(2,1)} fusion(bf16[1536,1280]{1,0:T(8,128)(2,1)S(1)} %copy-done.23, bf16[1536,2560]{1,0:T(8,128)(2,1)} %get-tuple-element.110), kind=kOutput, calls=%fused_computation.6 | convolution fusion | flops 10069606400 | bytes 18350080 | tf_op jit(solution)/shard_map/pd,pf->df/dot_general | solution.py:343
  437.8 23.4 %convert_reduce_fusion = (f32[2560]{0:T(1024)}, bf16[1536,2560]{1,0:T(8,128)(2,1)}) fusion(f32[1536,2560]{1,0:T(8,128)} %get-tuple-element.111, f32[2560]{0:T(1024)S(1)} %select_n.232, bf16[1536,1280]{1,0:T(8,128)(2,1)} %constant_dynamic-update-slice_fusion.2, bf16[1280,2560]{0,1:T(8,128)(2,1)} %bitcast.145), kind=kOutput, calls=%fused_computation | convolution fusion | flops 10117445632 | bytes 34099200 | tf_op jit(solution)/shard_map/pd,df->pf/dot_general | solution.py:343
  461.3 14.9 %fusion.66 = f32[1536,1280]{1,0:T(8,128)S(1)} fusion(bf16[1536,2560]{1,0:T(8,128)(2,1)} %get-tuple-element.113, bf16[1280,2560]{0,1:T(8,128)(2,1)} %bitcast.150), kind=kOutput, calls=%fused_computation.220 | convolution fusion | flops 10066329600 | bytes 22282240 | tf_op jit(solution)/shard_map/pf,df->pd/dot_general | solution.py:343
  478.1 16.1 %fusion.65 = f32[1536,1280]{1,0:T(8,128)S(1)} fusion(bf16[1536,2560]{1,0:T(8,128)(2,1)} %get-tuple-element.110, bf16[1280,2560]{0,1:T(8,128)(2,1)} %bitcast.146), kind=kOutput, calls=%fused_computation.219 | convolution fusion | flops 10066329600 | bytes 22282240 | tf_op jit(solution)/shard_map/pf,df->pd/dot_general | solution.py:343
  514.9 14.2 %convolution_convert_fusion.1 = bf16[1280,2560]{1,0:T(8,128)(2,1)} fusion(bf16[1536,2560]{1,0:T(8,128)(2,1)S(1)} %bitcast.185, bf16[768,1280]{1,0:T(8,128)(2,1)} %collective-permute-done.7, bf16[768,1280]{1,0:T(8,128)(2,1)} %add_convert_fusion), kind=kOutput, calls=%fused_computation.5 | convolution fusion | flops 10077470720 | bytes 18350080 | tf_op jit(solution)/shard_map/pd,pf->df/dot_general | solution.py:343
  541.1 71.4 %shard_map.282 = (bf16[1536,3072]{1,0:T(8,128)(2,1)}, f32[8,1,384]{2,1,0:T(1,128)S(1)}) custom-call(bf16[1536,3072]{1,0:T(8,128)(2,1)} %get-tuple-element.29.qkv_ref, bf16[1536,1024]{1,0:T(8,128)(2,1)S(1)} %copy-done.3, bf16[1536,1024]{1,0:T(8,128)(2,1)S(1)} %convolution_convert_fusion.6.grad_ref, f32[8,1,1536]{2,1,0:T(1,128)S(1)} %get-tuple-element.31.total_ref, ...), custom_call_target="tpu_custom_call" | custom-call | flops 24159191040 | bytes 25165824 | tf_op jit(solution)/shard_map/pallas_call | solution.py:200
  612.6 14.9 %convolution_convert_fusion = bf16[1280,3072]{1,0:T(8,128)(2,1)S(1)} fusion(bf16[1536,1280]{1,0:T(8,128)(2,1)S(1)} %copy-done.1, bf16[1536,3072]{1,0:T(8,128)(2,1)} %get-tuple-element.32), kind=kOutput, calls=%fused_computation.4 | convolution fusion | flops 12083527680 | bytes 21233664 | tf_op jit(solution)/shard_map/pd,pk->dk/dot_general | solution.py:343
  645.9 10.8 %copy.162 = bf16[1280,4,768]{0,2,1:T(8,128)(2,1)} copy(bf16[1280,4,768]{2,0,1:T(8,128)(2,1)} %bitcast.139) | data formatting | bytes 15728640 | tf_op jit(solution)/shard_map/convert_element_type | solution.py:438
  656.7 16.0 %fusion.67 = f32[1536,1280]{1,0:T(8,128)S(1)} fusion(bf16[1536,3072]{1,0:T(8,128)(2,1)} %get-tuple-element.32, bf16[1280,3072]{0,1:T(8,128)(2,1)} %bitcast.140), kind=kOutput, calls=%fused_computation.221 | convolution fusion | flops 12079595520 | bytes 25165824 | tf_op jit(solution)/shard_map/pk,dk->pd/dot_general | solution.py:343
  713.3 35.7 %collective-permute-done.22 = f32[16640]{0:T(1024)S(1)} collective-permute-done((f32[16640]{0:T(1024)S(1)}, f32[16640]{0:T(1024)S(1)}, u32[]{:S(2)}, u32[]{:S(2)}) %collective-permute-start.22) | collective-permute-done | bytes 66592 | tf_op jit(solution)/shard_map/ppermute | solution.py:337
  749.2 20.3 %collective-permute-done.23 = f32[16640]{0:T(1024)S(1)} collective-permute-done((f32[16640]{0:T(1024)S(1)}, f32[16640]{0:T(1024)S(1)}, u32[]{:S(2)}, u32[]{:S(2)}) %collective-permute-start.23) | collective-permute-done | bytes 66592 | tf_op jit(solution)/shard_map/ppermute | solution.py:337
  783.2 23.7 %collective-permute-done.33 = bf16[320,640]{1,0:T(8,128)(2,1)S(1)} collective-permute-done((bf16[320,640]{1,0:T(8,128)(2,1)S(1)}, bf16[320,640]{1,0:T(8,128)(2,1)S(1)}, u32[]{:S(2)}, u32[]{:S(2)}) %collective-permute-start.33) | collective-permute-done | bytes 409632 | tf_op jit(solution)/shard_map/ppermute | solution.py:328
  828.2 24.4 %collective-permute-done.29 = bf16[320,640]{1,0:T(8,128)(2,1)} collective-permute-done((bf16[320,640]{1,0:T(8,128)(2,1)}, bf16[320,640]{1,0:T(8,128)(2,1)}, u32[]{:S(2)}, u32[]{:S(2)}) %collective-permute-start.29) | collective-permute-done | bytes 409632 | tf_op jit(solution)/shard_map/ppermute | solution.py:328
  852.6 18.0 %collective-permute-done.30 = bf16[320,640]{1,0:T(8,128)(2,1)} collective-permute-done((bf16[320,640]{1,0:T(8,128)(2,1)S(1)}, bf16[320,640]{1,0:T(8,128)(2,1)}, u32[]{:S(2)}, u32[]{:S(2)}) %collective-permute-start.30) | collective-permute-done | bytes 409632 | tf_op jit(solution)/shard_map/ppermute | solution.py:328
  (354 shorter events, 243.7 us)
Async XLA Ops:
  7.2 136.0 %all-gather.4.cloned.1.call-start = ((), (), s32[]{:S(2)}) async-start(), calls=%async_computation.3 | async-start | bytes 7311360 | tf_op jit(solution)/shard_map/all_gather | solution.py:307
  24.6 355.6 %all-gather.6.cloned.1.call-start = ((), (), s32[]{:S(2)}) async-start(), calls=%async_computation.4 | async-start | bytes 6963200 | tf_op jit(solution)/shard_map/all_gather | solution.py:307
  25.4 364.5 %all-gather.8.cloned.1.call-start = ((), (), s32[]{:S(2)}) async-start(), calls=%async_computation.5 | async-start | bytes 6963200 | tf_op jit(solution)/shard_map/all_gather | solution.py:307
  26.8 39.3 %collective-permute-start = (bf16[384,1280]{1,0:T(8,128)(2,1)}, bf16[384,1280]{1,0:T(8,128)(2,1)S(1)}, u32[]{:S(2)}, u32[]{:S(2)}) collective-permute-start(bf16[384,1280]{1,0:T(8,128)(2,1)} %get-tuple-element.68), channel_id=1, source_target_pairs={{0,0},{1,1},{2,4},{3,5},{4,2},{5,3},{6,6},{7,7},{8,8},{9,9},{10,12... | collective-permute-start | bytes 2949128 | tf_op jit(solution)/shard_map/ppermute | solution.py:264
  31.3 70.5 %collective-permute-start.1 = (bf16[384,1280]{1,0:T(8,128)(2,1)}, bf16[384,1280]{1,0:T(8,128)(2,1)}, u32[]{:S(2)}, u32[]{:S(2)}) collective-permute-start(bf16[384,1280]{1,0:T(8,128)(2,1)} %get-tuple-element.69), channel_id=1, source_target_pairs={{0,1},{1,0},{2,5},{3,4},{4,3},{5,2},{6,7},{7,6},{8,9},{9,8},{10,13... | collective-permute-start | bytes 2949128 | tf_op jit(solution)/shard_map/ppermute | solution.py:264
  37.6 734.0 %reduce-scatter.8.cloned.1.call-start = ((), (), s32[]{:S(2)}) async-start(), calls=%async_computation.8 | async-start | bytes 8192000 | tf_op jit(solution)/shard_map/reduce_scatter | solution.py:316
  273.7 100.1 %collective-permute-start.6 = (bf16[768,1280]{1,0:T(8,128)(2,1)}, bf16[768,1280]{1,0:T(8,128)(2,1)}, u32[]{:S(2)}, u32[]{:S(2)}) collective-permute-start(bf16[768,1280]{1,0:T(8,128)(2,1)} %slice.426), channel_id=1, source_target_pairs={{0,4},{4,0},{1,5},{5,1},{2,6},{6,2},{3,7},{7,3},{8,12},{12,8},{9,1... | collective-permute-start | bytes 5898248 | tf_op jit(solution)/shard_map/ppermute | solution.py:248
  276.8 53.8 %collective-permute-start.11 = (bf16[384,1280]{1,0:T(8,128)(2,1)}, bf16[384,1280]{1,0:T(8,128)(2,1)}, u32[]{:S(2)}, u32[]{:S(2)}) collective-permute-start(bf16[384,1280]{1,0:T(8,128)(2,1)} %get-tuple-element.63), channel_id=1, source_target_pairs={{0,0},{1,1},{2,4},{3,5},{4,2},{5,3},{6,6},{7,7},{8,8},{9,9},{10,12... | collective-permute-start | bytes 2949128 | tf_op jit(solution)/shard_map/ppermute | solution.py:264
  279.7 89.7 %collective-permute-start.12 = (bf16[384,1280]{1,0:T(8,128)(2,1)}, bf16[384,1280]{1,0:T(8,128)(2,1)}, u32[]{:S(2)}, u32[]{:S(2)}) collective-permute-start(bf16[384,1280]{1,0:T(8,128)(2,1)} %get-tuple-element.62), channel_id=1, source_target_pairs={{0,1},{1,0},{2,5},{3,4},{4,3},{5,2},{6,7},{7,6},{8,9},{9,8},{10,13... | collective-permute-start | bytes 2949128 | tf_op jit(solution)/shard_map/ppermute | solution.py:264
  371.7 27.8 %collective-permute-start.13 = (bf16[768,1280]{1,0:T(8,128)(2,1)}, bf16[768,1280]{1,0:T(8,128)(2,1)}, u32[]{:S(2)}, u32[]{:S(2)}) collective-permute-start(bf16[768,1280]{1,0:T(8,128)(2,1)} %get-tuple-element.84), channel_id=1, source_target_pairs={{0,4},{4,0},{1,5},{5,1},{2,6},{6,2},{3,7},{7,3},{8,12},{12,8},{9,1... | collective-permute-start | bytes 5898248 | tf_op jit(solution)/shard_map/ppermute | solution.py:248
  437.8 376.8 %reduce-scatter.6.cloned.1.call-start = ((), (), s32[]{:S(2)}) async-start(), calls=%async_computation.7 | async-start | bytes 8192000 | tf_op jit(solution)/shard_map/reduce_scatter | solution.py:316
  533.5 286.3 %reduce-scatter.4.cloned.1.call-start = ((), (), s32[]{:S(2)}) async-start(), calls=%async_computation.6 | async-start | bytes 8192000 | tf_op jit(solution)/shard_map/reduce_scatter | solution.py:316
  679.5 93.5 %collective-permute-start.9 = (bf16[384,1280]{1,0:T(8,128)(2,1)}, bf16[384,1280]{1,0:T(8,128)(2,1)S(1)}, u32[]{:S(2)}, u32[]{:S(2)}) collective-permute-start(bf16[384,1280]{1,0:T(8,128)(2,1)} %get-tuple-element.67), channel_id=1, source_target_pairs={{0,0},{1,1},{4,2},{5,3},{2,4},{3,5},{6,6},{7,7},{8,8},{9,9},{12,10... | collective-permute-start | bytes 2949128 | tf_op jit(solution)/shard_map/ppermute | solution.py:279
  681.6 94.4 %collective-permute-start.10 = (bf16[384,1280]{1,0:T(8,128)(2,1)}, bf16[384,1280]{1,0:T(8,128)(2,1)S(1)}, u32[]{:S(2)}, u32[]{:S(2)}) collective-permute-start(bf16[384,1280]{1,0:T(8,128)(2,1)} %get-tuple-element.66), channel_id=1, source_target_pairs={{1,0},{0,1},{5,2},{4,3},{3,4},{2,5},{7,6},{6,7},{9,8},{8,9},{13,10... | collective-permute-start | bytes 2949128 | tf_op jit(solution)/shard_map/ppermute | solution.py:279
  693.4 83.9 %collective-permute-start.17 = (bf16[384,1280]{1,0:T(8,128)(2,1)}, bf16[384,1280]{1,0:T(8,128)(2,1)S(1)}, u32[]{:S(2)}, u32[]{:S(2)}) collective-permute-start(bf16[384,1280]{1,0:T(8,128)(2,1)} %get-tuple-element.61), channel_id=1, source_target_pairs={{0,0},{1,1},{4,2},{5,3},{2,4},{3,5},{6,6},{7,7},{8,8},{9,9},{12,10... | collective-permute-start | bytes 2949128 | tf_op jit(solution)/shard_map/ppermute | solution.py:279
  698.8 78.5 %collective-permute-start.18 = (bf16[384,1280]{1,0:T(8,128)(2,1)}, bf16[384,1280]{1,0:T(8,128)(2,1)}, u32[]{:S(2)}, u32[]{:S(2)}) collective-permute-start(bf16[384,1280]{1,0:T(8,128)(2,1)} %get-tuple-element.60), channel_id=1, source_target_pairs={{1,0},{0,1},{5,2},{4,3},{3,4},{2,5},{7,6},{6,7},{9,8},{8,9},{13,10... | collective-permute-start | bytes 2949128 | tf_op jit(solution)/shard_map/ppermute | solution.py:279
  713.3 35.8 %collective-permute-start.22 = (f32[16640]{0:T(1024)S(1)}, f32[16640]{0:T(1024)S(1)}, u32[]{:S(2)}, u32[]{:S(2)}) collective-permute-start(f32[16640]{0:T(1024)S(1)} %add.319), channel_id=1, source_target_pairs={{0,1},{1,0},{2,3},{3,2},{4,5},{5,4},{6,7},{7,6},{8,9},{9,8},{10,11... | collective-permute-start | bytes 199688 | tf_op jit(solution)/shard_map/ppermute | solution.py:337
  773.1 33.8 %collective-permute-start.33 = (bf16[320,640]{1,0:T(8,128)(2,1)S(1)}, bf16[320,640]{1,0:T(8,128)(2,1)S(1)}, u32[]{:S(2)}, u32[]{:S(2)}) collective-permute-start(bf16[320,640]{1,0:T(8,128)(2,1)S(1)} %get-tuple-element.72), channel_id=1, source_target_pairs={{0,2},{1,3},{2,0},{3,1},{4,6},{5,7},{6,4},{7,5},{8,10},{9,11},{10,... | collective-permute-start | bytes 1228808 | tf_op jit(solution)/shard_map/ppermute | solution.py:328
  775.9 36.2 %collective-permute-start.34 = (bf16[320,640]{1,0:T(8,128)(2,1)S(1)}, bf16[320,640]{1,0:T(8,128)(2,1)S(1)}, u32[]{:S(2)}, u32[]{:S(2)}) collective-permute-start(bf16[320,640]{1,0:T(8,128)(2,1)S(1)} %get-tuple-element.71), channel_id=1, source_target_pairs={{0,3},{1,0},{2,1},{3,2},{4,7},{5,4},{6,5},{7,6},{8,11},{9,8},{10,9... | collective-permute-start | bytes 1228808 | tf_op jit(solution)/shard_map/ppermute | solution.py:328
  816.8 35.7 %collective-permute-start.29 = (bf16[320,640]{1,0:T(8,128)(2,1)}, bf16[320,640]{1,0:T(8,128)(2,1)}, u32[]{:S(2)}, u32[]{:S(2)}) collective-permute-start(bf16[320,640]{1,0:T(8,128)(2,1)} %get-tuple-element.75), channel_id=1, source_target_pairs={{0,2},{1,3},{2,0},{3,1},{4,6},{5,7},{6,4},{7,5},{8,10},{9,11},{10,... | collective-permute-start | bytes 1228808 | tf_op jit(solution)/shard_map/ppermute | solution.py:328
  816.8 53.8 %collective-permute-start.30 = (bf16[320,640]{1,0:T(8,128)(2,1)S(1)}, bf16[320,640]{1,0:T(8,128)(2,1)}, u32[]{:S(2)}, u32[]{:S(2)}) collective-permute-start(bf16[320,640]{1,0:T(8,128)(2,1)S(1)} %get-tuple-element.74), channel_id=1, source_target_pairs={{0,3},{1,0},{2,1},{3,2},{4,7},{5,4},{6,5},{7,6},{8,11},{9,8},{10,9... | collective-permute-start | bytes 1228808 | tf_op jit(solution)/shard_map/ppermute | solution.py:328
  821.2 57.6 %collective-permute-start.24 = (bf16[320,640]{1,0:T(8,128)(2,1)S(1)}, bf16[320,640]{1,0:T(8,128)(2,1)S(1)}, u32[]{:S(2)}, u32[]{:S(2)}) collective-permute-start(bf16[320,640]{1,0:T(8,128)(2,1)S(1)} %get-tuple-element.76), channel_id=1, source_target_pairs={{0,1},{1,2},{2,3},{3,0},{4,5},{5,6},{6,7},{7,4},{8,9},{9,10},{10,1... | collective-permute-start | bytes 1228808 | tf_op jit(solution)/shard_map/ppermute | solution.py:328
  822.4 65.2 %collective-permute-start.25 = (bf16[320,640]{1,0:T(8,128)(2,1)S(1)}, bf16[320,640]{1,0:T(8,128)(2,1)S(1)}, u32[]{:S(2)}, u32[]{:S(2)}) collective-permute-start(bf16[320,640]{1,0:T(8,128)(2,1)S(1)} %get-tuple-element.78), channel_id=1, source_target_pairs={{0,2},{1,3},{2,0},{3,1},{4,6},{5,7},{6,4},{7,5},{8,10},{9,11},{10,... | collective-permute-start | bytes 1228808 | tf_op jit(solution)/shard_map/ppermute | solution.py:328
  828.2 59.9 %collective-permute-start.26 = (bf16[320,640]{1,0:T(8,128)(2,1)S(1)}, bf16[320,640]{1,0:T(8,128)(2,1)S(1)}, u32[]{:S(2)}, u32[]{:S(2)}) collective-permute-start(bf16[320,640]{1,0:T(8,128)(2,1)S(1)} %get-tuple-element.77), channel_id=1, source_target_pairs={{0,3},{1,0},{2,1},{3,2},{4,7},{5,4},{6,5},{7,6},{8,11},{9,8},{10,9... | collective-permute-start | bytes 1228808 | tf_op jit(solution)/shard_map/ppermute | solution.py:328
  (66 other events, 1092.2 us)
Sparse Core Ops, SparseCore 0:
  24.7 118.4 all-gather.3
  145.9 94.4 all-gather.5
  243.7 119.1 all-gather.7
  437.9 71.1 reduce-scatter.7
  533.6 71.2 reduce-scatter.5
  646.0 72.8 reduce-scatter.3

commit v4 on v3

--- a/solution.py
+++ b/solution.py
@@ -90,7 +90,7 @@
         vt_ref[:, at] = value.T.astype(jnp.bfloat16)
         return carry
 
-    lax.fori_loop(0, total // BLOCK, project, 0)
+    lax.fori_loop(0, total // BLOCK, project, 0, unroll=2)
 
     def mix(index, carry):
         at = pl.ds(pl.multiple_of(index * BLOCK, BLOCK), BLOCK)
@@ -103,7 +103,7 @@
         total_ref[0, :, at] = largest + jnp.log2(amount)
         return carry
 
-    lax.fori_loop(0, total // BLOCK, mix, 0)
+    lax.fori_loop(0, total // BLOCK, mix, 0, unroll=3)
 
 
 def attend(normed, weight, shift, cosine, sine, query_mark, key_mark):
@@ -334,7 +334,8 @@
         size, apart = lax.axis_size(axis), 1
         assert size & (size - 1) == 0
         while apart < size:
-            values = values + lax.ppermute(values, axis, [(i, i ^ apart) for i in range(size)])
+            moved = lax.ppermute(values, axis, [(i, i ^ apart) for i in range(size)])
+            values = values + moved
             apart *= 2
     return values
 
@@ -433,7 +434,8 @@
         size, -1, lines * attn_cols
     )[:, :, :length]
     fc1_full = flat(gather_all(block[:, attn_cols : attn_cols + half_units]), size)
-    fc2_full = flat(gather_all(block[:, attn_cols + half_units :]), size)
+    fc2_full = gather_all(block[:, attn_cols + half_units :])
+    fc2_full = flat(fc2_full, size)
     qkv_table, proj_table = pad_tables(half_cols)
     qkv_blocks = dot("zdc,ck->zdk", attn_full, qkv_table).astype(jnp.bfloat16)
     qkv_full = qkv_blocks.transpose(1, 0, 2).reshape(width, -1)
@@ -484,7 +486,8 @@
     middle = start_values + pair_sum(dot("pk,dk->pd", mixed, proj_full)) + proj_shift
     normed_two, unit_two, spread_two = normalize(middle, gain_two, shift_two)
     ffn_input = share(normed_two.astype(jnp.bfloat16))
-    before = dot("pd,df->pf", ffn_input, fc1_full) + fc1_shift
+    before = dot("pd,df->pf", ffn_input, fc1_full)
+    before = before + fc1_shift
     sigma = jax.nn.sigmoid(1.702 * before)
     after = (before * sigma).astype(jnp.bfloat16)
     outcome = middle + pair_sum(dot("pf,df->pd", after, fc2_full)) + fc2_shift

time: 912 us -> 908 us (level)
  Pallas kernels: 158 us -> 146 us
    pallas_call x1, Pallas kernels: 86.4 us -> 74.2 us  [attend(): pl.pallas_call(attend_kernel, grid=(heads,), in_specs=[whole(width), pl.B...]
  transfers between devices with their start and end apart: 42 -> 42, of which waited for: 21 -> 21; matrix products, arithmetic and copies ran while one was open for 31% -> 31% of each run, Pallas kernels for 17% -> 16%
where the time goes in v4:
time: 908 us; the launch traced here: 899 us
  waiting for transfers between devices  356 us (39%)
  matrix products  178 us (20%)
  Pallas kernels  146 us (16%)
  local copies, waits for them, and re-layouts  97.3 us (11%)
  other arithmetic  70.1 us (8%)
  starting transfers between devices  36.1 us (4%)
  between operations  16.1 us (2%)
    dot_general x21, matrix products, dot(): return jnp.einsum(form, left, right, preferred_element_type=jnp.float32)  178 us
    ppermute x4, waiting for transfers between devices, bring(): lax.ppermute(lax.dynamic_index_in_dim(packs, lax.rem(place + step, runs),...  158 us
    ppermute x9, waiting for transfers between devices, scatter_cols(): lax.ppermute(piece(place + step), 'z', pairs).astype(jnp.float32)  88.3 us
    pallas_call x1, Pallas kernels, attend(): pl.pallas_call(attend_kernel, grid=(heads,), in_specs=[whole(width), pl.B...  74.2 us
    pallas_call x1, Pallas kernels, attend_back(): pl.pallas_call(back_kernel, grid=(heads,), in_specs=[wide, thin, thin, pl...  71.4 us
    ppermute x5, waiting for transfers between devices, sum_all(): moved = lax.ppermute(values, axis, [(i, i ^ apart) for i in range(size)])  68.2 us
    all_gather x3, waiting for transfers between devices, gather_all(): return lax.all_gather(block, ('z', 'g'), axis=0, tiled=True)  37.6 us
    reshape x2, local copies, waits for them, and re-layouts, flat(): gathered.reshape(size, rows // size, cols).transpose(1, 0, 2)  19.2 us
  transfers between devices with their start and end apart: 42, of which 21 were waited for; matrix products, arithmetic and copies ran while one was open for 31% of the time, Pallas kernels for 16%

profile of v4, /device:TPU:11, one launch (start us, length us, event | category | flops | bytes accessed | tf_op | source)
XLA Modules:
  0.0 899.4 jit_solution(13417223460148275202)
XLA Ops:
  37.9 28.3 %collective-permute-done = bf16[384,1280]{1,0:T(8,128)(2,1)S(1)} collective-permute-done((bf16[384,1280]{1,0:T(8,128)(2,1)}, bf16[384,1280]{1,0:T(8,128)(2,1)S(1)}, u32[]{:S(2)}, u32[]{:S(2)}) %collective-permute-start) | collective-permute-done | bytes 983072 | tf_op jit(solution)/shard_map/ppermute | solution.py:264
  66.2 35.7 %collective-permute-done.1 = bf16[384,1280]{1,0:T(8,128)(2,1)} collective-permute-done((bf16[384,1280]{1,0:T(8,128)(2,1)}, bf16[384,1280]{1,0:T(8,128)(2,1)}, u32[]{:S(2)}, u32[]{:S(2)}) %collective-permute-start.1) | collective-permute-done | bytes 983072 | tf_op jit(solution)/shard_map/ppermute | solution.py:264
  105.6 37.6 %all-gather.4.cloned.1.call-done = bf16[5376,640]{1,0:T(8,128)(2,1)} async-done(((bf16[336,640]{1,0:T(8,128)(2,1)}), bf16[5376,640]{1,0:T(8,128)(2,1)}) %all-gather.4.cloned.1.call-update) | async-done | bytes 6881296 | tf_op jit(solution)/shard_map/all_gather | solution.py:307
  166.9 12.1 %convolution_convert_fusion.3.w_ref = bf16[4,1280,768]{2,1,0:T(8,128)(2,1)} fusion(bf16[4,1280,640]{2,1,0:T(8,128)(2,1)} %bitcast.148, bf16[640,768,1]{0,1,2:T(8,128)(2,1)S(1)} %copy-done.45), kind=kOutput, calls=%fused_computation.7 | convolution fusion | flops 5037096960 | bytes 15400960 | tf_op jit(solution)/shard_map/zdc,ck->zdk/dot_general | solution.py:344
  181.5 74.2 %shard_map.281 = (bf16[1536,3072]{1,0:T(8,128)(2,1)}, bf16[1536,1024]{1,0:T(8,128)(2,1)S(1)}, f32[8,1,1536]{2,1,0:T(1,128)S(1)}) custom-call(bf16[1536,1280]{1,0:T(8,128)(2,1)S(1)} %pad_maximum_fusion.1.x_ref, bf16[4,1280,768]{2,1,0:T(8,128)(2,1)} %convolution_convert_fusion.3.w_ref, f32[8,1,384]{2,1,0:T(1,128)S(1)} %reshape.258.b_ref, ...), custom_call_target="tpu_custom_call" | custom-call | flops 31406948352 | bytes 16515072 | tf_op jit(solution)/shard_map/pallas_call | solution.py:114
  268.9 41.6 %collective-permute-done.11 = bf16[384,1280]{1,0:T(8,128)(2,1)} collective-permute-done((bf16[384,1280]{1,0:T(8,128)(2,1)}, bf16[384,1280]{1,0:T(8,128)(2,1)}, u32[]{:S(2)}, u32[]{:S(2)}) %collective-permute-start.11) | collective-permute-done | bytes 983072 | tf_op jit(solution)/shard_map/ppermute | solution.py:264
  312.8 52.3 %collective-permute-done.12 = bf16[384,1280]{1,0:T(8,128)(2,1)} collective-permute-done((bf16[384,1280]{1,0:T(8,128)(2,1)}, bf16[384,1280]{1,0:T(8,128)(2,1)}, u32[]{:S(2)}, u32[]{:S(2)}) %collective-permute-start.12) | collective-permute-done | bytes 983072 | tf_op jit(solution)/shard_map/ppermute | solution.py:264
  375.8 9.7 %copy.160 = bf16[4,1280,640]{1,2,0:T(8,128)(2,1)} copy(bf16[4,1280,640]{2,1,0:T(8,128)(2,1)} %bitcast.143) | data formatting | bytes 13107200 | tf_op jit(solution)/shard_map/reshape | solution.py:312
  385.5 9.5 %copy.161 = bf16[4,1280,640]{1,2,0:T(8,128)(2,1)} copy(bf16[4,1280,640]{2,1,0:T(8,128)(2,1)} %bitcast.144) | data formatting | bytes 13107200 | tf_op jit(solution)/shard_map/reshape | solution.py:312
  398.3 20.3 %multiply_convert_fusion.1 = (bf16[1536,2560]{1,0:T(8,128)(2,1)}, f32[1536,2560]{1,0:T(8,128)}) fusion(f32[2560]{0:T(1024)S(1)} %select_n.232, bf16[1280,2560]{0,1:T(8,128)(2,1)} %bitcast.149, bf16[768,1280]{1,0:T(8,128)(2,1)} %collective-permute-done.7, bf16[768,1280]{1,0:T(8,128)(2,1)} %add_convert_fusion), kind=kOutput, calls=%fused_computation.2 | convolution fusion | flops 10101719040 | bytes 34088960 | tf_op jit(solution)/shard_map/pd,df->pf/dot_general | solution.py:344
  418.6 14.7 %convolution_convert_fusion.2 = bf16[1280,2560]{1,0:T(8,128)(2,1)} fusion(bf16[1536,1280]{1,0:T(8,128)(2,1)S(1)} %copy-done.23, bf16[1536,2560]{1,0:T(8,128)(2,1)} %get-tuple-element.110), kind=kOutput, calls=%fused_computation.6 | convolution fusion | flops 10069606400 | bytes 18350080 | tf_op jit(solution)/shard_map/pd,pf->df/dot_general | solution.py:344
  433.4 23.5 %convert_reduce_fusion = (f32[2560]{0:T(1024)}, bf16[1536,2560]{1,0:T(8,128)(2,1)}) fusion(f32[1536,2560]{1,0:T(8,128)} %get-tuple-element.111, f32[2560]{0:T(1024)S(1)} %select_n.232, bf16[1536,1280]{1,0:T(8,128)(2,1)} %constant_dynamic-update-slice_fusion.2, bf16[1280,2560]{0,1:T(8,128)(2,1)} %bitcast.145), kind=kOutput, calls=%fused_computation | convolution fusion | flops 10117445632 | bytes 34099200 | tf_op jit(solution)/shard_map/pd,df->pf/dot_general | solution.py:344
  456.9 15.0 %fusion.66 = f32[1536,1280]{1,0:T(8,128)S(1)} fusion(bf16[1536,2560]{1,0:T(8,128)(2,1)} %get-tuple-element.113, bf16[1280,2560]{0,1:T(8,128)(2,1)} %bitcast.150), kind=kOutput, calls=%fused_computation.220 | convolution fusion | flops 10066329600 | bytes 22282240 | tf_op jit(solution)/shard_map/pf,df->pd/dot_general | solution.py:344
  474.3 15.6 %fusion.65 = f32[1536,1280]{1,0:T(8,128)S(1)} fusion(bf16[1536,2560]{1,0:T(8,128)(2,1)} %get-tuple-element.110, bf16[1280,2560]{0,1:T(8,128)(2,1)} %bitcast.146), kind=kOutput, calls=%fused_computation.219 | convolution fusion | flops 10066329600 | bytes 22282240 | tf_op jit(solution)/shard_map/pf,df->pd/dot_general | solution.py:344
  510.9 14.2 %convolution_convert_fusion.1 = bf16[1280,2560]{1,0:T(8,128)(2,1)} fusion(bf16[1536,2560]{1,0:T(8,128)(2,1)S(1)} %bitcast.185, bf16[768,1280]{1,0:T(8,128)(2,1)} %collective-permute-done.7, bf16[768,1280]{1,0:T(8,128)(2,1)} %add_convert_fusion), kind=kOutput, calls=%fused_computation.5 | convolution fusion | flops 10077470720 | bytes 18350080 | tf_op jit(solution)/shard_map/pd,pf->df/dot_general | solution.py:344
  537.0 71.4 %shard_map.282 = (bf16[1536,3072]{1,0:T(8,128)(2,1)}, f32[8,1,384]{2,1,0:T(1,128)S(1)}) custom-call(bf16[1536,3072]{1,0:T(8,128)(2,1)} %get-tuple-element.29.qkv_ref, bf16[1536,1024]{1,0:T(8,128)(2,1)S(1)} %copy-done.3, bf16[1536,1024]{1,0:T(8,128)(2,1)S(1)} %convolution_convert_fusion.6.grad_ref, f32[8,1,1536]{2,1,0:T(1,128)S(1)} %get-tuple-element.31.total_ref, ...), custom_call_target="tpu_custom_call" | custom-call | flops 24159191040 | bytes 25165824 | tf_op jit(solution)/shard_map/pallas_call | solution.py:200
  608.5 14.9 %convolution_convert_fusion = bf16[1280,3072]{1,0:T(8,128)(2,1)S(1)} fusion(bf16[1536,1280]{1,0:T(8,128)(2,1)S(1)} %copy-done.1, bf16[1536,3072]{1,0:T(8,128)(2,1)} %get-tuple-element.32), kind=kOutput, calls=%fused_computation.4 | convolution fusion | flops 12083527680 | bytes 21233664 | tf_op jit(solution)/shard_map/pd,pk->dk/dot_general | solution.py:344
  641.6 10.6 %copy.162 = bf16[1280,4,768]{0,2,1:T(8,128)(2,1)} copy(bf16[1280,4,768]{2,0,1:T(8,128)(2,1)} %bitcast.139) | data formatting | bytes 15728640 | tf_op jit(solution)/shard_map/convert_element_type | solution.py:440
  652.2 16.3 %fusion.67 = f32[1536,1280]{1,0:T(8,128)S(1)} fusion(bf16[1536,3072]{1,0:T(8,128)(2,1)} %get-tuple-element.32, bf16[1280,3072]{0,1:T(8,128)(2,1)} %bitcast.140), kind=kOutput, calls=%fused_computation.221 | convolution fusion | flops 12079595520 | bytes 25165824 | tf_op jit(solution)/shard_map/pk,dk->pd/dot_general | solution.py:344
  708.9 35.3 %collective-permute-done.22 = f32[16640]{0:T(1024)S(1)} collective-permute-done((f32[16640]{0:T(1024)S(1)}, f32[16640]{0:T(1024)S(1)}, u32[]{:S(2)}, u32[]{:S(2)}) %collective-permute-start.22) | collective-permute-done | bytes 66592 | tf_op jit(solution)/shard_map/ppermute | solution.py:337
  744.3 20.9 %collective-permute-done.23 = f32[16640]{0:T(1024)S(1)} collective-permute-done((f32[16640]{0:T(1024)S(1)}, f32[16640]{0:T(1024)S(1)}, u32[]{:S(2)}, u32[]{:S(2)}) %collective-permute-start.23) | collective-permute-done | bytes 66592 | tf_op jit(solution)/shard_map/ppermute | solution.py:337
  778.9 24.3 %collective-permute-done.33 = bf16[320,640]{1,0:T(8,128)(2,1)S(1)} collective-permute-done((bf16[320,640]{1,0:T(8,128)(2,1)S(1)}, bf16[320,640]{1,0:T(8,128)(2,1)S(1)}, u32[]{:S(2)}, u32[]{:S(2)}) %collective-permute-start.33) | collective-permute-done | bytes 409632 | tf_op jit(solution)/shard_map/ppermute | solution.py:328
  823.9 24.4 %collective-permute-done.29 = bf16[320,640]{1,0:T(8,128)(2,1)} collective-permute-done((bf16[320,640]{1,0:T(8,128)(2,1)}, bf16[320,640]{1,0:T(8,128)(2,1)}, u32[]{:S(2)}, u32[]{:S(2)}) %collective-permute-start.29) | collective-permute-done | bytes 409632 | tf_op jit(solution)/shard_map/ppermute | solution.py:328
  848.3 18.0 %collective-permute-done.30 = bf16[320,640]{1,0:T(8,128)(2,1)} collective-permute-done((bf16[320,640]{1,0:T(8,128)(2,1)S(1)}, bf16[320,640]{1,0:T(8,128)(2,1)}, u32[]{:S(2)}, u32[]{:S(2)}) %collective-permute-start.30) | collective-permute-done | bytes 409632 | tf_op jit(solution)/shard_map/ppermute | solution.py:328
  (354 shorter events, 243.0 us)
Async XLA Ops:
  7.2 136.0 %all-gather.4.cloned.1.call-start = ((), (), s32[]{:S(2)}) async-start(), calls=%async_computation.3 | async-start | bytes 7311360 | tf_op jit(solution)/shard_map/all_gather | solution.py:307
  24.6 351.2 %all-gather.6.cloned.1.call-start = ((), (), s32[]{:S(2)}) async-start(), calls=%async_computation.4 | async-start | bytes 6963200 | tf_op jit(solution)/shard_map/all_gather | solution.py:307
  25.4 360.1 %all-gather.8.cloned.1.call-start = ((), (), s32[]{:S(2)}) async-start(), calls=%async_computation.5 | async-start | bytes 6963200 | tf_op jit(solution)/shard_map/all_gather | solution.py:307
  26.8 39.3 %collective-permute-start = (bf16[384,1280]{1,0:T(8,128)(2,1)}, bf16[384,1280]{1,0:T(8,128)(2,1)S(1)}, u32[]{:S(2)}, u32[]{:S(2)}) collective-permute-start(bf16[384,1280]{1,0:T(8,128)(2,1)} %get-tuple-element.68), channel_id=1, source_target_pairs={{0,0},{1,1},{2,4},{3,5},{4,2},{5,3},{6,6},{7,7},{8,8},{9,9},{10,12... | collective-permute-start | bytes 2949128 | tf_op jit(solution)/shard_map/ppermute | solution.py:264
  31.3 70.5 %collective-permute-start.1 = (bf16[384,1280]{1,0:T(8,128)(2,1)}, bf16[384,1280]{1,0:T(8,128)(2,1)}, u32[]{:S(2)}, u32[]{:S(2)}) collective-permute-start(bf16[384,1280]{1,0:T(8,128)(2,1)} %get-tuple-element.69), channel_id=1, source_target_pairs={{0,1},{1,0},{2,5},{3,4},{4,3},{5,2},{6,7},{7,6},{8,9},{9,8},{10,13... | collective-permute-start | bytes 2949128 | tf_op jit(solution)/shard_map/ppermute | solution.py:264
  37.6 729.7 %reduce-scatter.8.cloned.1.call-start = ((), (), s32[]{:S(2)}) async-start(), calls=%async_computation.8 | async-start | bytes 8192000 | tf_op jit(solution)/shard_map/reduce_scatter | solution.py:316
  261.4 108.0 %collective-permute-start.6 = (bf16[768,1280]{1,0:T(8,128)(2,1)}, bf16[768,1280]{1,0:T(8,128)(2,1)}, u32[]{:S(2)}, u32[]{:S(2)}) collective-permute-start(bf16[768,1280]{1,0:T(8,128)(2,1)} %slice.426), channel_id=1, source_target_pairs={{0,4},{4,0},{1,5},{5,1},{2,6},{6,2},{3,7},{7,3},{8,12},{12,8},{9,1... | collective-permute-start | bytes 5898248 | tf_op jit(solution)/shard_map/ppermute | solution.py:248
  264.5 46.0 %collective-permute-start.11 = (bf16[384,1280]{1,0:T(8,128)(2,1)}, bf16[384,1280]{1,0:T(8,128)(2,1)}, u32[]{:S(2)}, u32[]{:S(2)}) collective-permute-start(bf16[384,1280]{1,0:T(8,128)(2,1)} %get-tuple-element.63), channel_id=1, source_target_pairs={{0,0},{1,1},{2,4},{3,5},{4,2},{5,3},{6,6},{7,7},{8,8},{9,9},{10,12... | collective-permute-start | bytes 2949128 | tf_op jit(solution)/shard_map/ppermute | solution.py:264
  267.4 97.7 %collective-permute-start.12 = (bf16[384,1280]{1,0:T(8,128)(2,1)}, bf16[384,1280]{1,0:T(8,128)(2,1)}, u32[]{:S(2)}, u32[]{:S(2)}) collective-permute-start(bf16[384,1280]{1,0:T(8,128)(2,1)} %get-tuple-element.62), channel_id=1, source_target_pairs={{0,1},{1,0},{2,5},{3,4},{4,3},{5,2},{6,7},{7,6},{8,9},{9,8},{10,13... | collective-permute-start | bytes 2949128 | tf_op jit(solution)/shard_map/ppermute | solution.py:264
  367.4 27.8 %collective-permute-start.13 = (bf16[768,1280]{1,0:T(8,128)(2,1)}, bf16[768,1280]{1,0:T(8,128)(2,1)}, u32[]{:S(2)}, u32[]{:S(2)}) collective-permute-start(bf16[768,1280]{1,0:T(8,128)(2,1)} %get-tuple-element.84), channel_id=1, source_target_pairs={{0,4},{4,0},{1,5},{5,1},{2,6},{6,2},{3,7},{7,3},{8,12},{12,8},{9,1... | collective-permute-start | bytes 5898248 | tf_op jit(solution)/shard_map/ppermute | solution.py:248
  433.4 376.9 %reduce-scatter.6.cloned.1.call-start = ((), (), s32[]{:S(2)}) async-start(), calls=%async_computation.7 | async-start | bytes 8192000 | tf_op jit(solution)/shard_map/reduce_scatter | solution.py:316
  529.4 286.1 %reduce-scatter.4.cloned.1.call-start = ((), (), s32[]{:S(2)}) async-start(), calls=%async_computation.6 | async-start | bytes 8192000 | tf_op jit(solution)/shard_map/reduce_scatter | solution.py:316
  675.3 93.5 %collective-permute-start.9 = (bf16[384,1280]{1,0:T(8,128)(2,1)}, bf16[384,1280]{1,0:T(8,128)(2,1)S(1)}, u32[]{:S(2)}, u32[]{:S(2)}) collective-permute-start(bf16[384,1280]{1,0:T(8,128)(2,1)} %get-tuple-element.67), channel_id=1, source_target_pairs={{0,0},{1,1},{4,2},{5,3},{2,4},{3,5},{6,6},{7,7},{8,8},{9,9},{12,10... | collective-permute-start | bytes 2949128 | tf_op jit(solution)/shard_map/ppermute | solution.py:279
  677.5 94.2 %collective-permute-start.10 = (bf16[384,1280]{1,0:T(8,128)(2,1)}, bf16[384,1280]{1,0:T(8,128)(2,1)S(1)}, u32[]{:S(2)}, u32[]{:S(2)}) collective-permute-start(bf16[384,1280]{1,0:T(8,128)(2,1)} %get-tuple-element.66), channel_id=1, source_target_pairs={{1,0},{0,1},{5,2},{4,3},{3,4},{2,5},{7,6},{6,7},{9,8},{8,9},{13,10... | collective-permute-start | bytes 2949128 | tf_op jit(solution)/shard_map/ppermute | solution.py:279
  688.7 84.4 %collective-permute-start.17 = (bf16[384,1280]{1,0:T(8,128)(2,1)}, bf16[384,1280]{1,0:T(8,128)(2,1)S(1)}, u32[]{:S(2)}, u32[]{:S(2)}) collective-permute-start(bf16[384,1280]{1,0:T(8,128)(2,1)} %get-tuple-element.61), channel_id=1, source_target_pairs={{0,0},{1,1},{4,2},{5,3},{2,4},{3,5},{6,6},{7,7},{8,8},{9,9},{12,10... | collective-permute-start | bytes 2949128 | tf_op jit(solution)/shard_map/ppermute | solution.py:279
  694.1 78.9 %collective-permute-start.18 = (bf16[384,1280]{1,0:T(8,128)(2,1)}, bf16[384,1280]{1,0:T(8,128)(2,1)}, u32[]{:S(2)}, u32[]{:S(2)}) collective-permute-start(bf16[384,1280]{1,0:T(8,128)(2,1)} %get-tuple-element.60), channel_id=1, source_target_pairs={{1,0},{0,1},{5,2},{4,3},{3,4},{2,5},{7,6},{6,7},{9,8},{8,9},{13,10... | collective-permute-start | bytes 2949128 | tf_op jit(solution)/shard_map/ppermute | solution.py:279
  708.8 35.4 %collective-permute-start.22 = (f32[16640]{0:T(1024)S(1)}, f32[16640]{0:T(1024)S(1)}, u32[]{:S(2)}, u32[]{:S(2)}) collective-permute-start(f32[16640]{0:T(1024)S(1)} %add.319), channel_id=1, source_target_pairs={{0,1},{1,0},{2,3},{3,2},{4,5},{5,4},{6,7},{7,6},{8,9},{9,8},{10,11... | collective-permute-start | bytes 199688 | tf_op jit(solution)/shard_map/ppermute | solution.py:337
  768.8 34.5 %collective-permute-start.33 = (bf16[320,640]{1,0:T(8,128)(2,1)S(1)}, bf16[320,640]{1,0:T(8,128)(2,1)S(1)}, u32[]{:S(2)}, u32[]{:S(2)}) collective-permute-start(bf16[320,640]{1,0:T(8,128)(2,1)S(1)} %get-tuple-element.72), channel_id=1, source_target_pairs={{0,2},{1,3},{2,0},{3,1},{4,6},{5,7},{6,4},{7,5},{8,10},{9,11},{10,... | collective-permute-start | bytes 1228808 | tf_op jit(solution)/shard_map/ppermute | solution.py:328
  771.7 36.2 %collective-permute-start.34 = (bf16[320,640]{1,0:T(8,128)(2,1)S(1)}, bf16[320,640]{1,0:T(8,128)(2,1)S(1)}, u32[]{:S(2)}, u32[]{:S(2)}) collective-permute-start(bf16[320,640]{1,0:T(8,128)(2,1)S(1)} %get-tuple-element.71), channel_id=1, source_target_pairs={{0,3},{1,0},{2,1},{3,2},{4,7},{5,4},{6,5},{7,6},{8,11},{9,8},{10,9... | collective-permute-start | bytes 1228808 | tf_op jit(solution)/shard_map/ppermute | solution.py:328
  812.5 35.7 %collective-permute-start.29 = (bf16[320,640]{1,0:T(8,128)(2,1)}, bf16[320,640]{1,0:T(8,128)(2,1)}, u32[]{:S(2)}, u32[]{:S(2)}) collective-permute-start(bf16[320,640]{1,0:T(8,128)(2,1)} %get-tuple-element.75), channel_id=1, source_target_pairs={{0,2},{1,3},{2,0},{3,1},{4,6},{5,7},{6,4},{7,5},{8,10},{9,11},{10,... | collective-permute-start | bytes 1228808 | tf_op jit(solution)/shard_map/ppermute | solution.py:328
  812.5 53.8 %collective-permute-start.30 = (bf16[320,640]{1,0:T(8,128)(2,1)S(1)}, bf16[320,640]{1,0:T(8,128)(2,1)}, u32[]{:S(2)}, u32[]{:S(2)}) collective-permute-start(bf16[320,640]{1,0:T(8,128)(2,1)S(1)} %get-tuple-element.74), channel_id=1, source_target_pairs={{0,3},{1,0},{2,1},{3,2},{4,7},{5,4},{6,5},{7,6},{8,11},{9,8},{10,9... | collective-permute-start | bytes 1228808 | tf_op jit(solution)/shard_map/ppermute | solution.py:328
  816.9 57.6 %collective-permute-start.24 = (bf16[320,640]{1,0:T(8,128)(2,1)S(1)}, bf16[320,640]{1,0:T(8,128)(2,1)S(1)}, u32[]{:S(2)}, u32[]{:S(2)}) collective-permute-start(bf16[320,640]{1,0:T(8,128)(2,1)S(1)} %get-tuple-element.76), channel_id=1, source_target_pairs={{0,1},{1,2},{2,3},{3,0},{4,5},{5,6},{6,7},{7,4},{8,9},{9,10},{10,1... | collective-permute-start | bytes 1228808 | tf_op jit(solution)/shard_map/ppermute | solution.py:328
  818.1 65.2 %collective-permute-start.25 = (bf16[320,640]{1,0:T(8,128)(2,1)S(1)}, bf16[320,640]{1,0:T(8,128)(2,1)S(1)}, u32[]{:S(2)}, u32[]{:S(2)}) collective-permute-start(bf16[320,640]{1,0:T(8,128)(2,1)S(1)} %get-tuple-element.78), channel_id=1, source_target_pairs={{0,2},{1,3},{2,0},{3,1},{4,6},{5,7},{6,4},{7,5},{8,10},{9,11},{10,... | collective-permute-start | bytes 1228808 | tf_op jit(solution)/shard_map/ppermute | solution.py:328
  823.9 59.9 %collective-permute-start.26 = (bf16[320,640]{1,0:T(8,128)(2,1)S(1)}, bf16[320,640]{1,0:T(8,128)(2,1)S(1)}, u32[]{:S(2)}, u32[]{:S(2)}) collective-permute-start(bf16[320,640]{1,0:T(8,128)(2,1)S(1)} %get-tuple-element.77), channel_id=1, source_target_pairs={{0,3},{1,0},{2,1},{3,2},{4,7},{5,4},{6,5},{7,6},{8,11},{9,8},{10,9... | collective-permute-start | bytes 1228808 | tf_op jit(solution)/shard_map/ppermute | solution.py:328
  (66 other events, 1061.1 us)
Sparse Core Ops, SparseCore 0:
  24.7 118.4 all-gather.3
  145.9 94.4 all-gather.5
  243.7 118.6 all-gather.7
  433.5 70.0 reduce-scatter.7
  529.5 69.9 reduce-scatter.5
  641.7 71.4 reduce-scatter.3
